TPU v7x, 256 devices: a whole 4x4x8 slice. The times are simulated.
256 devices in a mesh: rep: 1, dp: 256 (over x, y, z, core).
Axes of the slice: x: 4, y: 4, z: 8, core: 2. Of those that a mesh axis runs over, the one named last changes fastest.
Arguments:
- x: bfloat16 [256, 1024, 768], P(('rep', 'dp'))
- dy: bfloat16 [256, 1024, 768], P(('rep', 'dp'))
- w_gate: bfloat16 [2, 768, 3072], replicated
- w_up: bfloat16 [2, 768, 3072], replicated
- w_down: bfloat16 [2, 3072, 768], replicated
- m_w_gate: float32 [2, 768, 3072], replicated
- m_w_up: float32 [2, 768, 3072], replicated
- m_w_down: float32 [2, 3072, 768], replicated
- v_w_gate: float32 [2, 768, 3072], replicated
- v_w_up: float32 [2, 768, 3072], replicated
- v_w_down: float32 [2, 3072, 768], replicated
Outputs:
- output 1: bfloat16 [2, 768, 3072], P('rep')
- output 2: bfloat16 [2, 768, 3072], P('rep')
- output 3: bfloat16 [2, 3072, 768], P('rep')
- output 4: float32 [2, 768, 3072], P('rep')
- output 5: float32 [2, 768, 3072], P('rep')
- output 6: float32 [2, 3072, 768], P('rep')
- output 7: float32 [2, 768, 3072], P('rep')
- output 8: float32 [2, 768, 3072], P('rep')
- output 9: float32 [2, 3072, 768], P('rep')
All inputs are finite; a program needn't handle non-finite values.
Results may differ from a plain program's by a relative error of at most 0.022.
Values are sent between devices in bfloat16 or wider.
A program may use at most 768 MiB of HBM per device.

v0:
```python
import jax
import jax.numpy as jnp
from jax import lax
from jax.sharding import PartitionSpec as P

NAMES = ("w_gate", "w_up", "w_down")


def matmul(a, w):
    return jnp.dot(a, w, preferred_element_type=jnp.float32).astype(jnp.bfloat16)


def normed(h):
    wide = h.astype(jnp.float32)
    scale = lax.rsqrt(jnp.mean(wide**2, -1, keepdims=True) + 1e-6)
    return (wide * scale).astype(jnp.bfloat16)


def layer(h, w):
    a = normed(h)
    gate = jnp.dot(a, w["w_gate"], preferred_element_type=jnp.float32)
    up = jnp.dot(a, w["w_up"], preferred_element_type=jnp.float32)
    return h + matmul((jax.nn.silu(gate) * up).astype(jnp.bfloat16), w["w_down"])


def adamw(w, m, v, g):
    m = 0.9 * m + 0.1 * g
    v = 0.95 * v + 0.05 * g * g
    step = m * lax.rsqrt(v + 1e-8) + 0.1 * w
    return (w - 0.02 * step).astype(jnp.bfloat16), m, v


def clipped(gradients, sum_of_squares, count):
    factor = jnp.minimum(1.0, 0.5 * lax.rsqrt(sum_of_squares / count + 1e-30))
    return [g * factor for g in gradients]


def solution(mesh):
    def step(x, dy, *arrays):
        weights, m, v = (arrays[i : i + 3] for i in (0, 3, 6))
        layers = weights[0].shape[0]
        h, kept = x[0], []
        for number in range(layers):
            kept.append(h)
            h = layer(h, {name: w[number] for name, w in zip(NAMES, weights, strict=True)})
        by_h, summed = dy[0], [None] * layers
        for number in reversed(range(layers)):
            _, back = jax.vjp(lambda w, h: layer(h, w), {name: w[number] for name, w in zip(NAMES, weights, strict=True)}, kept[number])
            by_w, by_h = back(by_h)
            summed[number] = [lax.psum(by_w[name], "dp") for name in NAMES]
        gradients = [jnp.stack([summed[number][i] for number in range(layers)]).astype(jnp.float32) for i in range(3)]
        gradients = clipped(gradients, sum(jnp.sum(g * g) for g in gradients), sum(g.size for g in gradients))
        new = [adamw(w.astype(jnp.float32), m, v, g) for w, m, v, g in zip(weights, m, v, gradients, strict=True)]
        return tuple(one[which] for which in range(3) for one in new)

    return jax.shard_map(
        step,
        mesh=mesh,
        in_specs=(P(("rep", "dp"), None, None),) * 2 + (P(None, None, None),) * 9,
        out_specs=(P("rep", None, None),) * 9,
        check_vma=False,
    )
```

profile of v0, /device:TPU:1, one launch (start us, length us, event | category | flops | bytes accessed | tf_op | source)
XLA Modules:
  0.0 716.8 jit_solution(11599176149739375073)
XLA Ops:
  7.2 1.7 copy.20
  9.3 2.7 copy.21
  12.1 9.2 %convolution_convert_fusion.1 = bf16[1024,3072]{1,0:T(8,128)(2,1)} fusion(bf16[2,3072,768]{2,1,0:T(8,128)(2,1)} %param.15, bf16[1,1024,768]{2,1,0:T(8,128)(2,1)} %param.12), kind=kOutput, calls=%fused_computation.64 | convolution fusion | flops 4834983936 | bytes 12582912 | tf_op jit(solution)/shard_map/transpose(jvp())/dot_general | solution.py:10
  21.3 10.6 %fusion.55 = f32[1024,3072]{1,0:T(8,128)} fusion(bf16[2,768,3072]{2,1,0:T(8,128)(2,1)} %param.13, bf16[1,1024,768]{2,1,0:T(8,128)(2,1)S(1)} %copy-done.4, f32[1024]{0:T(1024)S(1)} %add_rsqrt_fusion), kind=kOutput, calls=%fused_computation.88 | convolution fusion | flops 4834197504 | bytes 18878464 | tf_op jit(solution)/shard_map/dot_general | solution.py:21
  32.0 12.4 %multiply_convert_fusion.1 = (bf16[1024,3072]{1,0:T(8,128)(2,1)}, f32[1024,3072]{1,0:T(8,128)}) fusion(f32[1024,3072]{1,0:T(8,128)} %fusion.55, bf16[2,768,3072]{2,1,0:T(8,128)(2,1)S(1)} %bitcast.81, bf16[1,1024,768]{2,1,0:T(8,128)(2,1)S(1)} %copy-done.4, f32[1024]{0:T(1024)S(1)} %add_rsqrt_fusion), kind=kOutput, calls=%fused_computation.53 | convolution fusion | flops 4853071872 | bytes 37752832 | tf_op jit(solution)/shard_map/dot_general | solution.py:22
  44.4 8.8 %fusion.78 = (f32[1024]{0:T(1024)S(1)}, bf16[1024,768]{0,1:T(8,128)(2,1)S(1)}) fusion(bf16[1024,3072]{1,0:T(8,128)(2,1)} %get-tuple-element.24, bf16[2,3072,768]{2,1,0:T(8,128)(2,1)} %param.15, bf16[1,1024,768]{1,2,0:T(8,128)(2,1)S(1)} %copy.20), kind=kOutput, calls=%fused_computation.112 | convolution fusion | flops 4835769344 | bytes 14159872 | tf_op jit(solution)/shard_map/dot_general | solution.py:10
  53.1 8.3 %fusion.42 = f32[1024,3072]{1,0:T(8,128)} fusion(bf16[2,768,3072]{2,1,0:T(8,128)(2,1)S(1)} %bitcast.81, bf16[1024,768]{0,1:T(8,128)(2,1)S(1)} %get-tuple-element.27, f32[1024]{0:T(1024)S(1)} %fusion.108), kind=kOutput, calls=%fused_computation.75 | convolution fusion | flops 4834197504 | bytes 18878464 | tf_op jit(solution)/shard_map/jvp()/dot_general | solution.py:22
  61.5 18.2 %fusion.23 = (bf16[1024,3072]{1,0:T(8,128)(2,1)}, f32[1024,3072]{1,0:T(8,128)}) fusion(f32[1024,3072]{1,0:T(8,128)} %fusion.42, bf16[1024,3072]{1,0:T(8,128)(2,1)} %convolution_convert_fusion.1, bf16[2,768,3072]{2,1,0:T(8,128)(2,1)} %param.13, bf16[1024,768]{0,1:T(8,128)(2,1)S(1)} %get-tuple-element.27, f32[1024]{0:T(1024)S(1)} %fusion.108), kind=kOutput, calls=%fused_computation.44 | convolution fusion | flops 4871946240 | bytes 44044288 | tf_op jit(solution)/shard_map/jvp()/dot_general | solution.py:21
  79.7 11.6 %fusion.88 = bf16[1024,768]{0,1:T(8,128)(2,1)} fusion(bf16[2,768,3072]{2,1,0:T(8,128)(2,1)} %param.14, bf16[1024,3072]{1,0:T(8,128)(2,1)} %convolution_convert_fusion.1, f32[1024,3072]{1,0:T(8,128)} %get-tuple-element.29), kind=kOutput, calls=%fused_computation.118 | convolution fusion | flops 4851499008 | bytes 25165824 | tf_op jit(solution)/shard_map/transpose(jvp())/dot_general | solution.py:22
  91.3 11.3 %fusion.61 = bf16[1,768,3072]{2,1,0:T(8,128)(2,1)} fusion(bf16[1024,3072]{1,0:T(8,128)(2,1)} %convolution_convert_fusion.1, bf16[1024,768]{0,1:T(8,128)(2,1)S(1)} %get-tuple-element.27, f32[1024]{0:T(1024)S(1)} %fusion.108, f32[1024,3072]{1,0:T(8,128)} %get-tuple-element.29), kind=kOutput, calls=%fused_computation.94 | convolution fusion | flops 4855431168 | bytes 25169920 | tf_op jit(solution)/shard_map/transpose(jvp())/dot_general | solution.py:22
  102.5 11.5 %fusion.62 = bf16[1,3072,768]{2,1,0:T(8,128)(2,1)} fusion(f32[1024,3072]{1,0:T(8,128)S(1)} %bitcast.87, bf16[1,1024,768]{2,1,0:T(8,128)(2,1)S(1)} %copy-done.5, f32[1024,3072]{1,0:T(8,128)} %get-tuple-element.29), kind=kOutput, calls=%fused_computation.95 | convolution fusion | flops 4853071872 | bytes 31457280 | tf_op jit(solution)/shard_map/transpose(jvp())/dot_general | solution.py:10
  114.1 9.6 %fusion.63 = bf16[1,768,3072]{2,1,0:T(8,128)(2,1)} fusion(bf16[1024,3072]{1,0:T(8,128)(2,1)} %get-tuple-element.28, bf16[1024,768]{0,1:T(8,128)(2,1)S(1)} %get-tuple-element.27, f32[1024]{0:T(1024)S(1)} %fusion.108), kind=kOutput, calls=%fused_computation.96 | convolution fusion | flops 4834197504 | bytes 12587008 | tf_op jit(solution)/shard_map/transpose(jvp())/dot_general | solution.py:21
  123.7 7.4 %fusion.80 = (f32[1024]{0:T(1024)S(1)}, bf16[1024,768]{0,1:T(8,128)(2,1)S(1)}) fusion(bf16[1024,768]{0,1:T(8,128)(2,1)S(1)} %get-tuple-element.27, bf16[1024,768]{0,1:T(8,128)(2,1)S(1)} %copy-done.11, bf16[1024,3072]{1,0:T(8,128)(2,1)S(1)} %copy-done.10, bf16[2,768,3072]{2,1,0:T(8,128)(2,1)} %param.13), kind=kOutput, calls=%fused_computation.114 | convolution fusion | flops 4835769344 | bytes 15732736 | tf_op jit(solution)/shard_map/transpose(jvp())/dot_general | solution.py:21
  131.1 1.1 fusion.92
  132.3 5.6 convolution_convert_fusion
  137.9 9.9 %fusion.64 = bf16[1,3072,768]{2,1,0:T(8,128)(2,1)} fusion(bf16[1024,3072]{1,0:T(8,128)(2,1)} %get-tuple-element.24, bf16[1024,768]{0,1:T(8,128)(2,1)S(1)} %fusion.92), kind=kOutput, calls=%fused_computation.97 | convolution fusion | flops 4834197504 | bytes 12582912 | tf_op jit(solution)/shard_map/transpose(jvp())/dot_general | solution.py:10
  147.9 7.1 fusion.60
  155.0 13.2 %fusion.65 = bf16[1,768,3072]{2,1,0:T(8,128)(2,1)} fusion(f32[1024,3072]{1,0:T(8,128)} %fusion.55, f32[1024,3072]{1,0:T(8,128)} %get-tuple-element.25, bf16[1024,3072]{1,0:T(8,128)(2,1)S(1)} %convolution_convert_fusion, bf16[1,1024,768]{1,2,0:T(8,128)(2,1)S(1)} %copy-done.2, f32[1024]{0:T(1024)S(1)} %copy-done.9), kind=kOutput, calls=%fused_computation.98 | convolution fusion | flops 4871159808 | bytes 37752832 | tf_op jit(solution)/shard_map/transpose(jvp())/dot_general | solution.py:21
  168.2 414.8 %all-reduce.3.cloned.1.call-done = (bf16[1,768,3072]{2,1,0:T(8,128)(2,1)}, bf16[1,768,3072]{2,1,0:T(8,128)(2,1)}, bf16[1,768,3072]{2,1,0:T(8,128)(2,1)}, bf16[1,...) async-done(((bf16[1,768,3072]{2,1,0:T(8,128)(2,1)}, bf16[1,768,3072]{2,1,0:T(8,128)(2,1)}, bf16[1,768,3072]{2,1,0:T(8,128)(2,1)}, ...) | async-done | bytes 28311568 | tf_op jit(solution)/shard_map/psum | solution.py:50
  583.1 9.4 %fusion.9 = f32[]{:T(128)} fusion(bf16[1,768,3072]{2,1,0:T(8,128)(2,1)} %get-tuple-element.9, bf16[1,768,3072]{2,1,0:T(8,128)(2,1)} %get-tuple-element.10), kind=kLoop, calls=%fused_computation.26 | loop fusion | flops 18874368 | bytes 9437188 | tf_op jit(solution)/shard_map/reduce_sum | solution.py:52
  592.4 5.5 fusion.10
  599.2 9.3 %fusion.11 = f32[]{:T(128)} fusion(bf16[1,3072,768]{2,1,0:T(8,128)(2,1)} %get-tuple-element.13, bf16[1,3072,768]{2,1,0:T(8,128)(2,1)} %get-tuple-element.14), kind=kLoop, calls=%fused_computation.28 | loop fusion | flops 18874368 | bytes 9437188 | tf_op jit(solution)/shard_map/reduce_sum | solution.py:52
  609.2 37.1 %fusion.17 = (bf16[2,3072,768]{2,1,0:T(8,128)(2,1)}, f32[2,3072,768]{2,1,0:T(8,128)}, f32[2,3072,768]{2,1,0:T(8,128)}) fusion(bf16[2,3072,768]{2,1,0:T(8,128)(2,1)} %param.15, f32[]{:T(128)S(6)} %min_shard_map.3, bf16[1,3072,768]{2,1,0:T(8,128)(2,1)} %get-tuple-element.13, bf16[1,3072,768]{2,1,0:T(8,128)(2,1)} %get-tuple-element.14, ...), kind=kLoop, calls=%fused_computation.34 | loop fusion | flops 94371840 | bytes 103809024 | tf_op jit(solution)/shard_map/convert_element_type | solution.py:30
  646.3 63.3 %fusion.8 = (bf16[2,768,3072]{2,1,0:T(8,128)(2,1)}, f32[2,768,3072]{2,1,0:T(8,128)}, f32[2,768,3072]{2,1,0:T(8,128)}, bf16[2,768,3072]{2,1,0:T(8,128)(2,1)}, f32...) fusion(bf16[2,768,3072]{2,1,0:T(8,128)(2,1)} %param.13, f32[]{:T(128)S(6)} %min_shard_map.3, ...), kind=kLoop, calls=%fused_computation.25 | loop fusion | flops 188743680 | bytes 207618048 | tf_op jit(solution)/shard_map/convert_element_type | solution.py:30
  (68 shorter events, 0.6 us)
Async XLA Ops:
  7.2 575.9 %all-reduce.3.cloned.1.call-start = ((), (), s32[]{:S(2)}) async-start(), calls=%async_computation | async-start | bytes 56623104 | tf_op jit(solution)/shard_map/psum | solution.py:50
  8.9 35.4 %copy-start.1 = (bf16[1,1024,768]{1,2,0:T(8,128)(2,1)}, bf16[1,1024,768]{1,2,0:T(8,128)(2,1)S(1)}, u32[]{:S(2)}) copy-start(bf16[1,1024,768]{1,2,0:T(8,128)(2,1)S(1)} %copy.20) | copy-start | bytes 4718596
  9.3 22.6 %copy-start.8 = (f32[1024]{0:T(1024)}, f32[1024]{0:T(1024)S(1)}, u32[]{:S(2)}) copy-start(f32[1024]{0:T(1024)S(1)} %add_rsqrt_fusion) | copy-start | bytes 12292
  12.1 19.9 %slice-start = ((s8[9437184]{0:T(1024)(128)(4,1)}), s8[4194304]{0:T(1024)(128)(4,1)S(1)}, s32[]{:S(2)}) async-start(s8[9437184]{0:T(1024)(128)(4,1)} %bitcast.80), calls=%async_computation.1 | async-start | bytes 8388608
  12.1 19.9 %slice-start.1 = ((s8[9437184]{0:T(1024)(128)(4,1)}), s8[4194304]{0:T(1024)(128)(4,1)S(1)}, s32[]{:S(2)}) async-start(s8[9437184]{0:T(1024)(128)(4,1)} %bitcast.80), calls=%async_computation.2 | async-start | bytes 8388608
  21.3 10.6 %slice-start.2 = ((s8[9437184]{0:T(1024)(128)(4,1)}), s8[1048576]{0:T(1024)(128)(4,1)S(1)}, s32[]{:S(2)}) async-start(s8[9437184]{0:T(1024)(128)(4,1)} %bitcast.80), calls=%async_computation.3 | async-start | bytes 2097152
  79.7 22.8 %slice-start.7 = ((s8[12582912]{0:T(1024)(128)(4,1)}), s8[4194304]{0:T(1024)(128)(4,1)S(1)}, s32[]{:S(2)}) async-start(s8[12582912]{0:T(1024)(128)(4,1)} %bitcast.86), calls=%async_computation.8 | async-start | bytes 8388608
  79.7 22.8 %slice-start.8 = ((s8[12582912]{0:T(1024)(128)(4,1)}), s8[4194304]{0:T(1024)(128)(4,1)S(1)}, s32[]{:S(2)}) async-start(s8[12582912]{0:T(1024)(128)(4,1)} %bitcast.86), calls=%async_computation.9 | async-start | bytes 8388608
  91.3 11.3 %slice-start.9 = ((s8[12582912]{0:T(1024)(128)(4,1)}), s8[4194304]{0:T(1024)(128)(4,1)S(1)}, s32[]{:S(2)}) async-start(s8[12582912]{0:T(1024)(128)(4,1)} %bitcast.86), calls=%async_computation.10 | async-start | bytes 8388608
  91.3 11.3 %copy-start.5 = (bf16[1,1024,768]{2,1,0:T(8,128)(2,1)S(1)}, bf16[1,1024,768]{2,1,0:T(8,128)(2,1)}, u32[]{:S(2)}) copy-start(bf16[1,1024,768]{2,1,0:T(8,128)(2,1)} %param.12) | copy-start | bytes 4718596
  114.1 9.6 %copy-start.10 = (bf16[1024,3072]{1,0:T(8,128)(2,1)S(1)}, bf16[1024,3072]{1,0:T(8,128)(2,1)}, u32[]{:S(2)}) copy-start(bf16[1024,3072]{1,0:T(8,128)(2,1)} %get-tuple-element.28) | copy-start | bytes 18874372
  114.1 9.6 %copy-start.11 = (bf16[1024,768]{0,1:T(8,128)(2,1)S(1)}, bf16[1024,768]{0,1:T(8,128)(2,1)}, u32[]{:S(2)}) copy-start(bf16[1024,768]{0,1:T(8,128)(2,1)} %fusion.88) | copy-start | bytes 4718596
  114.1 18.2 %slice-start.10 = ((s8[9437184]{0:T(1024)(128)(4,1)}), s8[4194304]{0:T(1024)(128)(4,1)S(1)}, s32[]{:S(2)}) async-start(s8[9437184]{0:T(1024)(128)(4,1)} %bitcast.88), calls=%async_computation.11 | async-start | bytes 8388608
  114.1 18.2 %slice-start.11 = ((s8[9437184]{0:T(1024)(128)(4,1)}), s8[4194304]{0:T(1024)(128)(4,1)S(1)}, s32[]{:S(2)}) async-start(s8[9437184]{0:T(1024)(128)(4,1)} %bitcast.88), calls=%async_computation.12 | async-start | bytes 8388608
  132.3 15.5 %slice-start.13 = ((s8[12582912]{0:T(1024)(128)(4,1)}), s8[4194304]{0:T(1024)(128)(4,1)S(1)}, s32[]{:S(2)}) async-start(s8[12582912]{0:T(1024)(128)(4,1)} %bitcast.90), calls=%async_computation.14 | async-start | bytes 8388608
  132.3 15.5 %slice-start.14 = ((s8[12582912]{0:T(1024)(128)(4,1)}), s8[4194304]{0:T(1024)(128)(4,1)S(1)}, s32[]{:S(2)}) async-start(s8[12582912]{0:T(1024)(128)(4,1)} %bitcast.90), calls=%async_computation.15 | async-start | bytes 8388608
  137.9 10.0 %copy-start.2 = (bf16[1,1024,768]{1,2,0:T(8,128)(2,1)S(1)}, bf16[1,1024,768]{1,2,0:T(8,128)(2,1)}, u32[]{:S(2)}) copy-start(bf16[1,1024,768]{1,2,0:T(8,128)(2,1)} %copy-done.1) | copy-start | bytes 4718596
  137.9 10.0 %copy-start.9 = (f32[1024]{0:T(1024)S(1)}, f32[1024]{0:T(1024)}, u32[]{:S(2)}) copy-start(f32[1024]{0:T(1024)} %copy-done.8) | copy-start | bytes 12292
  137.9 10.0 %slice-start.15 = ((s8[12582912]{0:T(1024)(128)(4,1)}), s8[4194304]{0:T(1024)(128)(4,1)S(1)}, s32[]{:S(2)}) async-start(s8[12582912]{0:T(1024)(128)(4,1)} %bitcast.90), calls=%async_computation.16 | async-start | bytes 8388608
  583.1 9.4 %slice-start.5 = ((s8[4718592]{0:T(1024)(128)(4,1)}), s8[4194304]{0:T(1024)(128)(4,1)S(1)}, s32[]{:S(2)}) async-start(s8[4718592]{0:T(1024)(128)(4,1)} %bitcast.84), calls=%async_computation.6 | async-start | bytes 8388608
  583.1 9.4 %copy-start = (bf16[1,768,3072]{2,1,0:T(8,128)(2,1)S(1)}, bf16[1,768,3072]{2,1,0:T(8,128)(2,1)}, u32[]{:S(2)}) copy-start(bf16[1,768,3072]{2,1,0:T(8,128)(2,1)} %get-tuple-element.12) | copy-start | bytes 14155780
  583.1 9.4 %slice-start.6 = ((s8[4718592]{0:T(1024)(128)(4,1)}), s8[524288]{0:T(1024)(128)(4,1)S(1)}, s32[]{:S(2)}) async-start(s8[4718592]{0:T(1024)(128)(4,1)} %bitcast.84), calls=%async_computation.7 | async-start | bytes 1048576
  599.2 47.1 %slice-start.3 = ((s8[4718592]{0:T(1024)(128)(4,1)}), s8[524288]{0:T(1024)(128)(4,1)S(1)}, s32[]{:S(2)}) async-start(s8[4718592]{0:T(1024)(128)(4,1)} %bitcast.82), calls=%async_computation.4 | async-start | bytes 1048576
  609.2 37.1 %slice-start.4 = ((s8[4718592]{0:T(1024)(128)(4,1)}), s8[4194304]{0:T(1024)(128)(4,1)S(1)}, s32[]{:S(2)}) async-start(s8[4718592]{0:T(1024)(128)(4,1)} %bitcast.82), calls=%async_computation.5 | async-start | bytes 8388608
  (5 other events, 41.0 us)
Sparse Core Ops, SparseCore 0:
  168.4 414.6 all-reduce.2
where the time goes:
time: 725 us; the launch traced here: 717 us
  waiting for transfers between devices  415 us (57%)
  matrix products  155 us (21%)
  other arithmetic  126 us (17%)
  between operations  16.8 us (2%)
    psum x1, waiting for transfers between devices, step(): summed[number] = [lax.psum(by_w[name], 'dp') for name in NAMES]  415 us
    convert_element_type x2, other arithmetic, adamw(): return ((w - 0.02 * step).astype(jnp.bfloat16), m, v)  100 us
    dot_general x5, matrix products, layer(): gate = jnp.dot(a, w['w_gate'], preferred_element_type=jnp.float32)  59 us
    dot_general x5, matrix products, layer(): up = jnp.dot(a, w['w_up'], preferred_element_type=jnp.float32)  50.7 us
    dot_general x5, matrix products, matmul(): jnp.dot(a, w, preferred_element_type=jnp.float32).astype(jnp.bfloat16)  45 us
    reduce_sum x3, other arithmetic, step(): jnp.sum(g * g)  24.1 us
  transfers between devices with their start and end apart: 1, of which 1 were waited for; matrix products, arithmetic and copies ran while one was open for 0% of the time, Pallas kernels for 0%

commit v1 on v0

v1 whole, which is shorter than its diff:
```python
import functools

import jax
import jax.numpy as jnp
from jax import lax
from jax.experimental import pallas as pl
from jax.experimental.pallas import tpu as pltpu
from jax.sharding import PartitionSpec as P

NAMES = ("w_gate", "w_up", "w_down")
MESH = pl.DeviceIdType.MESH
NX, NY, NZ = 4, 4, 8
F32, BF16 = jnp.float32, jnp.bfloat16


def matmul(a, w):
    return jnp.dot(a, w, preferred_element_type=jnp.float32).astype(jnp.bfloat16)


def normed(h):
    wide = h.astype(jnp.float32)
    scale = lax.rsqrt(jnp.mean(wide**2, -1, keepdims=True) + 1e-6)
    return (wide * scale).astype(jnp.bfloat16)


def layer(h, w):
    a = normed(h)
    gate = jnp.dot(a, w["w_gate"], preferred_element_type=jnp.float32)
    up = jnp.dot(a, w["w_up"], preferred_element_type=jnp.float32)
    return h + matmul((jax.nn.silu(gate) * up).astype(jnp.bfloat16), w["w_down"])


def adamw(w, m, v, g):
    m = 0.9 * m + 0.1 * g
    v = 0.95 * v + 0.05 * g * g
    step = m * lax.rsqrt(v + 1e-8) + 0.1 * w
    return (w - 0.02 * step).astype(jnp.bfloat16), m, v


def div(a, b):
    return lax.div(a, jnp.int32(b))


def rem(a, b):
    return lax.rem(a, jnp.int32(b))


def first(s, i):
    return i + 1 - 2 * rem(i, 2) if s == 0 else 3 - i


def second(s, i):
    return first(1 - s, i)


def half(s, i):
    return rem(div(i + 1, 2), 2) if s == 0 else div(i, 2)


def part(s, i):
    return div(i, 2) if s == 0 else rem(i, 2)


def quarter(s, i):
    return 2 * half(s, i) + part(s, i)


class Xfer:
    def __init__(self, link, nbytes, src, dst, dev):
        self.link, self.nbytes, self.src, self.dst, self.dev = link, nbytes, src, dst, dev
        self.copy = None
        self.arrives = None


class Event:
    def __init__(self, waits, pre, work, cost, sends):
        self.waits, self.pre, self.work, self.cost, self.sends = waits, pre, work, cost, sends
        self.done = None


RATE = {"ici": 46.0e3, "d2d": 500.0e3}
DELAY = 2.2


def order_of(events):
    links, left, out, clock = {}, list(events), [], 0.0
    while left:
        best = None
        for e in left:
            if any(p.done is None for p in e.pre) or any(t.arrives is None for t in e.waits):
                continue
            ready = max([p.done for p in e.pre] + [t.arrives for t in e.waits] + [0.0])
            if best is None or max(ready, clock) < best[0]:
                best = (max(ready, clock), e)
        clock, e = best
        clock += e.cost
        e.done = clock
        for t in e.sends:
            begin = max(clock, links.get(t.link, 0.0))
            links[t.link] = begin + t.nbytes / RATE["d2d" if t.link == "d2d" else "ici"]
            t.arrives = links[t.link] + DELAY
        left.remove(e)
        out.append(e)
    return out, clock


def comm_kernel(ru, cu, *refs):
    (g1, u1, d1, g0, u0, d0, gu_out, dn_out, sq_out, own_ab, own_c, p_ab, p_c, r1, r2, r3, r4, rz, rc, rx1, rx2, ry, f_ab, acc, nz, ny, nx, nc,
     send_sem, recv_sem, load_sem, keep_sem) = refs
    grads = ((g0, u0, d0), (g1, u1, d1))
    me = lax.axis_index("dp")
    core = rem(me, 2)
    z = rem(div(me, 2), NZ)
    y = rem(div(me, 2 * NZ), NY)
    x = div(me, 2 * NZ * NY)
    other = 1 - core

    def at(x_=None, y_=None, z_=None, c_=None):
        pick = lambda v, d: d if v is None else v
        return ((pick(x_, x) * NY + pick(y_, y)) * NZ + pick(z_, z)) * 2 + pick(c_, core)

    R = lambda start, size: pl.ds(pl.multiple_of(start, 16), size)
    C = lambda start, size: pl.ds(pl.multiple_of(start, 128), size)

    barrier = pltpu.get_barrier_semaphore()
    peers = [at(c_=other)]
    peers += [at(x_=rem(x + d, NX)) for d in range(1, NX)]
    peers += [at(y_=rem(y + d, NY)) for d in range(1, NY)]
    peers += [at(z_=rem(z + d, NZ)) for d in range(1, NZ)]

    S = 4 * ru
    HC, QC = 4 * cu, 2 * cu
    DC = 2 * cu
    ZR = 2 * ru

    loads = {}
    for l in (1, 0):
        for c in range(2):
            loads[l, c] = pltpu.make_async_copy(grads[l][c].at[R(core * 2 * S, 2 * S), :], own_ab.at[l, c], load_sem.at[l, c])
        loads[l, 2] = pltpu.make_async_copy(grads[l][2].at[R(core * 16 * ZR, 16 * ZR), :], own_c.at[l], load_sem.at[l, 2])
        for k in range(3):
            loads[l, k].start()
    for p in peers:
        pl.semaphore_signal(barrier, inc=1, device_id={"dp": p}, device_id_type=MESH)
    pl.semaphore_wait(barrier, len(peers))

    xfers, events = [], []

    def xfer(link, rows, cols, src, dst, dev, hops=1):
        t = Xfer(link, rows * cols * 2 * hops, src, dst, dev)
        xfers.append(t)
        return t

    def event(waits, pre, work, cost, sends):
        e = Event(waits, pre, work, cost, sends)
        events.append(e)
        return e

    def total(dst, srcs, rows, cols):
        wide = min(cols, 2 * cu)
        across = cols // wide

        def block(i, _):
            r, c = (div(i, across), rem(i, across)) if across > 1 else (i, 0)

            def window(a):
                ref, lead, row, col = a
                return ref.at[(*lead, R(row + r * 16, 16), C(col + c * wide, wide))]

            s = window(srcs[0])[...].astype(F32)
            for a in srcs[1:]:
                s = s + window(a)[...].astype(F32)
            window(dst)[...] = s.astype(BF16)
            return 0

        lax.fori_loop(0, rows // 16 * across, block, 0)

    def add_squares(ref, lead, scale):
        for r in range(0, ru, 16):
            v = ref[(*lead, pl.ds(r, 16), slice(None))].astype(F32)
            v = v * v
            s = acc[...]
            for a in range(0, 16, 8):
                for b in range(0, cu, 128):
                    s = s + (scale * v[a : a + 8, b : b + 128])
            acc[...] = s

    adds = lambda rows, cols, n: rows * cols * n / 2.2e6 + 0.15

    acc[...] = jnp.zeros_like(acc)
    loaded = set()

    def need(*keys):
        for k in keys:
            if k not in loaded:
                loaded.add(k)
                loads[k].wait()

    d2d = {}
    firsts, seconds = [], []
    for l in (1, 0):
        for s in range(2):
            for c in range(2):
                ri = x if c == 0 else y
                for which, where, to in (("send", 1 - half(s, ri), firsts), ("keep", half(s, ri), seconds)):
                    row = s * S + where * 2 * ru
                    t = xfer("d2d", 2 * ru, 8 * cu,
                             functools.partial(lambda l, c, row: grads[l][c].at[R(other * 2 * S + row, 2 * ru), :], l, c, row),
                             functools.partial(lambda l, c, row: p_ab.at[l, c, R(row, 2 * ru), :], l, c, row), at(c_=other))
                    d2d[which, l, c, s] = t
                    to.append(t)
        for s in range(2):
            t = xfer("d2d", 8 * ZR, DC,
                     functools.partial(lambda l, s: grads[l][2].at[R(other * 16 * ZR + s * 8 * ZR, 8 * ZR), :], l, s),
                     functools.partial(lambda l, s: p_c.at[l, pl.ds(s * 8 * ZR, 8 * ZR), :], l, s), at(c_=other))
            d2d["c", l, s] = t
            firsts.append(t)
        firsts += seconds
        seconds = []
    begin = event([], [], lambda: None, 0.0, firsts)

    pieces_done = {}
    arrived = []
    for l in (1, 0):
        ends = []
        for c in range(2):
            ri, ci = (x, y) if c == 0 else (y, x)
            rax, cax = ("x", "y") if c == 0 else ("y", "x")
            rdev = (lambda i: at(x_=i)) if c == 0 else (lambda i: at(y_=i))
            cdev = (lambda i: at(y_=i)) if c == 0 else (lambda i: at(x_=i))
            for s in range(2):
                e1, e2 = ("e1", "e2") if s == 0 else ("e2", "e1")
                b1, b2, c1, c2 = half(s, ri), part(s, ri), half(s, ci), part(s, ci)
                out_rows, keep_rows = s * S + (1 - b1) * 2 * ru, s * S + b1 * 2 * ru
                q_out, q_keep = keep_rows + (1 - b2) * ru, keep_rows + b2 * ru
                k1 = functools.partial
                t1 = xfer(rax + e1, 2 * ru, 8 * cu, k1(lambda l, c, a: p_ab.at[l, c, R(a, 2 * ru), :], l, c, out_rows),
                          k1(lambda l, c, s: r1.at[l, c, s], l, c, s), rdev(first(s, ri)))
                t2 = xfer(rax + e2, ru, 8 * cu, k1(lambda l, c, a: p_ab.at[l, c, R(a, ru), :], l, c, q_out),
                          k1(lambda l, c, s: r2.at[l, c, s], l, c, s), rdev(second(s, ri)))
                t3 = xfer(cax + e1, ru, HC, k1(lambda l, c, a, b: p_ab.at[l, c, R(a, ru), C(b, HC)], l, c, q_keep, (1 - c1) * HC),
                          k1(lambda l, c, s: r3.at[l, c, s], l, c, s), cdev(first(s, ci)))
                t4 = xfer(cax + e2, ru, QC, k1(lambda l, c, a, b: p_ab.at[l, c, R(a, ru), C(b, QC)], l, c, q_keep, c1 * HC + (1 - c2) * QC),
                          k1(lambda l, c, s: r4.at[l, c, s], l, c, s), cdev(second(s, ci)))

                def w1(l=l, c=c, s=s, out_rows=out_rows):
                    need((l, c))
                    here = ((l, c), out_rows, 0)
                    total((p_ab, *here), [(p_ab, *here), (own_ab, *here)], 2 * ru, 8 * cu)

                def w2(l=l, c=c, s=s, q_out=q_out, b2=b2):
                    here = ((l, c), q_out, 0)
                    total((p_ab, *here), [(p_ab, *here), (own_ab, *here), (r1, (l, c, s), (1 - b2) * ru, 0)], ru, 8 * cu)

                def rest(cols_at, cols, more, l=l, c=c, s=s, q_keep=q_keep, b2=b2, c1=c1):
                    here = ((l, c), q_keep, cols_at)
                    srcs = [(p_ab, *here), (own_ab, *here), (r1, (l, c, s), b2 * ru, cols_at), (r2, (l, c, s), 0, cols_at)]
                    if more >= 1:
                        srcs.append((r3, (l, c, s), 0, cols_at - c1 * HC))
                    if more >= 2:
                        srcs.append((r4, (l, c, s), 0, 0))
                    total((p_ab, *here), srcs, ru, cols)

                w3 = functools.partial(rest, (1 - c1) * HC, HC, 0)
                w4 = functools.partial(rest, c1 * HC + (1 - c2) * QC, QC, 1)
                w5 = functools.partial(rest, c1 * HC + c2 * QC, QC, 2)
                ea = event([d2d["send", l, c, s]], [begin], w1, adds(2 * ru, 8 * cu, 2), [t1])
                eb = event([d2d["keep", l, c, s], t1], [ea], w2, adds(ru, 8 * cu, 3), [t2])
                ec = event([t2], [eb], w3, adds(ru, HC, 4), [t3])
                ed = event([t3], [ec], w4, adds(ru, QC, 5), [t4])
                ends.append(event([t4], [ed], w5, adds(ru, QC, 6), []))

        def piece(zz):
            c, k = div(zz, 4), rem(zz, 4)
            s, h = div(k, 2), rem(k, 2)
            qx = quarter(0, x) + s * (quarter(1, x) - quarter(0, x))
            qy = quarter(0, y) + s * (quarter(1, y) - quarter(0, y))
            q, cq = qx + c * (qy - qx), qy + c * (qx - qy)
            return c, s * S + q * ru, cq * QC + h * cu

        tz = []
        for d in range(1, NZ):
            zz = rem(z + d, NZ)
            c, a, b = piece(zz)
            tz.append(xfer("z+" if d <= 4 else "z-", ru, cu, functools.partial(lambda l, c, a, b: p_ab.at[l, c, R(a, ru), C(b, cu)], l, c, a, b),
                           functools.partial(lambda l, d: rz.at[l, d - 1], l, d), at(z_=zz), hops=min(d, NZ - d)))
        ez = event([], ends, lambda: None, 0.05, tz)
        mc, ma, mb = piece(z)
        keep_ab = pltpu.make_async_copy(f_ab.at[l], gu_out.at[mc, l, R(core * 2 * S + ma, ru), C(mb, cu)], keep_sem.at[l, 0])

        def wz(l=l, mc=mc, ma=ma, mb=mb, keep_ab=keep_ab):
            total((f_ab, (l,), 0, 0), [(p_ab, (l, mc), ma, mb)] + [(rz, (l, d), 0, 0) for d in range(NZ - 1)], ru, cu)
            add_squares(f_ab, (l,), 1.0)
            keep_ab.start()

        ta = [xfer("z+" if d <= 4 else "z-", ru, cu, functools.partial(lambda l: f_ab.at[l], l),
                   functools.partial(lambda l, c, a, b: gu_out.at[c, l, R(core * 2 * S + a, ru), C(b, cu)], l, mc, ma, mb), at(z_=rem(z + d, NZ)), hops=min(d, NZ - d))
              for d in range(1, NZ)]
        ef = event(tz, [ez], wz, 0.5, ta)
        pieces_done[l] = [ef]
        eg0 = event(ta, [ef], keep_ab.wait, 0.1, [])
        for c in range(2):
            ri, ci = (x, y) if c == 0 else (y, x)
            rax, cax = ("x", "y") if c == 0 else ("y", "x")
            rdev = (lambda i: at(x_=i)) if c == 0 else (lambda i: at(y_=i))
            cdev = (lambda i: at(y_=i)) if c == 0 else (lambda i: at(x_=i))
            for s in range(2):
                e1, e2 = ("e1", "e2") if s == 0 else ("e2", "e1")
                base = core * 2 * S + s * S

                def same(link, rows, cols, row, col, dev, l=l, c=c, base=base):
                    ref = functools.partial(lambda l, c, row, col, rows, cols: gu_out.at[c, l, R(row, rows), C(col, cols)], l, c, base + row, col, rows, cols)
                    return xfer(link, rows, cols, ref, ref, dev)

                q, q2 = quarter(s, ri), quarter(s, second(s, ri))
                ja = same(cax + e2, ru, QC, q * ru, quarter(s, ci) * QC, cdev(second(s, ci)))
                jb = same(cax + e1, ru, HC, q * ru, half(s, ci) * HC, cdev(first(s, ci)))
                jc = same(rax + e2, ru, 8 * cu, q * ru, 0, rdev(second(s, ri)))
                jd = same(rax + e1, ru, 8 * cu, q * ru, 0, rdev(first(s, ri)))
                je = same(rax + e1, ru, 8 * cu, q2 * ru, 0, rdev(first(s, ri)))
                f1 = quarter(s, first(s, ri))
                f2 = quarter(s, second(s, first(s, ri)))
                fw = [same("d2d", ru, 8 * cu, k * ru, 0, at(c_=other)) for k in (q, q2, f1, f2)]
                eg = event([], [eg0], lambda: None, 0.02, [ja])
                eh = event([ja], [eg], lambda: None, 0.02, [jb])
                ei = event([jb], [eh], lambda: None, 0.02, [jc, jd, fw[0]])
                ej = event([jc], [ei], lambda: None, 0.02, [je, fw[1]])
                ek = event([jd], [ej], lambda: None, 0.02, [fw[2]])
                event([je], [ek], lambda: None, 0.02, [fw[3]])
                arrived += fw

        for s in range(2):
            e1, e2 = ("xe1", "xe2") if s == 0 else ("xe2", "xe1")
            zl = "z+" if s == 0 else "z-"
            sg = 1 if s == 0 else -1
            nxt = at(z_=rem(z + sg + NZ, NZ))
            chunk = lambda t, sg=sg: rem(z - sg * (t + 1) + 2 * NZ, NZ)
            b1, b2 = half(s, x), part(s, x)
            base = s * 8 * ZR
            ring = []
            for t in range(NZ - 1):
                src = (functools.partial(lambda l, a: p_c.at[l, R(a, ZR), :], l, base + chunk(0) * ZR) if t == 0
                       else functools.partial(lambda l, s, t: rc.at[l, s, t - 1], l, s, t))
                ring.append(xfer(zl, ZR, DC, src, functools.partial(lambda l, s, t: rc.at[l, s, t], l, s, t), nxt))

            def wc0(l=l, a=base + chunk(0) * ZR):
                need((l, 2))
                here = ((l,), a, 0)
                total((p_c, *here), [(p_c, *here), (own_c, *here)], ZR, DC)

            def wcr(t, rows, cols, row, col, more, l=l, s=s, base=base, chunk=chunk):
                here = ((l,), base + chunk(t) * ZR + row, col)
                into = (rc, (l, s, t - 1), row, col)
                total(into, [into, (p_c, *here), (own_c, *here)] + more, rows, cols)

            ev = event([d2d["c", l, s]], [begin], wc0, adds(ZR, DC, 2), [ring[0]])
            for t in range(1, NZ - 1):
                ev = event([ring[t - 1]], [ev], functools.partial(wcr, t, ZR, DC, 0, 0, []), adds(ZR, DC, 3), [ring[t]])
            tx1 = xfer(e1, ru, DC, functools.partial(lambda l, s, a: rc.at[l, s, NZ - 2, R(a, ru), :], l, s, (1 - b1) * ru),
                       functools.partial(lambda l, s: rx1.at[l, s], l, s), at(x_=first(s, x)))
            tx2 = xfer(e2, ru, cu, functools.partial(lambda l, s, a, b: rc.at[l, s, NZ - 2, R(a, ru), C(b, cu)], l, s, b1 * ru, (1 - b2) * cu),
                       functools.partial(lambda l, s: rx2.at[l, s], l, s), at(x_=second(s, x)))
            ev = event([ring[NZ - 2]], [ev], functools.partial(wcr, NZ - 1, ru, DC, (1 - b1) * ru, 0, []), adds(ru, DC, 3), [tx1])
            ev = event([tx1], [ev], functools.partial(wcr, NZ - 1, ru, cu, b1 * ru, (1 - b2) * cu, [(rx1, (l, s), 0, (1 - b2) * cu)]), adds(ru, cu, 4), [tx2])

            def wx(l=l, s=s, base=base, b1=b1, b2=b2):
                row, col = b1 * ru, b2 * cu
                here = ((l,), base + z * ZR + row, col)
                total((ry, (l, s, y), 0, 0),
                      [(rc, (l, s, NZ - 2), row, col), (p_c, *here), (own_c, *here), (rx1, (l, s), 0, col), (rx2, (l, s), 0, 0)], ru, cu)

            mine = functools.partial(lambda l, s: ry.at[l, s, y], l, s)
            tys = [xfer("ye1" if d != 3 else "ye2", ru, cu, mine, mine, at(y_=rem(y + d, NY)), hops=2 if d == 2 else 1) for d in range(1, NY)]
            ev = event([tx2], [ev], wx, adds(ru, cu, 5), tys)
            g_base = core * 16 * ZR + base
            keep_c = pltpu.make_async_copy(rx2.at[l, s], dn_out.at[l, R(g_base + z * ZR + b1 * ru, ru), C(b2 * cu, cu)], keep_sem.at[l, 1 + s])

            def wy(l=l, s=s, keep_c=keep_c):
                total((rx2, (l, s), 0, 0), [(ry, (l, s, k), 0, 0) for k in range(NY)], ru, cu)
                add_squares(rx2, (l, s), 0.25)
                keep_c.start()

            def same_c(link, rows, cols, row, col, dev, src=None, l=l, g_base=g_base):
                ref = functools.partial(lambda l, row, col, rows, cols: dn_out.at[l, R(row, rows), C(col, cols)], l, g_base + row, col, rows, cols)
                return xfer(link, rows, cols, src or ref, ref, dev)

            ha = same_c(e2, ru, cu, z * ZR + b1 * ru, b2 * cu, at(x_=second(s, x)), src=functools.partial(lambda l, s: rx2.at[l, s], l, s))
            hb = same_c(e1, ru, DC, z * ZR + b1 * ru, 0, at(x_=first(s, x)))
            ev = event(tys, [ev], wy, 0.3, [ha])
            pieces_done[l].append(ev)
            ev = event([ha], [ev], keep_c.wait, 0.1, [hb])
            got, prev = hb, ev
            for t in range(NZ):
                held = rem(z - sg * t + 2 * NZ, NZ) * ZR
                fwd = [same_c("d2d", ZR, DC, held, 0, at(c_=other))]
                arrived += fwd
                go = [same_c(zl, ZR, DC, held, 0, nxt)] if t < NZ - 1 else []
                prev = event([got], [prev], lambda: None, 0.02, go + fwd)
                got = go[0] if go else None

    def stage(ref, slot, n, peers_, pre, waits, work):
        mine = lambda: ref.at[slot]
        ts = [Xfer("n", 4096, mine, mine, p) for p in peers_]
        xfers.extend(ts)
        return ts, event(waits, pre, work, 0.1, ts)

    def put(ref, slot, from_):
        def work():
            if from_ is None:
                ref[slot] = acc[...]
            else:
                r, n = from_
                s = r[0]
                for k in range(1, n):
                    s = s + r[k]
                ref[slot] = s
        return work

    ts, ev = stage(nz, z, NZ, [at(z_=rem(z + d, NZ)) for d in range(1, NZ)], pieces_done[0] + pieces_done[1], [], put(nz, z, None))
    ts, ev = stage(ny, y, NY, [at(y_=rem(y + d, NY)) for d in range(1, NY)], [ev], ts, put(ny, y, (nz, NZ)))
    ts, ev = stage(nx, x, NX, [at(x_=rem(x + d, NX)) for d in range(1, NX)], [ev], ts, put(nx, x, (ny, NY)))
    ts, ev = stage(nc, core, 2, [at(c_=other)], [ev], ts, put(nc, core, (nx, NX)))

    def last():
        sq_out[...] = nc[0] + nc[1]

    event(ts, [ev], last, 0.1, [])
    event(arrived, [], lambda: None, 0.1, [])

    ids = {id(t): k for k, t in enumerate(xfers)}
    assert len(ids) <= send_sem.shape[0], len(ids)
    ordered, _ = order_of(events)
    for e in ordered:
        for t in e.waits:
            t.copy.wait_recv()
        e.work()
        for t in e.sends:
            k = ids[id(t)]
            t.copy = pltpu.make_async_remote_copy(src_ref=t.src(), dst_ref=t.dst(), send_sem=send_sem.at[k], recv_sem=recv_sem.at[k],
                                                  device_id={"dp": t.dev}, device_id_type=MESH)
            t.copy.start()
    for t in xfers:
        t.copy.wait_send()


N_XFERS = 320


def all_reduce(ru, cu, g1, u1, d1, g0, u0, d0):
    rows, ff, d = 16 * ru // 2 * 1, 8 * cu, 2 * cu
    S, ZR, DC = 4 * ru, 2 * ru, 2 * cu
    any_ = pl.BlockSpec(memory_space=pl.ANY)
    V = pltpu.VMEM
    return pl.pallas_call(
        functools.partial(comm_kernel, ru, cu),
        name="grad_sum",
        out_shape=(jax.ShapeDtypeStruct((2, 2, *g1.shape), BF16), jax.ShapeDtypeStruct((2, *d1.shape), BF16), jax.ShapeDtypeStruct((8, 128), F32)),
        in_specs=[any_] * 6,
        out_specs=(any_, any_, pl.BlockSpec(memory_space=pltpu.VMEM)),
        scratch_shapes=[
            V((2, 2, 2 * S, 8 * cu), BF16), V((2, 16 * ZR, DC), BF16),
            V((2, 2, 2 * S, 8 * cu), BF16), V((2, 16 * ZR, DC), BF16),
            V((2, 2, 2, 2 * ru, 8 * cu), BF16), V((2, 2, 2, ru, 8 * cu), BF16), V((2, 2, 2, ru, 4 * cu), BF16), V((2, 2, 2, ru, 2 * cu), BF16),
            V((2, NZ - 1, ru, cu), BF16), V((2, 2, NZ - 1, ZR, DC), BF16), V((2, 2, ru, DC), BF16), V((2, 2, ru, cu), BF16), V((2, 2, NY, ru, cu), BF16),
            V((2, ru, cu), BF16), V((8, 128), F32), V((NZ, 8, 128), F32), V((NY, 8, 128), F32), V((NX, 8, 128), F32), V((2, 8, 128), F32),
            pltpu.SemaphoreType.DMA((N_XFERS,)), pltpu.SemaphoreType.DMA((N_XFERS,)), pltpu.SemaphoreType.DMA((2, 3)), pltpu.SemaphoreType.DMA((2, 3)),
        ],
        compiler_params=pltpu.CompilerParams(collective_id=0, has_side_effects=True, vmem_limit_bytes=50 * 2**20),
    )(g1, u1, d1, g0, u0, d0)


def solution(mesh):
    def step(x, dy, *arrays):
        weights, m, v = (arrays[i : i + 3] for i in (0, 3, 6))
        layers = weights[0].shape[0]
        h, kept = x[0], []
        for number in range(layers):
            kept.append(h)
            h = layer(h, {name: w[number] for name, w in zip(NAMES, weights, strict=True)})
        by_h, by_w = dy[0], [None] * layers
        for number in reversed(range(layers)):
            _, back = jax.vjp(lambda w, h: layer(h, w), {name: w[number] for name, w in zip(NAMES, weights, strict=True)}, kept[number])
            by_w[number], by_h = back(by_h)
        d, ff = weights[0].shape[1:]
        gu, down, squares = all_reduce(d // 16, ff // 8, *[by_w[number][name] for number in (1, 0) for name in NAMES])
        gradients = [gu[0], gu[1], down]
        count = sum(g.size for g in gradients)
        factor = jnp.minimum(1.0, 0.5 * lax.rsqrt(jnp.sum(squares) / count + 1e-30))
        new = [adamw(w.astype(jnp.float32), m, v, g.astype(jnp.float32) * factor) for w, m, v, g in zip(weights, m, v, gradients, strict=True)]
        return tuple(one[which] for which in range(3) for one in new)

    return jax.shard_map(
        step,
        mesh=mesh,
        in_specs=(P(("rep", "dp"), None, None),) * 2 + (P(None, None, None),) * 9,
        out_specs=(P("rep", None, None),) * 9,
        check_vma=False,
    )
```

time: 725 us -> 453 us (0.62)
  waiting for transfers between devices: 415 us -> 0 us
  Pallas kernels: 0 us -> 169 us
  other arithmetic: 126 us -> 109 us
  between operations: 16.8 us -> 1.99 us
    psum x1 -> x0, waiting for transfers between devices: 415 us -> none  [step(): summed[number] = [lax.psum(by_w[name], 'dp') for name in NAMES]]
    pallas_call x0 -> x1, Pallas kernels: none -> 169 us  [all_reduce(): pl.pallas_call(functools.partial(comm_kernel, ru, cu), name='grad_sum', o...]
    reduce_sum x3 -> x1, other arithmetic: 24.1 us -> 0.6 us  [step(): factor = jnp.minimum(1.0, 0.5 * lax.rsqrt(jnp.sum(squares) / count + 1e-30))]
  transfers between devices with their start and end apart: 1 -> 0, of which waited for: 1 -> 0; matrix products, arithmetic and copies ran while one was open for 0% -> 0% of each run, Pallas kernels for 0% -> 0%
where the time goes in v1:
time: 453 us; the launch traced here: 446 us
  Pallas kernels  169 us (37%)
  matrix products  162 us (36%)
  other arithmetic  109 us (24%)
    pallas_call x1, Pallas kernels, all_reduce(): pl.pallas_call(functools.partial(comm_kernel, ru, cu), name='grad_sum', o...  169 us
    convert_element_type x2, other arithmetic, adamw(): return ((w - 0.02 * step).astype(jnp.bfloat16), m, v)  105 us
    dot_general x5, matrix products, layer(): gate = jnp.dot(a, w['w_gate'], preferred_element_type=jnp.float32)  62.1 us
    dot_general x5, matrix products, layer(): up = jnp.dot(a, w['w_up'], preferred_element_type=jnp.float32)  50.1 us
    dot_general x5, matrix products, matmul(): jnp.dot(a, w, preferred_element_type=jnp.float32).astype(jnp.bfloat16)  49.5 us

profile of v1, /device:TPU:1, one launch (start us, length us, event | category | flops | bytes accessed | tf_op | source)
XLA Modules:
  0.0 445.9 jit_solution(65384666149752162)
XLA Ops:
  0.6 1.7 copy.20
  2.4 0.4 fusion.59
  2.8 11.6 %fusion.48 = f32[1024,3072]{1,0:T(8,128)} fusion(bf16[2,768,3072]{2,1,0:T(8,128)(2,1)} %param.13, bf16[1,1024,768]{2,1,0:T(8,128)(2,1)} %param.11, f32[1024]{0:T(1024)S(1)} %add_rsqrt_fusion), kind=kOutput, calls=%fused_computation.78 | convolution fusion | flops 4834197504 | bytes 18878464 | tf_op jit(solution)/shard_map/dot_general | solution.py:28
  14.4 12.4 %multiply_convert_fusion.1 = (bf16[1024,3072]{1,0:T(8,128)(2,1)}, f32[1024,3072]{1,0:T(8,128)}) fusion(f32[1024,3072]{1,0:T(8,128)} %fusion.48, bf16[2,768,3072]{2,1,0:T(8,128)(2,1)S(1)} %bitcast.83, bf16[1,1024,768]{2,1,0:T(8,128)(2,1)S(1)} %copy-done.2, f32[1024]{0:T(1024)S(1)} %add_rsqrt_fusion), kind=kOutput, calls=%fused_computation.46 | convolution fusion | flops 4853071872 | bytes 37752832 | tf_op jit(solution)/shard_map/dot_general | solution.py:29
  26.8 8.8 %fusion.63 = (f32[1024]{0:T(1024)S(1)}, bf16[1024,768]{0,1:T(8,128)(2,1)S(1)}) fusion(bf16[1024,3072]{1,0:T(8,128)(2,1)} %get-tuple-element.27, bf16[2,3072,768]{2,1,0:T(8,128)(2,1)} %param.15, bf16[1,1024,768]{1,2,0:T(8,128)(2,1)S(1)} %copy.20), kind=kOutput, calls=%fused_computation.96 | convolution fusion | flops 4835769344 | bytes 14159872 | tf_op jit(solution)/shard_map/dot_general | solution.py:17
  35.6 0.6 copy-done.4
  36.2 8.1 %fusion.40 = f32[1024,3072]{1,0:T(8,128)} fusion(bf16[2,768,3072]{2,1,0:T(8,128)(2,1)S(1)} %bitcast.83, bf16[1024,768]{0,1:T(8,128)(2,1)S(1)} %get-tuple-element.30, f32[1024]{0:T(1024)S(1)} %fusion.93), kind=kOutput, calls=%fused_computation.70 | convolution fusion | flops 4834197504 | bytes 18878464 | tf_op jit(solution)/shard_map/jvp()/dot_general | solution.py:29
  44.3 9.8 %convolution_convert_fusion.1 = bf16[1024,3072]{1,0:T(8,128)(2,1)} fusion(bf16[2,3072,768]{2,1,0:T(8,128)(2,1)} %param.15, bf16[1,1024,768]{2,1,0:T(8,128)(2,1)S(1)} %copy-done.3), kind=kOutput, calls=%fused_computation.54 | convolution fusion | flops 4834983936 | bytes 12582912 | tf_op jit(solution)/shard_map/transpose(jvp())/dot_general | solution.py:17
  54.0 18.2 %fusion.16 = (bf16[1024,3072]{1,0:T(8,128)(2,1)}, f32[1024,3072]{1,0:T(8,128)}) fusion(f32[1024,3072]{1,0:T(8,128)} %fusion.40, bf16[1024,3072]{1,0:T(8,128)(2,1)} %convolution_convert_fusion.1, bf16[2,768,3072]{2,1,0:T(8,128)(2,1)} %param.13, bf16[1024,768]{0,1:T(8,128)(2,1)S(1)} %get-tuple-element.30, f32[1024]{0:T(1024)S(1)} %fusion.93), kind=kOutput, calls=%fused_computation.37 | convolution fusion | flops 4871946240 | bytes 44044288 | tf_op jit(solution)/shard_map/jvp()/dot_general | solution.py:28
  72.2 9.6 %convolution_convert_fusion.3.refs_0_ = bf16[768,3072]{1,0:T(8,128)(2,1)} fusion(bf16[1024,3072]{1,0:T(8,128)(2,1)} %get-tuple-element.31, bf16[1024,768]{0,1:T(8,128)(2,1)S(1)} %get-tuple-element.30, f32[1024]{0:T(1024)S(1)} %fusion.93), kind=kOutput, calls=%fused_computation.61 | convolution fusion | flops 4834197504 | bytes 12587008 | tf_op jit(solution)/shard_map/transpose(jvp())/dot_general | solution.py:28
  81.8 10.0 %fusion.33.refs_1_ = bf16[768,3072]{1,0:T(8,128)(2,1)} fusion(bf16[1024,3072]{1,0:T(8,128)(2,1)S(1)} %copy-done.8, bf16[1024,768]{0,1:T(8,128)(2,1)S(1)} %get-tuple-element.30, f32[1024]{0:T(1024)S(1)} %fusion.93, f32[1024,3072]{1,0:T(8,128)} %get-tuple-element.32), kind=kOutput, calls=%fused_computation.63 | convolution fusion | flops 4855431168 | bytes 25169920 | tf_op jit(solution)/shard_map/transpose(jvp())/dot_general | solution.py:29
  91.8 13.2 %fusion.32.refs_2_ = bf16[3072,768]{1,0:T(8,128)(2,1)} fusion(f32[1024,3072]{1,0:T(8,128)} %fusion.40, bf16[1,1024,768]{2,1,0:T(8,128)(2,1)S(1)} %copy-done.3, f32[1024,3072]{1,0:T(8,128)} %get-tuple-element.32), kind=kOutput, calls=%fused_computation.62 | convolution fusion | flops 4853071872 | bytes 31457280 | tf_op jit(solution)/shard_map/transpose(jvp())/dot_general | solution.py:17
  105.1 9.8 %fusion.73 = bf16[1024,768]{0,1:T(8,128)(2,1)S(1)} fusion(bf16[2,768,3072]{2,1,0:T(8,128)(2,1)S(1)} %bitcast.85, bf16[1024,3072]{1,0:T(8,128)(2,1)} %convolution_convert_fusion.1, f32[1024,3072]{1,0:T(8,128)} %get-tuple-element.32), kind=kOutput, calls=%fused_computation.102 | convolution fusion | flops 4851499008 | bytes 25165824 | tf_op jit(solution)/shard_map/transpose(jvp())/dot_general | solution.py:29
  114.9 9.7 %fusion.65 = (f32[1024]{0:T(1024)S(1)}, bf16[1024,768]{0,1:T(8,128)(2,1)}) fusion(bf16[1024,768]{0,1:T(8,128)(2,1)S(1)} %get-tuple-element.30, bf16[1024,768]{0,1:T(8,128)(2,1)S(1)} %fusion.73, bf16[1024,3072]{1,0:T(8,128)(2,1)} %get-tuple-element.31, bf16[2,768,3072]{2,1,0:T(8,128)(2,1)} %param.13), kind=kOutput, calls=%fused_computation.98 | convolution fusion | flops 4835769344 | bytes 15732736 | tf_op jit(solution)/shard_map/transpose(jvp())/dot_general | solution.py:28
  124.6 1.7 copy.21
  126.3 2.5 fusion.77
  128.8 8.1 %convolution_convert_fusion = bf16[1024,3072]{1,0:T(8,128)(2,1)S(1)} fusion(bf16[1024,768]{0,1:T(8,128)(2,1)S(1)} %fusion.77, bf16[2,3072,768]{2,1,0:T(8,128)(2,1)} %param.15), kind=kOutput, calls=%fused_computation.53 | convolution fusion | flops 4834983936 | bytes 12582912 | tf_op jit(solution)/shard_map/transpose(jvp())/dot_general | solution.py:17
  136.9 13.0 %fusion.29.refs_3_ = bf16[768,3072]{1,0:T(8,128)(2,1)} fusion(f32[1024,3072]{1,0:T(8,128)} %fusion.48, f32[1024,3072]{1,0:T(8,128)} %get-tuple-element.28, bf16[1024,3072]{1,0:T(8,128)(2,1)S(1)} %convolution_convert_fusion, bf16[1,1024,768]{1,2,0:T(8,128)(2,1)S(1)} %copy-done.1, f32[1024]{0:T(1024)S(1)} %copy-done.7), kind=kOutput, calls=%fused_computation.59 | convolution fusion | flops 4871159808 | bytes 37752832 | tf_op jit(solution)/shard_map/transpose(jvp())/dot_general | solution.py:28
  150.0 9.9 %fusion.34.refs_4_ = bf16[768,3072]{1,0:T(8,128)(2,1)} fusion(bf16[1024,3072]{1,0:T(8,128)(2,1)S(1)} %convolution_convert_fusion, f32[1024,3072]{1,0:T(8,128)} %fusion.48, bf16[1,1024,768]{1,2,0:T(8,128)(2,1)S(1)} %copy-done.1, f32[1024]{0:T(1024)S(1)} %copy-done.7), kind=kOutput, calls=%fused_computation.64 | convolution fusion | flops 4855431168 | bytes 25169920 | tf_op jit(solution)/shard_map/transpose(jvp())/dot_general | solution.py:29
  159.8 9.7 %convolution_convert_fusion.2.refs_5_ = bf16[3072,768]{1,0:T(8,128)(2,1)} fusion(bf16[1024,3072]{1,0:T(8,128)(2,1)} %get-tuple-element.27, bf16[1024,768]{0,1:T(8,128)(2,1)S(1)} %fusion.77), kind=kOutput, calls=%fused_computation.60 | convolution fusion | flops 4834197504 | bytes 12582912 | tf_op jit(solution)/shard_map/transpose(jvp())/dot_general | solution.py:17
  169.5 169.4 %grad_sum.1 = (bf16[2,2,768,3072]{3,2,1,0:T(8,128)(2,1)}, bf16[2,3072,768]{2,1,0:T(8,128)(2,1)}, f32[8,128]{1,0:T(8,128)S(1)}) custom-call(bf16[768,3072]{1,0:T(8,128)(2,1)} %convolution_convert_fusion.3.refs_0_, bf16[768,3072]{1,0:T(8,128)(2,1)} %fusion.33.refs_1_, bf16[3072,768]{1,0:T(8,128)(2,1)} %fusion.32.refs_2_, bf16[768,3072]{1,0:T(8,128)(2,1)} %fusion.29.refs_3_, ...), custom_call_target="tpu_custom_call" | custom-call | tf_op jit(solution)/shard_map/grad_sum/pallas_call | solution.py:454
  338.9 0.6 reduce_sum.41
  340.2 68.7 %fusion.5 = (bf16[2,768,3072]{2,1,0:T(8,128)(2,1)}, f32[2,768,3072]{2,1,0:T(8,128)}, f32[2,768,3072]{2,1,0:T(8,128)}, bf16[2,768,3072]{2,1,0:T(8,128)(2,1)}, f32...) fusion(bf16[2,768,3072]{2,1,0:T(8,128)(2,1)} %param.14, f32[]{:T(128)S(6)} %min_shard_map.3, ...), kind=kLoop, calls=%fused_computation.16 | loop fusion | flops 160432128 | bytes 207618048 | tf_op jit(solution)/shard_map/convert_element_type | solution.py:37
  408.9 36.6 %fusion.8 = (bf16[2,3072,768]{2,1,0:T(8,128)(2,1)}, f32[2,3072,768]{2,1,0:T(8,128)}, f32[2,3072,768]{2,1,0:T(8,128)}) fusion(bf16[2,3072,768]{2,1,0:T(8,128)(2,1)} %param.15, f32[]{:T(128)S(6)} %min_shard_map.3, bf16[2,3072,768]{2,1,0:T(8,128)(2,1)} %get-tuple-element.14, f32[2,3072,768]{2,1,0:T(8,128)} %param.21, f32[2,3072,768]{2,1,0:T(8,128)} %param.18), kind=kLoop, calls=%fused_computation.19 | loop fusion | flops 80216064 | bytes 103809024 | tf_op jit(solution)/shard_map/convert_element_type | solution.py:37
  (34 shorter events, 0.1 us)
Async XLA Ops:
  2.4 24.5 %copy-start = (bf16[1,1024,768]{1,2,0:T(8,128)(2,1)}, bf16[1,1024,768]{1,2,0:T(8,128)(2,1)S(1)}, u32[]{:S(2)}) copy-start(bf16[1,1024,768]{1,2,0:T(8,128)(2,1)S(1)} %copy.20) | copy-start | bytes 4718596
  2.4 12.0 %slice-start = ((s8[9437184]{0:T(1024)(128)(4,1)}), s8[4194304]{0:T(1024)(128)(4,1)S(1)}, s32[]{:S(2)}) async-start(s8[9437184]{0:T(1024)(128)(4,1)} %bitcast.82), calls=%async_computation | async-start | bytes 8388608
  2.8 11.6 %copy-start.6 = (f32[1024]{0:T(1024)}, f32[1024]{0:T(1024)S(1)}, u32[]{:S(2)}) copy-start(f32[1024]{0:T(1024)S(1)} %add_rsqrt_fusion) | copy-start | bytes 12292
  2.8 11.6 %slice-start.1 = ((s8[9437184]{0:T(1024)(128)(4,1)}), s8[4194304]{0:T(1024)(128)(4,1)S(1)}, s32[]{:S(2)}) async-start(s8[9437184]{0:T(1024)(128)(4,1)} %bitcast.82), calls=%async_computation.1 | async-start | bytes 8388608
  2.8 11.6 %slice-start.2 = ((s8[9437184]{0:T(1024)(128)(4,1)}), s8[1048576]{0:T(1024)(128)(4,1)S(1)}, s32[]{:S(2)}) async-start(s8[9437184]{0:T(1024)(128)(4,1)} %bitcast.82), calls=%async_computation.2 | async-start | bytes 2097152
  2.8 11.6 %copy-start.2 = (bf16[1,1024,768]{2,1,0:T(8,128)(2,1)S(1)}, bf16[1,1024,768]{2,1,0:T(8,128)(2,1)}, u32[]{:S(2)}) copy-start(bf16[1,1024,768]{2,1,0:T(8,128)(2,1)} %param.11) | copy-start | bytes 4718596
  35.6 0.6 copy-start.4
  36.2 8.1 %copy-start.3 = (bf16[1,1024,768]{2,1,0:T(8,128)(2,1)S(1)}, bf16[1,1024,768]{2,1,0:T(8,128)(2,1)}, u32[]{:S(2)}) copy-start(bf16[1,1024,768]{2,1,0:T(8,128)(2,1)} %param.12) | copy-start | bytes 4718596
  72.2 9.6 %copy-start.8 = (bf16[1024,3072]{1,0:T(8,128)(2,1)S(1)}, bf16[1024,3072]{1,0:T(8,128)(2,1)}, u32[]{:S(2)}) copy-start(bf16[1024,3072]{1,0:T(8,128)(2,1)} %convolution_convert_fusion.1) | copy-start | bytes 18874372
  81.8 23.2 %slice-start.3 = ((s8[9437184]{0:T(1024)(128)(4,1)}), s8[4194304]{0:T(1024)(128)(4,1)S(1)}, s32[]{:S(2)}) async-start(s8[9437184]{0:T(1024)(128)(4,1)} %bitcast.84), calls=%async_computation.3 | async-start | bytes 8388608
  81.8 23.2 %slice-start.4 = ((s8[9437184]{0:T(1024)(128)(4,1)}), s8[4194304]{0:T(1024)(128)(4,1)S(1)}, s32[]{:S(2)}) async-start(s8[9437184]{0:T(1024)(128)(4,1)} %bitcast.84), calls=%async_computation.4 | async-start | bytes 8388608
  91.8 13.2 %slice-start.5 = ((s8[9437184]{0:T(1024)(128)(4,1)}), s8[1048576]{0:T(1024)(128)(4,1)S(1)}, s32[]{:S(2)}) async-start(s8[9437184]{0:T(1024)(128)(4,1)} %bitcast.84), calls=%async_computation.5 | async-start | bytes 2097152
  114.8 11.4 %copy-start.5 = (f32[1024]{0:T(1024)S(1)}, f32[1024]{0:T(1024)}, u32[]{:S(2)}) copy-start(f32[1024]{0:T(1024)} %copy-done.4) | copy-start | bytes 12292
  128.8 8.1 %copy-start.1 = (bf16[1,1024,768]{1,2,0:T(8,128)(2,1)S(1)}, bf16[1,1024,768]{1,2,0:T(8,128)(2,1)}, u32[]{:S(2)}) copy-start(bf16[1,1024,768]{1,2,0:T(8,128)(2,1)} %copy-done) | copy-start | bytes 4718596
  128.8 8.1 %copy-start.7 = (f32[1024]{0:T(1024)S(1)}, f32[1024]{0:T(1024)}, u32[]{:S(2)}) copy-start(f32[1024]{0:T(1024)} %copy-done.6) | copy-start | bytes 12292

commit v2 on v1

--- a/solution.py
+++ b/solution.py
@@ -7,27 +7,177 @@
 from jax.experimental.pallas import tpu as pltpu
 from jax.sharding import PartitionSpec as P
 
-NAMES = ("w_gate", "w_up", "w_down")
 MESH = pl.DeviceIdType.MESH
 NX, NY, NZ = 4, 4, 8
 F32, BF16 = jnp.float32, jnp.bfloat16
 
 
-def matmul(a, w):
-    return jnp.dot(a, w, preferred_element_type=jnp.float32).astype(jnp.bfloat16)
-
-
-def normed(h):
-    wide = h.astype(jnp.float32)
-    scale = lax.rsqrt(jnp.mean(wide**2, -1, keepdims=True) + 1e-6)
-    return (wide * scale).astype(jnp.bfloat16)
-
-
-def layer(h, w):
-    a = normed(h)
-    gate = jnp.dot(a, w["w_gate"], preferred_element_type=jnp.float32)
-    up = jnp.dot(a, w["w_up"], preferred_element_type=jnp.float32)
-    return h + matmul((jax.nn.silu(gate) * up).astype(jnp.bfloat16), w["w_down"])
+NN = (((1,), (0,)), ((), ()))
+NT = (((1,), (1,)), ((), ()))
+TN = (((0,), (0,)), ((), ()))
+
+
+def dot(a, b, dims=NN):
+    return lax.dot_general(a, b, dims, preferred_element_type=F32)
+
+
+def scale_of(wide):
+    return lax.rsqrt(jnp.mean(wide * wide, -1, keepdims=True) + 1e-6)
+
+
+def normed_f(h):
+    wide = h.astype(F32)
+    return (wide * scale_of(wide)).astype(BF16)
+
+
+def forward_kernel(blocks, tiles, x_ref, wg_ref, wu_ref, wd_ref, g_ref, u_ref, a0_ref, h_ref, a1_ref, total):
+    j = pl.program_id(0)
+    n = x_ref.shape[0]
+    b = n // blocks
+
+    @pl.when(j == 0)
+    def _():
+        def body(k, _):
+            rows = pl.ds(pl.multiple_of(k * 64, 64), 64)
+            a0_ref[rows, :] = normed_f(x_ref[rows, :])
+            total[rows, :] = jnp.zeros((64, total.shape[1]), F32)
+            return 0
+        lax.fori_loop(0, n // 64, body, 0)
+
+    for k in range(blocks):
+        rows = pl.ds(k * b, b)
+        a = a0_ref[rows, :]
+        g = dot(a, wg_ref[0])
+        u = dot(a, wu_ref[0])
+        g_ref[rows, :] = g
+        u_ref[rows, :] = u
+        p = (g * jax.nn.sigmoid(g) * u).astype(BF16)
+        total[rows, :] += dot(p, wd_ref[0])
+
+    @pl.when(j == tiles - 1)
+    def _():
+        def body(k, _):
+            rows = pl.ds(pl.multiple_of(k * 64, 64), 64)
+            h = x_ref[rows, :] + total[rows, :].astype(BF16)
+            h_ref[rows, :] = h
+            a1_ref[rows, :] = normed_f(h)
+            return 0
+        lax.fori_loop(0, n // 64, body, 0)
+
+
+def forward(x, wg, wu, wd, tile=512, blocks=4):
+    n, d = x.shape
+    ff = wg.shape[2]
+    tiles = ff // tile
+    whole = pl.BlockSpec((n, d), lambda j: (0, 0))
+    return pl.pallas_call(
+        functools.partial(forward_kernel, blocks, tiles),
+        name="layer0_forward",
+        grid=(tiles,),
+        in_specs=[whole, pl.BlockSpec((1, d, tile), lambda j: (0, 0, j)), pl.BlockSpec((1, d, tile), lambda j: (0, 0, j)), pl.BlockSpec((1, tile, d), lambda j: (0, j, 0))],
+        out_specs=[pl.BlockSpec((n, tile), lambda j: (0, j)), pl.BlockSpec((n, tile), lambda j: (0, j)), whole, whole, whole],
+        out_shape=[jax.ShapeDtypeStruct((n, ff), F32)] * 2 + [jax.ShapeDtypeStruct((n, d), BF16)] * 3,
+        scratch_shapes=[pltpu.VMEM((n, d), F32)],
+        compiler_params=pltpu.CompilerParams(dimension_semantics=("arbitrary",), vmem_limit_bytes=60 * 2**20),
+        cost_estimate=pl.CostEstimate(flops=6 * n * d * ff, bytes_accessed=8 * n * ff + 6 * d * ff + 8 * n * d, transcendentals=n * ff),
+    )(x, wg, wu, wd)
+
+
+def backward_tile(g, u, dp):
+    sig = jax.nn.sigmoid(g)
+    act = g * sig
+    p = (act * u).astype(BF16)
+    du = (dp * act).astype(BF16)
+    dg = (dp * u * (sig + act * (1.0 - sig))).astype(BF16)
+    return p, dg, du
+
+
+def last_kernel(blocks, tiles, a_ref, h_ref, dy_ref, wg_ref, wu_ref, wd_ref, dwg_ref, dwu_ref, dwd_ref, dh_ref, p_s, dg_s, du_s, by_g, by_u):
+    j = pl.program_id(0)
+    n, d = a_ref.shape
+    b = n // blocks
+
+    @pl.when(j == 0)
+    def _():
+        def body(k, _):
+            rows = pl.ds(pl.multiple_of(k * 64, 64), 64)
+            by_g[rows, :] = jnp.zeros((64, d), F32)
+            by_u[rows, :] = jnp.zeros((64, d), F32)
+            return 0
+        lax.fori_loop(0, n // 64, body, 0)
+
+    for k in range(blocks):
+        rows = pl.ds(k * b, b)
+        a = a_ref[rows, :]
+        g = dot(a, wg_ref[0])
+        u = dot(a, wu_ref[0])
+        dp = dot(dy_ref[rows, :], wd_ref[0], NT).astype(BF16).astype(F32)
+        p, dg, du = backward_tile(g, u, dp)
+        p_s[rows, :], dg_s[rows, :], du_s[rows, :] = p, dg, du
+        by_g[rows, :] += dot(dg, wg_ref[0], NT)
+        by_u[rows, :] += dot(du, wu_ref[0], NT)
+    dwg_ref[...] = dot(a_ref[...], dg_s[...], TN).astype(BF16)
+    dwu_ref[...] = dot(a_ref[...], du_s[...], TN).astype(BF16)
+    dwd_ref[...] = dot(p_s[...], dy_ref[...], TN).astype(BF16)
+
+    @pl.when(j == tiles - 1)
+    def _():
+        def body(k, _):
+            rows = pl.ds(pl.multiple_of(k * 32, 32), 32)
+            by_a = (by_g[rows, :].astype(BF16) + by_u[rows, :].astype(BF16)).astype(F32)
+            wide = h_ref[rows, :].astype(F32)
+            s = scale_of(wide)
+            by_h = by_a * s - wide * (s * s * s * jnp.mean(by_a * wide, -1, keepdims=True))
+            dh_ref[rows, :] = dy_ref[rows, :] + by_h.astype(BF16)
+            return 0
+        lax.fori_loop(0, n // 32, body, 0)
+
+
+def last(a, h, dy, wg, wu, wd, tile=512, blocks=4):
+    n, d = a.shape
+    ff = wg.shape[2]
+    tiles = ff // tile
+    whole = pl.BlockSpec((n, d), lambda j: (0, 0))
+    return pl.pallas_call(
+        functools.partial(last_kernel, blocks, tiles),
+        name="layer1_both",
+        grid=(tiles,),
+        in_specs=[whole] * 3 + [pl.BlockSpec((1, d, tile), lambda j: (1, 0, j)), pl.BlockSpec((1, d, tile), lambda j: (1, 0, j)), pl.BlockSpec((1, tile, d), lambda j: (1, j, 0))],
+        out_specs=[pl.BlockSpec((d, tile), lambda j: (0, j)), pl.BlockSpec((d, tile), lambda j: (0, j)), pl.BlockSpec((tile, d), lambda j: (j, 0)), whole],
+        out_shape=[jax.ShapeDtypeStruct((d, ff), BF16), jax.ShapeDtypeStruct((d, ff), BF16), jax.ShapeDtypeStruct((ff, d), BF16), jax.ShapeDtypeStruct((n, d), BF16)],
+        scratch_shapes=[pltpu.VMEM((n, tile), BF16)] * 3 + [pltpu.VMEM((n, d), F32)] * 2,
+        compiler_params=pltpu.CompilerParams(dimension_semantics=("arbitrary",), vmem_limit_bytes=60 * 2**20),
+        cost_estimate=pl.CostEstimate(flops=16 * n * d * ff, bytes_accessed=12 * d * ff + 8 * n * d, transcendentals=n * ff),
+    )(a, h, dy, wg, wu, wd)
+
+
+def first_kernel(blocks, a_ref, dh_ref, g_ref, u_ref, wd_ref, dwg_ref, dwu_ref, dwd_ref, p_s, dg_s, du_s):
+    n = a_ref.shape[0]
+    b = n // blocks
+    for k in range(blocks):
+        rows = pl.ds(k * b, b)
+        dp = dot(dh_ref[rows, :], wd_ref[0], NT).astype(BF16).astype(F32)
+        p_s[rows, :], dg_s[rows, :], du_s[rows, :] = backward_tile(g_ref[rows, :], u_ref[rows, :], dp)
+    dwd_ref[...] = dot(p_s[...], dh_ref[...], TN).astype(BF16)
+    dwg_ref[...] = dot(a_ref[...], dg_s[...], TN).astype(BF16)
+    dwu_ref[...] = dot(a_ref[...], du_s[...], TN).astype(BF16)
+
+
+def first_backward(a, dh, g, u, wd, tile=512, blocks=4):
+    n, d = a.shape
+    ff = g.shape[1]
+    whole = pl.BlockSpec((n, d), lambda j: (0, 0))
+    return pl.pallas_call(
+        functools.partial(first_kernel, blocks),
+        name="layer0_backward",
+        grid=(ff // tile,),
+        in_specs=[whole] * 2 + [pl.BlockSpec((n, tile), lambda j: (0, j))] * 2 + [pl.BlockSpec((1, tile, d), lambda j: (0, j, 0))],
+        out_specs=[pl.BlockSpec((d, tile), lambda j: (0, j)), pl.BlockSpec((d, tile), lambda j: (0, j)), pl.BlockSpec((tile, d), lambda j: (j, 0))],
+        out_shape=[jax.ShapeDtypeStruct((d, ff), BF16), jax.ShapeDtypeStruct((d, ff), BF16), jax.ShapeDtypeStruct((ff, d), BF16)],
+        scratch_shapes=[pltpu.VMEM((n, tile), BF16)] * 3,
+        compiler_params=pltpu.CompilerParams(dimension_semantics=("arbitrary",), vmem_limit_bytes=60 * 2**20),
+        cost_estimate=pl.CostEstimate(flops=8 * n * d * ff, bytes_accessed=8 * n * ff + 8 * d * ff + 4 * n * d, transcendentals=n * ff),
+    )(a, dh, g, u, wd)
 
 
 def adamw(w, m, v, g):
@@ -472,17 +622,11 @@
 def solution(mesh):
     def step(x, dy, *arrays):
         weights, m, v = (arrays[i : i + 3] for i in (0, 3, 6))
-        layers = weights[0].shape[0]
-        h, kept = x[0], []
-        for number in range(layers):
-            kept.append(h)
-            h = layer(h, {name: w[number] for name, w in zip(NAMES, weights, strict=True)})
-        by_h, by_w = dy[0], [None] * layers
-        for number in reversed(range(layers)):
-            _, back = jax.vjp(lambda w, h: layer(h, w), {name: w[number] for name, w in zip(NAMES, weights, strict=True)}, kept[number])
-            by_w[number], by_h = back(by_h)
+        gate, up, a0, h, a1 = forward(x[0], *weights)
+        *by_1, by_h = last(a1, h, dy[0], *weights)
+        by_0 = first_backward(a0, by_h, gate, up, weights[2])
         d, ff = weights[0].shape[1:]
-        gu, down, squares = all_reduce(d // 16, ff // 8, *[by_w[number][name] for number in (1, 0) for name in NAMES])
+        gu, down, squares = all_reduce(d // 16, ff // 8, *by_1, *by_0)
         gradients = [gu[0], gu[1], down]
         count = sum(g.size for g in gradients)
         factor = jnp.minimum(1.0, 0.5 * lax.rsqrt(jnp.sum(squares) / count + 1e-30))

time: 453 us -> 387 us (0.85); the launches traced: 446 us -> 386 us
  matrix products: 162 us -> 0 us
  Pallas kernels: 169 us -> 279 us
    dot_general x15 -> x0, matrix products: 162 us -> none  [the longest x5 62.1 us: layer(): gate = jnp.dot(a, w['w_gate'], preferred_element_type=jnp.float32)]
    pallas_call x0 -> x3, Pallas kernels: none -> 110 us  [the longest x1 54.5 us: last(): pl.pallas_call(functools.partial(last_kernel, blocks, tiles), name='layer...]
where the time goes in v2:
time: 387 us; the launch traced here: 386 us
  Pallas kernels  279 us (72%)
  other arithmetic  106 us (27%)
    pallas_call x1, Pallas kernels, all_reduce(): pl.pallas_call(functools.partial(comm_kernel, ru, cu), name='grad_sum', o...  169 us
    convert_element_type x2, other arithmetic, adamw(): return ((w - 0.02 * step).astype(jnp.bfloat16), m, v)  105 us
    pallas_call x1, Pallas kernels, last(): pl.pallas_call(functools.partial(last_kernel, blocks, tiles), name='layer...  54.5 us
    pallas_call x1, Pallas kernels, forward(): pl.pallas_call(functools.partial(forward_kernel, blocks, tiles), name='la...  28 us
    pallas_call x1, Pallas kernels, first_backward(): pl.pallas_call(functools.partial(first_kernel, blocks), name='layer0_back...  27.3 us

profile of v2, /device:TPU:1, one launch (start us, length us, event | category | flops | bytes accessed | tf_op | source)
XLA Modules:
  0.0 386.4 jit_solution(1001428268771056251)
XLA Ops:
  0.6 28.0 %layer0_forward.1 = (f32[1024,3072]{1,0:T(8,128)}, f32[1024,3072]{1,0:T(8,128)}, bf16[1024,768]{1,0:T(8,128)(2,1)}, bf16[1024,768]{1,0:T(8,128)(2,1)}, bf16[1024,768]{1,0:T(8,128)(2,1)}) custom-call(bf16[1024,768]{1,0:T(8,128)(2,1)} %bitcast.16, bf16[2,768,3072]{2,1,0:T(8,128)(2,1)} %wg_ref.3, bf16[2,768,3072]{2,1,0:T(8,128)(2,1)} %wu_ref.3, ...), custom_call_target="tpu_custom_call" | custom-call | flops 14495514624 | bytes 45613056 | tf_op jit(solution)/shard_map/layer0_forward/pallas_call | solution.py:73
  28.6 54.5 %layer1_both.1 = (bf16[768,3072]{1,0:T(8,128)(2,1)}, bf16[768,3072]{1,0:T(8,128)(2,1)}, bf16[3072,768]{1,0:T(8,128)(2,1)}, bf16[1024,768]{1,0:T(8,128)(2,1)}) custom-call(bf16[1024,768]{1,0:T(8,128)(2,1)} %get-tuple-element.24.a_ref, bf16[1024,768]{1,0:T(8,128)(2,1)} %get-tuple-element.25.h_ref, bf16[1024,768]{1,0:T(8,128)(2,1)} %bitcast.17, ...), custom_call_target="tpu_custom_call" | custom-call | flops 38654705664 | bytes 34603008 | tf_op jit(solution)/shard_map/layer1_both/pallas_call | solution.py:141
  83.2 27.3 %layer0_backward.1 = (bf16[768,3072]{1,0:T(8,128)(2,1)}, bf16[768,3072]{1,0:T(8,128)(2,1)}, bf16[3072,768]{1,0:T(8,128)(2,1)}) custom-call(bf16[1024,768]{1,0:T(8,128)(2,1)} %get-tuple-element.29.a_ref, bf16[1024,768]{1,0:T(8,128)(2,1)} %get-tuple-element.30.dh_ref, f32[1024,3072]{1,0:T(8,128)} %get-tuple-element.31.g_ref, ...), custom_call_target="tpu_custom_call" | custom-call | flops 19327352832 | bytes 47185920 | tf_op jit(solution)/shard_map/layer0_backward/pallas_call | solution.py:170
  110.4 169.2 %grad_sum.1 = (bf16[2,2,768,3072]{3,2,1,0:T(8,128)(2,1)}, bf16[2,3072,768]{2,1,0:T(8,128)(2,1)}, f32[8,128]{1,0:T(8,128)S(1)}) custom-call(bf16[768,3072]{1,0:T(8,128)(2,1)} %get-tuple-element.26.refs_0_, bf16[768,3072]{1,0:T(8,128)(2,1)} %get-tuple-element.27.refs_1_, bf16[3072,768]{1,0:T(8,128)(2,1)} %get-tuple-element.28.refs_2_, ...), custom_call_target="tpu_custom_call" | custom-call | tf_op jit(solution)/shard_map/grad_sum/pallas_call | solution.py:604
  279.6 0.6 reduce_sum.9
  280.9 68.9 %fusion.5 = (bf16[2,768,3072]{2,1,0:T(8,128)(2,1)}, f32[2,768,3072]{2,1,0:T(8,128)}, f32[2,768,3072]{2,1,0:T(8,128)}, bf16[2,768,3072]{2,1,0:T(8,128)(2,1)}, f32...) fusion(bf16[2,768,3072]{2,1,0:T(8,128)(2,1)} %wu_ref.3, f32[]{:T(128)S(6)} %min_shard_map.3, ...), kind=kLoop, calls=%fused_computation.14 | loop fusion | flops 160432128 | bytes 207618048 | tf_op jit(solution)/shard_map/convert_element_type | solution.py:187
  349.8 36.6 %fusion.8 = (bf16[2,3072,768]{2,1,0:T(8,128)(2,1)}, f32[2,3072,768]{2,1,0:T(8,128)}, f32[2,3072,768]{2,1,0:T(8,128)}) fusion(bf16[2,3072,768]{2,1,0:T(8,128)(2,1)} %wd_ref.5, f32[]{:T(128)S(6)} %min_shard_map.3, bf16[2,3072,768]{2,1,0:T(8,128)(2,1)} %get-tuple-element.38, f32[2,3072,768]{2,1,0:T(8,128)} %param.21, f32[2,3072,768]{2,1,0:T(8,128)} %param.18), kind=kLoop, calls=%fused_computation.17 | loop fusion | flops 80216064 | bytes 103809024 | tf_op jit(solution)/shard_map/convert_element_type | solution.py:187

commit v3 on v0

v3 whole, which is shorter than its diff:
```python
import functools

import jax
import jax.numpy as jnp
from jax import lax
from jax.experimental import pallas as pl
from jax.experimental.pallas import tpu as pltpu
from jax.sharding import PartitionSpec as P

LOGICAL = pl.DeviceIdType.LOGICAL
NX, NY, NZ, CORES = 4, 4, 8, 2
F32, BF16 = jnp.float32, jnp.bfloat16
NN = (((1,), (0,)), ((), ()))
NT = (((1,), (1,)), ((), ()))
TN = (((0,), (0,)), ((), ()))
ANY = pl.BlockSpec(memory_space=pl.ANY)
VMEM = pl.BlockSpec(memory_space=pltpu.VMEM)
SUBLANES, LANES = 16, 128
TILES, PARTS = 12, 3
BLOCK = (8, LANES)
NUMBER_OF_XFERS = 680


def dot(a, b, dims=NN):
    return lax.dot_general(a, b, dims, preferred_element_type=F32)


def scale_of(wide):
    return lax.rsqrt(jnp.mean(wide * wide, -1, keepdims=True) + 1e-6)


def normed(h):
    wide = h.astype(F32)
    return (wide * scale_of(wide)).astype(BF16)


def by_rows(n, step, body):
    def at(k, _):
        body(pl.ds(pl.multiple_of(k * step, step), step))
        return _

    lax.fori_loop(0, n // step, at, 0)


def turned(a, a_t):
    def slab(k, _):
        at = pl.ds(pl.multiple_of(k * LANES, LANES), LANES)
        a_t[at, :] = a[:, at].T
        return _

    lax.fori_loop(0, a.shape[1] // LANES, slab, 0)


def forward_kernel(blocks, x_ref, wg_ref, wu_ref, wd_ref, g_ref, u_ref, a0_t, h_ref, a1_ref, a1_t, a0_ref, total):
    j = pl.program_id(0)
    n = x_ref.shape[0]
    b = n // blocks

    @pl.when(j == 0)
    def _():
        def body(rows):
            a0_ref[rows, :] = normed(x_ref[rows, :])
            total[rows, :] = jnp.zeros_like(total[rows, :])

        by_rows(n, 64, body)
        turned(a0_ref, a0_t)

    for k in range(blocks):
        rows = pl.ds(k * b, b)
        a = a0_ref[rows, :]
        g = dot(a, wg_ref[0])
        u = dot(a, wu_ref[0])
        for to, by in ((g_ref, g), (u_ref, u)):
            for t in range(to.shape[0]):
                to[t, rows, :] = by[:, t * to.shape[2] : (t + 1) * to.shape[2]]
        p = (g * jax.nn.sigmoid(g) * u).astype(BF16)
        total[rows, :] += dot(p, wd_ref[0])

    @pl.when(j == pl.num_programs(0) - 1)
    def _():
        def body(rows):
            h = x_ref[rows, :] + total[rows, :].astype(BF16)
            h_ref[rows, :] = h
            a1_ref[rows, :] = normed(h)

        by_rows(n, 64, body)
        turned(a1_ref, a1_t)


def blocks_of(shape, *index):
    return pl.BlockSpec(shape, lambda j: tuple(j if i is None else i for i in index))


def forward(x, wg, wu, wd, tile=512, blocks=4):
    (n, d), ff = x.shape, wg.shape[-1]
    whole, wide = blocks_of((n, d), 0, 0), blocks_of((tile * TILES // ff, n, ff // TILES), None, 0, 0)
    turned_ = blocks_of((d, n), 0, 0)
    return pl.pallas_call(
        functools.partial(forward_kernel, blocks),
        name="layer0_forward",
        grid=(ff // tile,),
        in_specs=[whole] + [blocks_of((1, d, tile), 0, 0, None)] * 2 + [blocks_of((1, tile, d), 0, None, 0)],
        out_specs=[wide, wide, turned_, whole, whole, turned_],
        out_shape=[jax.ShapeDtypeStruct((TILES, n, ff // TILES), F32)] * 2 + [jax.ShapeDtypeStruct(s, BF16) for s in ((d, n), (n, d), (n, d), (d, n))],
        scratch_shapes=[pltpu.VMEM((n, d), BF16), pltpu.VMEM((n, d), F32)],
        compiler_params=pltpu.CompilerParams(vmem_limit_bytes=60 << 20),
    )(x, wg, wu, wd)


def backward_tile(g, u, dp):
    sig = jax.nn.sigmoid(g)
    act = g * sig
    return (act * u).astype(BF16), (dp * u * (sig + act * (1.0 - sig))).astype(BF16), (dp * act).astype(BF16)


def div(a, b):
    return lax.div(a, jnp.int32(b))


def rem(a, b):
    return lax.rem(a, jnp.int32(b))


def once(f):
    known = {}

    def g(s, i):
        key = s, id(i)
        if key not in known:
            known[key] = i, f(s, i)
        return known[key][1]

    return g


@once
def first(s, i):
    return NX - 1 - i if s else i + 1 - 2 * rem(i, 2)


def second(s, i):
    return first(1 - s, i)


@once
def half(s, i):
    return div(i, 2) if s else rem(div(i + 1, 2), 2)


@once
def part(s, i):
    return rem(i, 2) if s else div(i, 2)


@once
def quarter(s, i):
    return 2 * half(s, i) + part(s, i)


def place(start, size, unit):
    return pl.ds(start if isinstance(start, int) else pl.multiple_of(start, unit), size)


class Xfer:
    def __init__(self, link, count, hops, src, dst, dev):
        self.link, self.count, self.size, self.src, self.dst, self.dev = link, count, 2 * count * hops, src, dst, dev
        self.arrives = None


class Event:
    def __init__(self, waits, pre, work, cost, sends):
        self.waits, self.pre, self.work, self.cost, self.sends = waits, pre, work, cost, sends
        self.done = None


RATE, CHIP_RATE, DELAY, SLACK = 45.0e3, 450.0e3, 2.2, 0.6
STEPS = ((0.8, 0.8, 0.55, 0.55, 0.55), (0.55, 0.55), (0.45, 0.45, 0.5, 0.5, 0.5))
SLOTS = [part for phase in STEPS for part in phase * TILES]


def order_of(events, slots):
    links, left, groups, clock, done = {}, list(events), [[]], 0.0, 0
    while left:
        best = None
        for e in left:
            if any(done < p if isinstance(p, int) else p.done is None for p in e.pre) or any(t.arrives is None for t in e.waits):
                continue
            ready = max([p.done for p in e.pre if not isinstance(p, int)] + [t.arrives + (SLACK if done < len(slots) else 0.0) for t in e.waits] + [0.0])
            if best is None or max(ready, clock) < best[0]:
                best = (max(ready, clock), e)
        if done < len(slots) and (best is None or best[0] > clock):
            clock += slots[done]
            done += 1
            groups.append([])
            continue
        clock, e = best
        clock += e.cost + 0.02 * (len(e.waits) + len(e.sends))
        e.done = clock
        for t in e.sends:
            begin = max(clock, links.get(t.link, 0.0))
            links[t.link] = begin + t.size / (CHIP_RATE if t.link == "chip" else RATE)
            t.arrives = links[t.link] + DELAY
        left.remove(e)
        groups[-1].append(e)
    return groups, clock


def plan(here, refs, ru, cu):
    x, y, z, core = here
    (own_ab, own_c, p_ab, p_c, r1, r2, r3, r4, rz, rc, rx, ry, f_ab, f_c, acc, norms, gu_out, dn_out, sq_out, total, squares, need, local) = refs
    other = 1 - core
    xfers, events = [], []
    part_of = functools.partial

    devices, me = {}, ((x * NY + y) * NZ + z) * CORES + core
    steps = dict(x=(x, NY * NZ * CORES), y=(y, NZ * CORES), z=(z, CORES), core=(core, 1))

    def at(**to):
        ((axis, there),) = to.items()
        if (axis, id(there)) not in devices:
            i, stride = steps[axis]
            devices[axis, id(there)] = there, me + (there - i) * stride
        return devices[axis, id(there)][1]

    def window(ref, lead, row, rows, col, cols):
        return lambda: ref.at[(*lead, place(row, rows, SUBLANES), place(col, cols, LANES))]

    def block(ref, *lead):
        return lambda: ref.at[lead]

    def xfer(link, count, src, dst, hops=1, **to):
        t = Xfer(link, count, hops, src, dst, at(**to))
        xfers.append(t)
        return t

    others = {axis: [rem(k + d, n) for d in range(1, n)] for axis, k, n in (("x", x, NX), ("y", y, NY), ("z", z, NZ), ("core", core, CORES))}

    def to_all(axis, n, size, src, dst):
        ts = []
        for d in range(1, n):
            to, back = others[axis][d - 1], d * 2 > n
            ts.append(xfer(axis + "+-"[back], size, src(d, to), dst(d, to), n - d if back else d, **{axis: to}))
        return ts

    def event(waits, pre, work=lambda: None, cost=0.03, sends=()):
        e = Event(waits, pre, work, cost, sends)
        events.append(e)
        return e

    def adds(size, n):
        return size * n / 1.6e6 + 0.1

    D, FF = SUBLANES * ru, NZ * cu
    HD, S = D // 2, D // 4
    HC, QC = FF // 2, FF // 4
    CR = cu // 2
    XR = CR // 4
    around = [z * CR] + [to * CR for to in others["z"]]
    arrived, pieces = [], []

    for i in range(2 * PARTS):
        l, f0 = 1 - i // PARTS, i % PARTS * FF
        begin = event([], [(TILES // PARTS) * (i % PARTS + 1) * len(STEPS[0]) + (0 if l else len(SLOTS) - TILES * len(STEPS[0]))], part_of(need, i), 0.3)

        ends = []
        for c in range(2):
            ri, ci, rax, cax = (y, x, "y", "x") if c else (x, y, "x", "y")
            for s in range(2):
                k1, k2, e1, e2 = (i, c), (i, c, s), "+-"[s], "-+"[s]
                b1, b2, c1, c2 = half(s, ri), part(s, ri), half(s, ci), part(s, ci)
                keep = s * S + b1 * 2 * ru
                away, out, q = s * S + (1 - b1) * 2 * ru, keep + (1 - b2) * ru, keep + b2 * ru
                col1, col2, mine = (1 - c1) * HC, c1 * HC + (1 - c2) * QC, c1 * HC + c2 * QC
                t1 = xfer(rax + e1, 2 * ru * FF, window(p_ab, k1, away, 2 * ru, 0, FF), block(r1, *k2), **{rax: first(s, ri)})
                t2 = xfer(rax + e2, ru * FF, window(p_ab, k1, out, ru, 0, FF), block(r2, *k2), **{rax: second(s, ri)})
                t3 = xfer(cax + e1, ru * HC, window(p_ab, k1, q, ru, col1, HC), block(r3, *k2), **{cax: first(s, ci)})
                t4 = xfer(cax + e2, ru * QC, window(p_ab, k1, q, ru, col2, QC), block(r4, *k2), **{cax: second(s, ci)})

                def work(row, col, rows, cols, n, k1=k1, k2=k2, b2=b2, c1=c1):
                    to = (k1, row, col)
                    more = [(r1, k2, (b2 if n > 1 else 1 - b2) * ru, col), (r2, k2, 0, col), (r3, k2, 0, col - c1 * HC), (r4, k2, 0, 0)]
                    total((p_ab, *to), [(p_ab, *to), (own_ab, *to)] + more[:n], rows, cols)

                e, prev = begin, []
                for n, (t, row, col, rows, cols) in enumerate(((t1, away, 0, 2 * ru, FF), (t2, out, 0, ru, FF), (t3, q, col1, ru, HC), (t4, q, col2, ru, QC), (None, q, mine, ru, QC))):
                    e = event(prev, [e], part_of(work, row, col, rows, cols, n), adds(rows * cols, n + 2), [t] if t else [])
                    prev = [t]
                ends.append(e)

        def piece(to):
            c, k = div(to, 4), rem(to, 4)
            s, h = div(k, 2), rem(k, 2)
            qx = quarter(0, x) + s * (quarter(1, x) - quarter(0, x))
            qy = quarter(0, y) + s * (quarter(1, y) - quarter(0, y))
            return c, s * S + (qx + c * (qy - qx)) * ru, (qy + c * (qx - qy)) * QC + h * cu

        def from_piece(d, to, i=i):
            c, a, b = piece(to)
            return window(p_ab, (i, c), a, ru, b, cu)

        tz = to_all("z", NZ, ru * cu, from_piece, lambda d, to, i=i: block(rz, i, d - 1))
        e = event([], ends, sends=tz)
        mc, ma, mb = piece(z)
        home, mine = window(gu_out, (mc, l), core * HD + ma, ru, f0 + mb, cu), block(f_ab, i)

        def work(i=i, mc=mc, ma=ma, mb=mb, mine=mine, home=home):
            total((f_ab, (i,), 0, 0), [(p_ab, (i, mc), ma, mb)] + [(rz, (i, d), 0, 0) for d in range(NZ - 1)], ru, cu)
            squares(f_ab, (i,), 1.0)
            local(i, 0, mine, home).start()

        ta = to_all("z", NZ, ru * cu, lambda d, to, m=mine: m, lambda d, to, h=home: h)
        e = event(tz, [e], work, 0.4, ta)
        pieces.append(e)
        spread = event(ta, [e], lambda i=i, mine=mine, home=home: local(i, 0, mine, home).wait(), 0.1)
        for c in range(2):
            ri, ci, rax, cax = (y, x, "y", "x") if c else (x, y, "x", "y")
            for s in range(2):
                e1, e2 = "+-"[s], "-+"[s]

                def same(link, row, rows, col, cols, l=l, c=c, f0=f0, s=s, **to):
                    ref = window(gu_out, (c, l), core * HD + s * S + row * ru, rows * ru, f0 + col, cols)
                    return xfer(link, rows * ru * cols, ref, ref, **to)

                q, b1 = quarter(s, ri), 2 * half(s, ri)
                ts = [same(cax + e2, q, 1, quarter(s, ci) * QC, QC, **{cax: second(s, ci)}), same(cax + e1, q, 1, half(s, ci) * HC, HC, **{cax: first(s, ci)}),
                      same(rax + e2, q, 1, 0, FF, **{rax: second(s, ri)}), same(rax + e1, b1, 2, 0, FF, **{rax: first(s, ri)})]
                fw = [same("chip", b, 2, 0, FF, core=other) for b in (b1, 2 - b1)]
                e = spread
                for n, t in enumerate(ts):
                    e = event(ts[n - 1 : n], [e], sends=[t] + fw[: n // 3])
                event(ts[-1:], [e], sends=fw[1:])
                arrived += fw

        for s in range(2):
            key, base = (i, s), s * HC
            arms = ((1, "z+", 0, 4 - s), (-1, "z-", 4 - s, 3 + s))
            chunk = lambda k, base=base: base + around[k % NZ]

            def work(slots, row, into, i=i, key=key):
                to = ((i,), row, 0)
                total(into or (p_c, *to), [(p_c, *to), (own_c, *to)] + [(rc, (*key, t), 0, 0) for t in slots], CR, HD)

            ends, lasts = [], []
            for sg, zl, slot, n in arms:
                nxt, e, prev = others["z"][-(sg < 0)], begin, []
                for t in range(n):
                    row, into = chunk(sg * (n - t)), (rc, (*key, slot + t - 1), 0, 0) if t else None
                    ring = xfer(zl, CR * HD, block(rc, *key, slot + t - 1) if t else window(p_c, (i,), row, CR, 0, HD), block(rc, *key, slot + t), z=nxt)
                    e = event(prev, [e], part_of(work, [slot + t - 1] if t else [], row, into), adds(CR * HD, 3), [ring])
                    prev = [ring]
                ends.append(e)
                lasts += prev
            tx = to_all("x", NX, XR * HD, lambda d, to, key=key: window(rc, (*key, 3 - key[1]), to * XR, XR, 0, HD), lambda d, to, key=key: block(rx, *key, d - 1))
            e = event(lasts, ends, part_of(work, [3 - s, NZ - 2], chunk(0), (rc, (*key, 3 - s), 0, 0)), adds(CR * HD, 4), tx)

            def work_x(key=key):
                total((ry, (*key, y), 0, 0), [(rc, (*key, 3 - key[1]), x * XR, 0)] + [(rx, (*key, d), 0, 0) for d in range(NX - 1)], XR, HD)

            mine = block(ry, *key, y)
            ty = to_all("y", NY, XR * HD, lambda d, to, m=mine: m, lambda d, to, m=mine: m)
            e = event(tx, [e], work_x, adds(XR * HD, 4), ty)
            home, mine = window(dn_out, (l,), f0 + base + z * CR + x * XR, XR, core * HD, HD), block(f_c, *key)

            def work_y(key=key, mine=mine, home=home):
                total((f_c, key, 0, 0), [(ry, (*key, k), 0, 0) for k in range(NY)], XR, HD)
                squares(f_c, key, 1.0 / NY)
                local(key[0], 1 + key[1], mine, home).start()

            hx = to_all("x", NX, XR * HD, lambda d, to, m=mine: m, lambda d, to, h=home: h)
            e = event(ty, [e], work_y, 0.3, hx)
            pieces.append(e)
            e = event(hx, [e], lambda key=key, mine=mine, home=home: local(key[0], 1 + key[1], mine, home).wait(), 0.1)
            prev, ends = [[], []], [e, e]
            for t in range(4):
                for k, (sg, zl, slot, n) in enumerate(arms):
                    if t < n:
                        ref = window(dn_out, (l,), f0 + chunk(-sg * t), CR, core * HD, HD)
                        ring = xfer(zl, CR * HD, ref, ref, z=others["z"][-(sg < 0)])
                        ends[k] = event(prev[k], [ends[k]], sends=[ring])
                        prev[k] = [ring]
            ref = window(dn_out, (l,), f0 + base, HC, core * HD, HD)
            arrived.append(xfer("chip", HC * HD, ref, ref, core=other))
            event(prev[0] + prev[1], ends, sends=arrived[-1:])

    e, ts, prev = None, [], None
    for axis, k, n, ref in (("z", z, NZ, norms[0]), ("y", y, NY, norms[1]), ("x", x, NX, norms[2]), ("core", core, CORES, norms[3])):
        def work(ref=ref, k=k, prev=prev):
            if prev is None:
                ref[k] = acc[...]
            else:
                ref[k] = functools.reduce(lambda a, b: a + b, [prev[0][j] for j in range(prev[1])])

        new = [xfer("n", SUBLANES * LANES, block(ref, k), block(ref, k), **{axis: to}) for to in others[axis]]
        e = event(ts, pieces if e is None else [e], work, 0.15, new)
        ts, prev = new, (ref, n)

    def finish():
        sq_out[...] = norms[3][0] + norms[3][1]

    event(ts, [e], finish, 0.1)
    event(arrived, [])
    return xfers, events


def sum_kernel(ru, cu, *refs):
    (a1, a1_t, h, dy, a0_t, gate, up, wg, wu, wd, gu_out, dn_out, sq_out, dg, du, own_ab, own_c, p_ab, p_c, r1, r2, r3, r4, rz, rc, rx, ry, f_ab, f_c,
     acc, nz, ny, nx, nc, dh, send_sem, recv_sem, load_sem, keep_sem, tile_sem, out_sem, in_sem) = refs
    me = lax.axis_index("dp")
    core, z, y, x = rem(me, CORES), rem(div(me, CORES), NZ), rem(div(me, CORES * NZ), NY), div(me, CORES * NZ * NY)
    other = 1 - core
    D = SUBLANES * ru
    HD = D // 2
    n = h.shape[0]
    per = TILES // PARTS
    tile = NZ * cu // per
    partner = me + 1 - 2 * core
    slice_of = lambda j: pl.ds(pl.multiple_of(j * tile, LANES), tile)

    barrier = pltpu.get_barrier_semaphore()
    dev = lambda x, y, z, core: ((x * NY + y) * NZ + z) * CORES + core
    peers = [dev(x, y, z, other)] + [dev(rem(x + d, NX), y, z, core) for d in range(1, NX)]
    peers += [dev(x, rem(y + d, NY), z, core) for d in range(1, NY)] + [dev(x, y, rem(z + d, NZ), core) for d in range(1, NZ)]
    for p in peers:
        pl.semaphore_signal(barrier, inc=1, device_id=p, device_id_type=LOGICAL)
    pl.semaphore_wait(barrier, len(peers))

    def tile_sends(j, srcs=None, slot=0):
        i, cols = div(j, per), slice_of(rem(j, per))
        dsts = [p_ab.at[i, c, :, cols] for c in range(2)] + [p_c.at[i, cols, :]]
        return [pltpu.make_async_remote_copy(src_ref=src, dst_ref=dst, send_sem=out_sem.at[slot, k], recv_sem=in_sem.at[j, k], device_id=partner,
                                             device_id_type=LOGICAL) for k, (src, dst) in enumerate(zip(srcs or dsts, dsts, strict=True))]

    def total(dst, srcs, rows, cols):
        wide = next(cols // k for k in range(1, cols) if cols % (k * LANES) == 0 and cols // k <= 4 * LANES)
        tall = next(rows // k for k in range(1, rows) if rows % (k * SUBLANES) == 0 and rows // k * wide <= SUBLANES * LANES * 16)
        across = cols // wide

        many = rows // tall * across

        def block(i, _):
            if many > 1:
                r, c = (div(i, across) * tall, rem(i, across) * wide) if across > 1 else (i * tall, None)

            def at(a):
                ref, lead, row, col = a
                row, col = (row, col) if many == 1 else (row + r, col if c is None else col + c)
                return ref.at[(*lead, place(row, tall, SUBLANES), place(col, wide, LANES))]

            s = at(srcs[0])[...].astype(F32)
            for a in srcs[1:]:
                s = s + at(a)[...].astype(F32)
            at(dst)[...] = s.astype(BF16)
            return _

        if many > 1:
            lax.fori_loop(0, many, block, 0)
        else:
            block(0, 0)

    def squares(ref, lead, weight):
        rows, cols = ref.shape[len(lead):]
        for r in range(0, rows, SUBLANES):
            v = ref[(*lead, pl.ds(r, SUBLANES), slice(None))].astype(F32)
            v = v * v
            s = acc[...]
            for a in range(0, SUBLANES, BLOCK[0]):
                for b in range(0, cols, LANES):
                    s = s + weight * v[a : a + BLOCK[0], b : b + LANES]
            acc[...] = s

    def need(i):
        def wait(j, _):
            for t in tile_sends(j):
                t.wait_recv()
            return _

        lax.fori_loop(i * per, (i + 1) * per, wait, 0)

    def local(l, k, src, dst):
        return pltpu.make_async_copy(src(), dst(), keep_sem.at[l, k])

    acc[...] = jnp.zeros_like(acc)
    xfers, events = plan((x, y, z, core), (own_ab, own_c, p_ab, p_c, r1, r2, r3, r4, rz, rc, rx, ry, f_ab, f_c, acc, (nz, ny, nx, nc),
                                           gu_out, dn_out, sq_out, total, squares, need, local), ru, cu)
    counts = sorted(t.count for t in xfers)
    ids = {id(t): k for k, t in enumerate(sorted(xfers, key=lambda t: t.count))}
    groups, _ = order_of(events, SLOTS)

    def copy_of(src, dst, k, dev):
        return pltpu.make_async_remote_copy(src_ref=src, dst_ref=dst, send_sem=send_sem.at[k], recv_sem=recv_sem.at[k], device_id=dev, device_id_type=LOGICAL)

    def wait_of(count, k):
        cols = next(c for c in range(NZ * cu, 0, -LANES) if count % (c * SUBLANES) == 0)
        some = p_ab.at[0, 0, pl.ds(0, count // cols), pl.ds(0, cols)]
        return copy_of(some, some, k, me)

    def emit(group):
        for e in group:
            for t in e.waits:
                wait_of(t.count, ids[id(t)]).wait_recv()
            e.work()
            for t in e.sends:
                copy_of(t.src(), t.dst(), ids[id(t)], t.dev).start()

    def choose(j, options):
        middle = len(options) // 2
        if middle == 0:
            emit(options[0])
        elif any(options):
            pl.when(j < middle)(lambda: choose(j, options[:middle]))
            pl.when(j >= middle)(lambda: choose(j - middle, options[middle:]))

    def steps(srcs, bufs, *parts):
        mine = groups[: TILES * len(parts)]
        del groups[: TILES * len(parts)]

        def copies(j, slot):
            return [pltpu.make_async_copy(src(j), buf.at[slot], tile_sem.at[slot, k]) for k, (src, buf) in enumerate(zip(srcs, bufs, strict=True))]

        for t in copies(0, 0):
            t.start()

        def step(j, carry):
            slot = rem(j, 2)
            for t in copies(j, slot):
                t.wait()

            @pl.when(j + 1 < TILES)
            def _():
                for t in copies(j + 1, 1 - slot):
                    t.start()

            for k, part in enumerate(parts):
                part(j, slot)
                choose(j, mine[k :: len(parts)])
            return carry

        lax.fori_loop(0, TILES, step, 0)

    emit(groups.pop(0))
    tail = groups.pop()
    groups.append([])

    def fetch(*pairs):
        copies = [pltpu.make_async_copy(src, dst, load_sem.at[k]) for k, (src, dst) in enumerate(pairs)]
        for t in copies:
            t.start()
        return lambda: [t.wait() for t in copies]

    mine, yours = (pl.ds(pl.multiple_of(c * HD, LANES), HD) for c in (core, other))
    rows_out = pl.ds(pl.multiple_of(other * HD, SUBLANES), HD)
    staged = lambda st_ab, st_c, slot: [st_ab.at[slot, 0, rows_out, :], st_ab.at[slot, 1, rows_out, :], st_c.at[slot, :, yours]]

    def sent(j, slot, st):
        for t in tile_sends(j, staged(*st, slot), slot):
            t.wait_send()

    def term(j, slot, c, a, b, st):
        i, cols = div(j, per), slice_of(rem(j, per))
        st_ab, st_c = st
        if c < 2:
            st_ab[slot, c] = dot(a[...], b[...]).astype(BF16)
            own_ab[i, c, :, cols] = st_ab[slot, c, pl.ds(pl.multiple_of(core * HD, SUBLANES), HD), :]
        else:
            st_c[slot] = dot(a[...], b[...], TN).astype(BF16)
            own_c[i, cols, :] = st_c[slot, :, mine]
            for t in tile_sends(j, staged(st_ab, st_c, slot), slot):
                t.start()

    blocks = [pl.ds(k * (n // 4), n // 4) for k in range(4)]

    def layer_1(wgbuf, wubuf, wdbuf, a_s, a_t, dy_s, p_s, dgbuf, dubuf, *st):
        fetch((a1, a_s), (dy, dy_s), (a1_t, a_t))()

        def outs(j, slot):
            return [pltpu.make_async_copy(buf.at[slot], to.at[j], keep_sem.at[2 * PARTS + slot, k]) for k, (buf, to) in enumerate(((dgbuf, dg), (dubuf, du)))]

        def through(which, j, slot):
            if which == 0:
                @pl.when(j > 1)
                def _():
                    sent(j - 2, slot, st)
                    for t in outs(j - 2, slot):
                        t.wait()

            for rows in blocks[which::2]:
                a = a_s[rows, :]
                dp = dot(dy_s[rows, :], wdbuf[slot], NT).astype(BF16).astype(F32)
                p_s[rows, :], dgbuf[slot, rows, :], dubuf[slot, rows, :] = backward_tile(dot(a, wgbuf[slot]), dot(a, wubuf[slot]), dp)

        def down(j, slot):
            term(j, slot, 2, p_s, dy_s, st)
            for t in outs(j, slot):
                t.start()

        steps([lambda j: wg.at[1, :, slice_of(j)], lambda j: wu.at[1, :, slice_of(j)], lambda j: wd.at[1, slice_of(j), :]], [wgbuf, wubuf, wdbuf], functools.partial(through, 0),
              functools.partial(through, 1), lambda j, slot: term(j, slot, 0, a_t, dgbuf.at[slot], st), lambda j, slot: term(j, slot, 1, a_t, dubuf.at[slot], st), down)
        for k in range(2):
            sent(TILES - 2 + k, k, st)
            for t in outs(TILES - 2 + k, k):
                t.wait()

    V = lambda *s: pltpu.VMEM(s, BF16)
    W = lambda *s: pltpu.VMEM(s, F32)
    stages = V(2, 2, D, tile), V(2, tile, D)
    pl.run_scoped(layer_1, V(2, D, tile), V(2, D, tile), V(2, tile, D), V(n, D), V(D, n), V(n, D), V(n, tile), V(2, n, tile), V(2, n, tile), *stages)

    def by_input(gbuf, ubuf, wgbuf, wubuf, by_g, by_u, h_s, dy_s):
        arrived = fetch((h, h_s), (dy, dy_s))

        def clear(rows):
            by_g[rows, :] = jnp.zeros_like(by_g[rows, :])
            by_u[rows, :] = jnp.zeros_like(by_u[rows, :])

        by_rows(n, 64, clear)

        def part(which, j, slot):
            for rows in blocks[which::2]:
                by_g[rows, :] += dot(gbuf[slot, rows, :], wgbuf[slot], NT)
                by_u[rows, :] += dot(ubuf[slot, rows, :], wubuf[slot], NT)

        steps([lambda j: dg.at[j], lambda j: du.at[j], lambda j: wg.at[1, :, slice_of(j)], lambda j: wu.at[1, :, slice_of(j)]], [gbuf, ubuf, wgbuf, wubuf],
              functools.partial(part, 0), functools.partial(part, 1))
        arrived()

        def back(rows):
            by_a = (by_g[rows, :].astype(BF16) + by_u[rows, :].astype(BF16)).astype(F32)
            wide = h_s[rows, :].astype(F32)
            s = scale_of(wide)
            by_h = by_a * s - wide * (s * s * s * jnp.mean(by_a * wide, -1, keepdims=True))
            dh[rows, :] = dy_s[rows, :] + by_h.astype(BF16)

        by_rows(n, 32, back)

    pl.run_scoped(by_input, V(2, n, tile), V(2, n, tile), V(2, D, tile), V(2, D, tile), W(n, D), W(n, D), V(n, D), V(n, D))

    def layer_0(gbuf, ubuf, wbuf, a_t, p_s, dg_s, du_s, *st):
        fetch((a0_t, a_t))()

        def through(which, j, slot):
            if which == 0:
                @pl.when(j > 1)
                def _():
                    sent(TILES + j - 2, slot, st)

            for rows in blocks[which::2]:
                dp = dot(dh[rows, :], wbuf[slot], NT).astype(BF16).astype(F32)
                p_s[rows, :], dg_s[rows, :], du_s[rows, :] = backward_tile(gbuf[slot, rows, :], ubuf[slot, rows, :], dp)

        steps([lambda j: gate.at[j], lambda j: up.at[j], lambda j: wd.at[0, slice_of(j), :]], [gbuf, ubuf, wbuf], functools.partial(through, 0),
              functools.partial(through, 1), *[lambda j, slot, k=k: term(TILES + j, slot, *k, st) for k in ((0, a_t, dg_s), (1, a_t, du_s), (2, p_s, dh))])
        for k in range(2):
            sent(2 * TILES - 2 + k, k, st)

    pl.run_scoped(layer_0, W(2, n, tile), W(2, n, tile), V(2, tile, D), V(D, n), V(n, tile), V(n, tile), V(n, tile), *stages)
    emit(tail)
    for count in sorted(set(counts)):
        def wait(k, carry, count=count):
            wait_of(count, k).wait_send()
            return carry

        lax.fori_loop(counts.index(count), counts.index(count) + counts.count(count), wait, 0)


def gradient_sums(a1, a1_t, h, dy, a0_t, gate, up, wg, wu, wd):
    (n, d), ff = h.shape, wg.shape[-1]
    ru, cu = d // SUBLANES, ff // NZ // PARTS
    HD, CR, fs, N = d // 2, cu // 2, ff // PARTS, 2 * PARTS
    V = lambda *s: pltpu.VMEM(s, BF16)
    W = lambda *s: pltpu.VMEM(s, F32)
    DMA = lambda *s: pltpu.SemaphoreType.DMA(s)
    return pl.pallas_call(
        functools.partial(sum_kernel, ru, cu),
        name="gradient_sums",
        out_shape=(jax.ShapeDtypeStruct((2, 2, d, ff), BF16), jax.ShapeDtypeStruct((2, ff, d), BF16), jax.ShapeDtypeStruct(BLOCK, F32)) + (jax.ShapeDtypeStruct((TILES, n, ff // TILES), BF16),) * 2,
        in_specs=[ANY] * 10,
        out_specs=(ANY, ANY, VMEM, ANY, ANY),
        scratch_shapes=[
            V(N, 2, HD, fs), V(N, fs, HD), V(N, 2, HD, fs), V(N, fs, HD),
            V(N, 2, 2, 2 * ru, fs), V(N, 2, 2, ru, fs), V(N, 2, 2, ru, fs // 2), V(N, 2, 2, ru, fs // 4),
            V(N, NZ - 1, ru, cu), V(N, 2, NZ - 1, CR, HD), V(N, 2, NX - 1, CR // 4, HD), V(N, 2, NY, CR // 4, HD), V(N, ru, cu), V(N, 2, CR // 4, HD),
            W(*BLOCK), W(NZ, *BLOCK), W(NY, *BLOCK), W(NX, *BLOCK), W(CORES, *BLOCK),
            V(n, d),
            DMA(NUMBER_OF_XFERS), DMA(NUMBER_OF_XFERS), DMA(3), DMA(N + 2, 3), DMA(2, 4), DMA(2, 3), DMA(2 * TILES, 3),
        ],
        compiler_params=pltpu.CompilerParams(collective_id=0, has_side_effects=True, vmem_limit_bytes=62 << 20),
    )(a1, a1_t, h, dy, a0_t, gate, up, wg, wu, wd)


def adamw(w, m, v, g):
    m = 0.9 * m + 0.1 * g
    v = 0.95 * v + 0.05 * g * g
    step = m * lax.rsqrt(v + 1e-8) + 0.1 * w
    return (w - 0.02 * step).astype(BF16), m, v


def solution(mesh):
    def step(x, dy, *arrays):
        weights, m, v = (arrays[i : i + 3] for i in (0, 3, 6))
        gate, up, a0_t, h, a1, a1_t = forward(x[0], *weights)
        gu, down, squares, *_ = gradient_sums(a1, a1_t, h, dy[0], a0_t, gate, up, *weights)
        gradients = [gu[0], gu[1], down]
        count = sum(g.size for g in gradients)
        factor = jnp.minimum(1.0, 0.5 * lax.rsqrt(jnp.sum(squares) / count + 1e-30))
        new = [adamw(w.astype(F32), m, v, g.astype(F32) * factor) for w, m, v, g in zip(weights, m, v, gradients, strict=True)]
        return tuple(one[which] for which in range(3) for one in new)

    whole = P(None, None, None)
    return jax.shard_map(
        step,
        mesh=mesh,
        in_specs=(P(("rep", "dp"), None, None),) * 2 + (whole,) * 9,
        out_specs=(P("rep", None, None),) * 9,
        check_vma=False,
    )
```

time: 725 us -> 387 us (0.53); the launches traced: 717 us -> 386 us
  waiting for transfers between devices: 415 us -> 0 us
  Pallas kernels: 0 us -> 278 us
  matrix products: 155 us -> 0 us
  other arithmetic: 126 us -> 107 us
  between operations: 16.8 us -> 1.35 us
    psum x1 -> x0, waiting for transfers between devices: 415 us -> none  [step(): summed[number] = [lax.psum(by_w[name], 'dp') for name in NAMES]]
    pallas_call x0 -> x2, Pallas kernels: none -> 278 us  [the longest x1 248 us: gradient_sums(): pl.pallas_call(functools.partial(sum_kernel, ru, cu), name='gradient_sums...]
    dot_general x15 -> x0, matrix products: 155 us -> none  [the longest x5 59 us: layer(): gate = jnp.dot(a, w['w_gate'], preferred_element_type=jnp.float32)]
    reduce_sum x4 -> x1, other arithmetic: 24.5 us -> 1.29 us  [step(): factor = jnp.minimum(1.0, 0.5 * lax.rsqrt(jnp.sum(squares) / count + 1e-30))]
  transfers between devices with their start and end apart: 1 -> 0, of which waited for: 1 -> 0; matrix products, arithmetic and copies ran while one was open for 0% -> 0% of each run, Pallas kernels for 0% -> 0%
where the time goes in v3:
time: 387 us; the launch traced here: 386 us
  Pallas kernels  278 us (72%)
  other arithmetic  107 us (28%)
    pallas_call x1, Pallas kernels, gradient_sums(): pl.pallas_call(functools.partial(sum_kernel, ru, cu), name='gradient_sums...  248 us
    convert_element_type x2, other arithmetic, adamw(): return ((w - 0.02 * step).astype(BF16), m, v)  105 us
    pallas_call x1, Pallas kernels, forward(): pl.pallas_call(functools.partial(forward_kernel, blocks), name='layer0_fo...  29.7 us

profile of v3, /device:TPU:1, one launch (start us, length us, event | category | flops | bytes accessed | tf_op | source)
XLA Modules:
  0.0 386.1 jit_solution(5339516921319483045)
XLA Ops:
  0.6 29.7 %layer0_forward.1 = (f32[12,1024,256]{2,1,0:T(8,128)}, f32[12,1024,256]{2,1,0:T(8,128)}, bf16[768,1024]{1,0:T(8,128)(2,1)}, bf16[1024,768]{1,0:T(8,128)(2,1)}, b...) custom-call(bf16[1024,768]{1,0:T(8,128)(2,1)} %bitcast.16, bf16[2,768,3072]{2,1,0:T(8,128)(2,1)} %refs_7_.1, ...), custom_call_target="tpu_custom_call" | custom-call | tf_op jit(solution)/shard_map/layer0_forward/pallas_call | solution.py:98
  30.4 248.3 %gradient_sums.1 = (bf16[2,2,768,3072]{3,2,1,0:T(8,128)(2,1)}, bf16[2,3072,768]{2,1,0:T(8,128)(2,1)}, f32[8,128]{1,0:T(8,128)}, bf16[12,1024,256]{2,1,0:T(8,128)(2,1)}, bf16[12,1024,256]{2,1,0:T(8,128)(2,1)}) custom-call(bf16[1024,768]{1,0:T(8,128)(2,1)} %get-tuple-element.18.refs_0_, bf16[768,1024]{1,0:T(8,128)(2,1)} %get-tuple-element.19.refs_1_, ...), custom_call_target="tpu_custom_call" | custom-call | tf_op jit(solution)/shard_map/gradient_sums/pallas_call | solution.py:672
  278.7 1.3 reduce_sum.9
  280.6 68.9 %fusion.5 = (bf16[2,768,3072]{2,1,0:T(8,128)(2,1)}, f32[2,768,3072]{2,1,0:T(8,128)}, f32[2,768,3072]{2,1,0:T(8,128)}, bf16[2,768,3072]{2,1,0:T(8,128)(2,1)}, f32...) fusion(bf16[2,768,3072]{2,1,0:T(8,128)(2,1)} %refs_8_.1, f32[]{:T(128)S(6)} %min_shard_map.3, ...), kind=kLoop, calls=%fused_computation.14 | loop fusion | flops 160432128 | bytes 207618048 | tf_op jit(solution)/shard_map/convert_element_type | solution.py:694
  349.5 36.6 %fusion.8 = (bf16[2,3072,768]{2,1,0:T(8,128)(2,1)}, f32[2,3072,768]{2,1,0:T(8,128)}, f32[2,3072,768]{2,1,0:T(8,128)}) fusion(bf16[2,3072,768]{2,1,0:T(8,128)(2,1)} %refs_9_.1, f32[]{:T(128)S(6)} %min_shard_map.3, bf16[2,3072,768]{2,1,0:T(8,128)(2,1)} %get-tuple-element.26, f32[2,3072,768]{2,1,0:T(8,128)} %param.21, f32[2,3072,768]{2,1,0:T(8,128)} %param.18), kind=kLoop, calls=%fused_computation.17 | loop fusion | flops 80216064 | bytes 103809024 | tf_op jit(solution)/shard_map/convert_element_type | solution.py:694

commit v4 on v3

--- a/solution.py
+++ b/solution.py
@@ -16,7 +16,7 @@
 ANY = pl.BlockSpec(memory_space=pl.ANY)
 VMEM = pl.BlockSpec(memory_space=pltpu.VMEM)
 SUBLANES, LANES = 16, 128
-TILES, PARTS = 12, 3
+TILES, PARTS = 12, 1
 BLOCK = (8, LANES)
 NUMBER_OF_XFERS = 680
 
@@ -51,66 +51,100 @@
     lax.fori_loop(0, a.shape[1] // LANES, slab, 0)
 
 
-def forward_kernel(blocks, x_ref, wg_ref, wu_ref, wd_ref, g_ref, u_ref, a0_t, h_ref, a1_ref, a1_t, a0_ref, total):
-    j = pl.program_id(0)
-    n = x_ref.shape[0]
-    b = n // blocks
-
-    @pl.when(j == 0)
-    def _():
-        def body(rows):
-            a0_ref[rows, :] = normed(x_ref[rows, :])
-            total[rows, :] = jnp.zeros_like(total[rows, :])
-
-        by_rows(n, 64, body)
-        turned(a0_ref, a0_t)
-
-    for k in range(blocks):
-        rows = pl.ds(k * b, b)
-        a = a0_ref[rows, :]
-        g = dot(a, wg_ref[0])
-        u = dot(a, wu_ref[0])
-        for to, by in ((g_ref, g), (u_ref, u)):
-            for t in range(to.shape[0]):
-                to[t, rows, :] = by[:, t * to.shape[2] : (t + 1) * to.shape[2]]
-        p = (g * jax.nn.sigmoid(g) * u).astype(BF16)
-        total[rows, :] += dot(p, wd_ref[0])
-
-    @pl.when(j == pl.num_programs(0) - 1)
-    def _():
-        def body(rows):
-            h = x_ref[rows, :] + total[rows, :].astype(BF16)
-            h_ref[rows, :] = h
-            a1_ref[rows, :] = normed(h)
-
-        by_rows(n, 64, body)
-        turned(a1_ref, a1_t)
-
-
-def blocks_of(shape, *index):
-    return pl.BlockSpec(shape, lambda j: tuple(j if i is None else i for i in index))
-
-
-def forward(x, wg, wu, wd, tile=512, blocks=4):
-    (n, d), ff = x.shape, wg.shape[-1]
-    whole, wide = blocks_of((n, d), 0, 0), blocks_of((tile * TILES // ff, n, ff // TILES), None, 0, 0)
-    turned_ = blocks_of((d, n), 0, 0)
-    return pl.pallas_call(
-        functools.partial(forward_kernel, blocks),
-        name="layer0_forward",
-        grid=(ff // tile,),
-        in_specs=[whole] + [blocks_of((1, d, tile), 0, 0, None)] * 2 + [blocks_of((1, tile, d), 0, None, 0)],
-        out_specs=[wide, wide, turned_, whole, whole, turned_],
-        out_shape=[jax.ShapeDtypeStruct((TILES, n, ff // TILES), F32)] * 2 + [jax.ShapeDtypeStruct(s, BF16) for s in ((d, n), (n, d), (n, d), (d, n))],
-        scratch_shapes=[pltpu.VMEM((n, d), BF16), pltpu.VMEM((n, d), F32)],
-        compiler_params=pltpu.CompilerParams(vmem_limit_bytes=60 << 20),
-    )(x, wg, wu, wd)
+def blocks_of(shape, index):
+    return pl.BlockSpec(shape, lambda j: index(j))
 
 
 def backward_tile(g, u, dp):
     sig = jax.nn.sigmoid(g)
     act = g * sig
     return (act * u).astype(BF16), (dp * u * (sig + act * (1.0 - sig))).astype(BF16), (dp * act).astype(BF16)
+
+
+def layers_kernel(tiles, x_ref, dy_ref, wg_ref, wu_ref, wd_ref, g_ref, u_ref, a0_t, dh_ref, dwg_ref, dwu_ref, dwd_ref, a_s, a_t, h_s, by_g, by_u, p_s, dg_s, du_s):
+    j = pl.program_id(0)
+    n, d = x_ref.shape
+    blocks = [pl.ds(k * (n // 4), n // 4) for k in range(4)]
+
+    def clear(rows):
+        by_g[rows, :] = jnp.zeros_like(by_g[rows, :])
+
+    @pl.when(j == 0)
+    def _():
+        def body(rows):
+            a_s[rows, :] = normed(x_ref[rows, :])
+            clear(rows)
+
+        by_rows(n, 64, body)
+        turned(a_s, a0_t)
+
+    @pl.when(j < tiles)
+    def _():
+        for rows in blocks:
+            a = a_s[rows, :]
+            g = dot(a, wg_ref[0])
+            u = dot(a, wu_ref[0])
+            for to, by in ((g_ref, g), (u_ref, u)):
+                for t in range(to.shape[0]):
+                    to[t, rows, :] = by[:, t * to.shape[2] : (t + 1) * to.shape[2]]
+            by_g[rows, :] += dot((g * jax.nn.sigmoid(g) * u).astype(BF16), wd_ref[0])
+
+    @pl.when(j == tiles - 1)
+    def _():
+        def body(rows):
+            h = x_ref[rows, :] + by_g[rows, :].astype(BF16)
+            h_s[rows, :] = h
+            a_s[rows, :] = normed(h)
+            clear(rows)
+            by_u[rows, :] = jnp.zeros_like(by_u[rows, :])
+
+        by_rows(n, 64, body)
+        turned(a_s, a_t)
+
+    @pl.when(j >= tiles)
+    def _():
+        for rows in blocks:
+            a = a_s[rows, :]
+            dp = dot(dy_ref[rows, :], wd_ref[0], NT).astype(BF16).astype(F32)
+            p_s[rows, :], dg, du = backward_tile(dot(a, wg_ref[0]), dot(a, wu_ref[0]), dp)
+            dg_s[rows, :], du_s[rows, :] = dg, du
+            by_g[rows, :] += dot(dg, wg_ref[0], NT)
+            by_u[rows, :] += dot(du, wu_ref[0], NT)
+        dwg_ref[...] = dot(a_t[...], dg_s[...]).astype(BF16)
+        dwu_ref[...] = dot(a_t[...], du_s[...]).astype(BF16)
+        dwd_ref[...] = dot(p_s[...], dy_ref[...], TN).astype(BF16)
+
+    @pl.when(j == pl.num_programs(0) - 1)
+    def _():
+        def body(rows):
+            by_a = (by_g[rows, :].astype(BF16) + by_u[rows, :].astype(BF16)).astype(F32)
+            wide = h_s[rows, :].astype(F32)
+            s = scale_of(wide)
+            by_h = by_a * s - wide * (s * s * s * jnp.mean(by_a * wide, -1, keepdims=True))
+            dh_ref[rows, :] = dy_ref[rows, :] + by_h.astype(BF16)
+
+        by_rows(n, 32, body)
+
+
+def layers(x, dy, wg, wu, wd, tile=512):
+    (n, d), ff = x.shape, wg.shape[-1]
+    tiles, per = ff // tile, tile * TILES // ff
+    early, late = lambda j: jnp.minimum(j, tiles - 1), lambda j: jnp.maximum(j - tiles, 0)
+    whole, turned_ = blocks_of((n, d), lambda j: (0, 0)), blocks_of((d, n), lambda j: (0, 0))
+    wide = blocks_of((per, n, ff // TILES), lambda j: (early(j), 0, 0))
+    weight = blocks_of((1, d, tile), lambda j: (j // tiles, 0, j % tiles))
+    across = blocks_of((d, tile), lambda j: (0, late(j)))
+    V = lambda *s: pltpu.VMEM(s, BF16)
+    return pl.pallas_call(
+        functools.partial(layers_kernel, tiles),
+        name="layers",
+        grid=(2 * tiles,),
+        in_specs=[whole, whole, weight, weight, blocks_of((1, tile, d), lambda j: (j // tiles, j % tiles, 0))],
+        out_specs=[wide, wide, turned_, whole, across, across, blocks_of((tile, d), lambda j: (late(j), 0))],
+        out_shape=[jax.ShapeDtypeStruct((TILES, n, ff // TILES), F32)] * 2 + [jax.ShapeDtypeStruct(s, BF16) for s in ((d, n), (n, d), (d, ff), (d, ff), (ff, d))],
+        scratch_shapes=[V(n, d), V(d, n), V(n, d), pltpu.VMEM((n, d), F32), pltpu.VMEM((n, d), F32), V(n, tile), V(n, tile), V(n, tile)],
+        compiler_params=pltpu.CompilerParams(vmem_limit_bytes=62 << 20),
+    )(x, dy, wg, wu, wd)
 
 
 def div(a, b):
@@ -168,14 +202,15 @@
 
 
 class Event:
-    def __init__(self, waits, pre, work, cost, sends):
-        self.waits, self.pre, self.work, self.cost, self.sends = waits, pre, work, cost, sends
+    def __init__(self, waits, pre, work, cost, sends, late):
+        self.waits, self.pre, self.work, self.cost, self.sends, self.late = waits, pre, work, cost, sends, late
         self.done = None
 
 
-RATE, CHIP_RATE, DELAY, SLACK = 45.0e3, 450.0e3, 2.2, 0.6
-STEPS = ((0.8, 0.8, 0.55, 0.55, 0.55), (0.55, 0.55), (0.45, 0.45, 0.5, 0.5, 0.5))
-SLOTS = [part for phase in STEPS for part in phase * TILES]
+RATE, CHIP_RATE, DELAY, GAP, SLACK = 46.0e3, 450.0e3, 2.3, 0.1, 0.5
+LATE = {("share", 0): -2, ("share", 1): 2, ("across", 0): 1, ("across", 1): 2, ("halve", 0): 1, ("round", 0): -2}
+STEP = (0.6, 0.6, 0.65, 0.65, 0.65)
+SLOTS = STEP * TILES
 
 
 def order_of(events, slots):
@@ -186,19 +221,19 @@
             if any(done < p if isinstance(p, int) else p.done is None for p in e.pre) or any(t.arrives is None for t in e.waits):
                 continue
             ready = max([p.done for p in e.pre if not isinstance(p, int)] + [t.arrives + (SLACK if done < len(slots) else 0.0) for t in e.waits] + [0.0])
-            if best is None or max(ready, clock) < best[0]:
+            if best is None or max(ready, clock) + e.late < best[0] + best[1].late:
                 best = (max(ready, clock), e)
-        if done < len(slots) and (best is None or best[0] > clock):
+        if done < len(slots) and (best is None or best[0] + best[1].late > clock):
             clock += slots[done]
             done += 1
             groups.append([])
             continue
         clock, e = best
-        clock += e.cost + 0.02 * (len(e.waits) + len(e.sends))
+        clock += e.cost
         e.done = clock
         for t in e.sends:
             begin = max(clock, links.get(t.link, 0.0))
-            links[t.link] = begin + t.size / (CHIP_RATE if t.link == "chip" else RATE)
+            links[t.link] = begin + GAP + t.size / (CHIP_RATE if t.link == "chip" else RATE)
             t.arrives = links[t.link] + DELAY
         left.remove(e)
         groups[-1].append(e)
@@ -207,7 +242,7 @@
 
 def plan(here, refs, ru, cu):
     x, y, z, core = here
-    (own_ab, own_c, p_ab, p_c, r1, r2, r3, r4, rz, rc, rx, ry, f_ab, f_c, acc, norms, gu_out, dn_out, sq_out, total, squares, need, local) = refs
+    (grads, own_ab, own_c, p_ab, p_c, r1, r2, r3, r4, rz, rc, rx, ry, f_ab, f_c, acc, norms, gu_out, dn_out, sq_out, total, squares, need, local) = refs
     other = 1 - core
     xfers, events = [], []
     part_of = functools.partial
@@ -242,13 +277,15 @@
             ts.append(xfer(axis + "+-"[back], size, src(d, to), dst(d, to), n - d if back else d, **{axis: to}))
         return ts
 
-    def event(waits, pre, work=lambda: None, cost=0.03, sends=()):
-        e = Event(waits, pre, work, cost, sends)
+    def event(waits, pre, work=lambda: None, cost=0.05, sends=()):
+        e = Event(waits, pre, work, cost, sends, LATE.get(kind, 0))
         events.append(e)
         return e
 
+    kind = None
+
     def adds(size, n):
-        return size * n / 1.6e6 + 0.1
+        return size * n / 2.0e6 + 0.15
 
     D, FF = SUBLANES * ru, NZ * cu
     HD, S = D // 2, D // 4
@@ -260,7 +297,18 @@
 
     for i in range(2 * PARTS):
         l, f0 = 1 - i // PARTS, i % PARTS * FF
-        begin = event([], [(TILES // PARTS) * (i % PARTS + 1) * len(STEPS[0]) + (0 if l else len(SLOTS) - TILES * len(STEPS[0]))], part_of(need, i), 0.3)
+        kind = "halve", l
+        begins = {}
+        if l:
+            for s in range(2):
+                for c in range(2):
+                    begins[c, s] = xfer("chip", S * FF, window(grads[c], (), other * HD + s * S, S, f0, FF), window(p_ab, (i, c), s * S, S, 0, FF), core=other)
+                begins[2, s] = xfer("chip", HC * HD, window(grads[2], (), f0 + s * HC, HC, other * HD, HD), window(p_c, (i,), s * HC, HC, 0, HD), core=other)
+            e = event([], [], sends=list(begins.values()))
+            begins = {k: event([t], [e], part_of(need, (i, *k))) for k, t in begins.items()}
+        else:
+            e = event([], [len(SLOTS) * (i % PARTS + 1) // PARTS], part_of(need, (i, 0, 0)), 0.3)
+            begins = {(c, s): e for c in range(3) for s in range(2)}
 
         ends = []
         for c in range(2):
@@ -281,7 +329,7 @@
                     more = [(r1, k2, (b2 if n > 1 else 1 - b2) * ru, col), (r2, k2, 0, col), (r3, k2, 0, col - c1 * HC), (r4, k2, 0, 0)]
                     total((p_ab, *to), [(p_ab, *to), (own_ab, *to)] + more[:n], rows, cols)
 
-                e, prev = begin, []
+                e, prev = begins[c, s], []
                 for n, (t, row, col, rows, cols) in enumerate(((t1, away, 0, 2 * ru, FF), (t2, out, 0, ru, FF), (t3, q, col1, ru, HC), (t4, q, col2, ru, QC), (None, q, mine, ru, QC))):
                     e = event(prev, [e], part_of(work, row, col, rows, cols, n), adds(rows * cols, n + 2), [t] if t else [])
                     prev = [t]
@@ -298,6 +346,7 @@
             c, a, b = piece(to)
             return window(p_ab, (i, c), a, ru, b, cu)
 
+        kind = "share", l
         tz = to_all("z", NZ, ru * cu, from_piece, lambda d, to, i=i: block(rz, i, d - 1))
         e = event([], ends, sends=tz)
         mc, ma, mb = piece(z)
@@ -316,6 +365,8 @@
             ri, ci, rax, cax = (y, x, "y", "x") if c else (x, y, "x", "y")
             for s in range(2):
                 e1, e2 = "+-"[s], "-+"[s]
+
+                kind = "spread", l
 
                 def same(link, row, rows, col, cols, l=l, c=c, f0=f0, s=s, **to):
                     ref = window(gu_out, (c, l), core * HD + s * S + row * ru, rows * ru, f0 + col, cols)
@@ -332,7 +383,7 @@
                 arrived += fw
 
         for s in range(2):
-            key, base = (i, s), s * HC
+            key, base, kind = (i, s), s * HC, ("down", l)
             arms = ((1, "z+", 0, 4 - s), (-1, "z-", 4 - s, 3 + s))
             chunk = lambda k, base=base: base + around[k % NZ]
 
@@ -342,7 +393,7 @@
 
             ends, lasts = [], []
             for sg, zl, slot, n in arms:
-                nxt, e, prev = others["z"][-(sg < 0)], begin, []
+                nxt, e, prev = others["z"][-(sg < 0)], begins[2, s], []
                 for t in range(n):
                     row, into = chunk(sg * (n - t)), (rc, (*key, slot + t - 1), 0, 0) if t else None
                     ring = xfer(zl, CR * HD, block(rc, *key, slot + t - 1) if t else window(p_c, (i,), row, CR, 0, HD), block(rc, *key, slot + t), z=nxt)
@@ -356,7 +407,7 @@
             def work_x(key=key):
                 total((ry, (*key, y), 0, 0), [(rc, (*key, 3 - key[1]), x * XR, 0)] + [(rx, (*key, d), 0, 0) for d in range(NX - 1)], XR, HD)
 
-            mine = block(ry, *key, y)
+            mine, kind = block(ry, *key, y), ("across", l)
             ty = to_all("y", NY, XR * HD, lambda d, to, m=mine: m, lambda d, to, m=mine: m)
             e = event(tx, [e], work_x, adds(XR * HD, 4), ty)
             home, mine = window(dn_out, (l,), f0 + base + z * CR + x * XR, XR, core * HD, HD), block(f_c, *key)
@@ -369,8 +420,9 @@
             hx = to_all("x", NX, XR * HD, lambda d, to, m=mine: m, lambda d, to, h=home: h)
             e = event(ty, [e], work_y, 0.3, hx)
             pieces.append(e)
-            e = event(hx, [e], lambda key=key, mine=mine, home=home: local(key[0], 1 + key[1], mine, home).wait(), 0.1)
+            e = event(hx, [e, spread], lambda key=key, mine=mine, home=home: local(key[0], 1 + key[1], mine, home).wait(), 0.1)
             prev, ends = [[], []], [e, e]
+            kind = "round", l
             for t in range(4):
                 for k, (sg, zl, slot, n) in enumerate(arms):
                     if t < n:
@@ -382,6 +434,7 @@
             arrived.append(xfer("chip", HC * HD, ref, ref, core=other))
             event(prev[0] + prev[1], ends, sends=arrived[-1:])
 
+    kind = None
     e, ts, prev = None, [], None
     for axis, k, n, ref in (("z", z, NZ, norms[0]), ("y", y, NY, norms[1]), ("x", x, NX, norms[2]), ("core", core, CORES, norms[3])):
         def work(ref=ref, k=k, prev=prev):
@@ -403,18 +456,24 @@
 
 
 def sum_kernel(ru, cu, *refs):
-    (a1, a1_t, h, dy, a0_t, gate, up, wg, wu, wd, gu_out, dn_out, sq_out, dg, du, own_ab, own_c, p_ab, p_c, r1, r2, r3, r4, rz, rc, rx, ry, f_ab, f_c,
-     acc, nz, ny, nx, nc, dh, send_sem, recv_sem, load_sem, keep_sem, tile_sem, out_sem, in_sem) = refs
+    (g1, u1, d1, a0_t, dh, gate, up, wd, gu_out, dn_out, sq_out, own_ab, own_c, p_ab, p_c, r1, r2, r3, r4, rz, rc, rx, ry, f_ab, f_c,
+     acc, nz, ny, nx, nc, gbuf, ubuf, wbuf, p_s, dg_s, du_s, st_ab, st_c, send_sem, recv_sem, load_sem, keep_sem, tile_sem, out_sem, in_sem) = refs
     me = lax.axis_index("dp")
     core, z, y, x = rem(me, CORES), rem(div(me, CORES), NZ), rem(div(me, CORES * NZ), NY), div(me, CORES * NZ * NY)
     other = 1 - core
     D = SUBLANES * ru
     HD = D // 2
-    n = h.shape[0]
+    n = dh.shape[0]
     per = TILES // PARTS
     tile = NZ * cu // per
     partner = me + 1 - 2 * core
     slice_of = lambda j: pl.ds(pl.multiple_of(j * tile, LANES), tile)
+
+    mine, yours = (pl.ds(pl.multiple_of(c * HD, LANES), HD) for c in (core, other))
+    loads = [pltpu.make_async_copy(src, dst, load_sem.at[k]) for k, (src, dst) in enumerate(((g1.at[mine, :], own_ab.at[0, 0]), (u1.at[mine, :], own_ab.at[0, 1]),
+                                                                                             (d1.at[:, mine], own_c.at[0])))]
+    for t in loads:
+        t.start()
 
     barrier = pltpu.get_barrier_semaphore()
     dev = lambda x, y, z, core: ((x * NY + y) * NZ + z) * CORES + core
@@ -425,7 +484,7 @@
     pl.semaphore_wait(barrier, len(peers))
 
     def tile_sends(j, srcs=None, slot=0):
-        i, cols = div(j, per), slice_of(rem(j, per))
+        i, cols = PARTS + div(j, per), slice_of(rem(j, per))
         dsts = [p_ab.at[i, c, :, cols] for c in range(2)] + [p_c.at[i, cols, :]]
         return [pltpu.make_async_remote_copy(src_ref=src, dst_ref=dst, send_sem=out_sem.at[slot, k], recv_sem=in_sem.at[j, k], device_id=partner,
                                              device_id_type=LOGICAL) for k, (src, dst) in enumerate(zip(srcs or dsts, dsts, strict=True))]
@@ -468,19 +527,25 @@
                     s = s + weight * v[a : a + BLOCK[0], b : b + LANES]
             acc[...] = s
 
-    def need(i):
+    def need(key):
+        i, c, s = key
+        if i < PARTS:
+            if s == 0:
+                loads[c].wait()
+            return
+
         def wait(j, _):
             for t in tile_sends(j):
                 t.wait_recv()
             return _
 
-        lax.fori_loop(i * per, (i + 1) * per, wait, 0)
+        lax.fori_loop((i - PARTS) * per, (i - PARTS + 1) * per, wait, 0)
 
     def local(l, k, src, dst):
         return pltpu.make_async_copy(src(), dst(), keep_sem.at[l, k])
 
     acc[...] = jnp.zeros_like(acc)
-    xfers, events = plan((x, y, z, core), (own_ab, own_c, p_ab, p_c, r1, r2, r3, r4, rz, rc, rx, ry, f_ab, f_c, acc, (nz, ny, nx, nc),
+    xfers, events = plan((x, y, z, core), ((g1, u1, d1), own_ab, own_c, p_ab, p_c, r1, r2, r3, r4, rz, rc, rx, ry, f_ab, f_c, acc, (nz, ny, nx, nc),
                                            gu_out, dn_out, sq_out, total, squares, need, local), ru, cu)
     counts = sorted(t.count for t in xfers)
     ids = {id(t): k for k, t in enumerate(sorted(xfers, key=lambda t: t.count))}
@@ -541,118 +606,37 @@
     tail = groups.pop()
     groups.append([])
 
-    def fetch(*pairs):
-        copies = [pltpu.make_async_copy(src, dst, load_sem.at[k]) for k, (src, dst) in enumerate(pairs)]
-        for t in copies:
-            t.start()
-        return lambda: [t.wait() for t in copies]
-
-    mine, yours = (pl.ds(pl.multiple_of(c * HD, LANES), HD) for c in (core, other))
-    rows_out = pl.ds(pl.multiple_of(other * HD, SUBLANES), HD)
-    staged = lambda st_ab, st_c, slot: [st_ab.at[slot, 0, rows_out, :], st_ab.at[slot, 1, rows_out, :], st_c.at[slot, :, yours]]
-
-    def sent(j, slot, st):
-        for t in tile_sends(j, staged(*st, slot), slot):
+    rows_in, rows_out = (pl.ds(pl.multiple_of(c * HD, SUBLANES), HD) for c in (core, other))
+    staged = lambda slot: [st_ab.at[slot, 0, rows_out, :], st_ab.at[slot, 1, rows_out, :], st_c.at[slot, :, yours]]
+    blocks = [pl.ds(k * (n // 4), n // 4) for k in range(4)]
+
+    def through(which, j, slot):
+        if which == 0:
+            @pl.when(j > 1)
+            def _():
+                for t in tile_sends(j - 2, staged(slot), slot):
+                    t.wait_send()
+
+        for rows in blocks[which::2]:
+            dp = dot(dh[rows, :], wbuf[slot], NT).astype(BF16).astype(F32)
+            p_s[rows, :], dg_s[rows, :], du_s[rows, :] = backward_tile(gbuf[slot, rows, :], ubuf[slot, rows, :], dp)
+
+    def term(c, j, slot):
+        i, cols = PARTS + div(j, per), slice_of(rem(j, per))
+        if c < 2:
+            st_ab[slot, c] = dot(a0_t[...], (dg_s, du_s)[c][...]).astype(BF16)
+            own_ab[i, c, :, cols] = st_ab[slot, c, rows_in, :]
+        else:
+            st_c[slot] = dot(p_s[...], dh[...], TN).astype(BF16)
+            own_c[i, cols, :] = st_c[slot, :, mine]
+            for t in tile_sends(j, staged(slot), slot):
+                t.start()
+
+    steps([lambda j: gate.at[j], lambda j: up.at[j], lambda j: wd.at[0, slice_of(j), :]], [gbuf, ubuf, wbuf],
+          *[functools.partial(f, k) for f, k in ((through, 0), (through, 1), (term, 0), (term, 1), (term, 2))])
+    for k in range(2):
+        for t in tile_sends(TILES - 2 + k, staged(k), k):
             t.wait_send()
-
-    def term(j, slot, c, a, b, st):
-        i, cols = div(j, per), slice_of(rem(j, per))
-        st_ab, st_c = st
-        if c < 2:
-            st_ab[slot, c] = dot(a[...], b[...]).astype(BF16)
-            own_ab[i, c, :, cols] = st_ab[slot, c, pl.ds(pl.multiple_of(core * HD, SUBLANES), HD), :]
-        else:
-            st_c[slot] = dot(a[...], b[...], TN).astype(BF16)
-            own_c[i, cols, :] = st_c[slot, :, mine]
-            for t in tile_sends(j, staged(st_ab, st_c, slot), slot):
-                t.start()
-
-    blocks = [pl.ds(k * (n // 4), n // 4) for k in range(4)]
-
-    def layer_1(wgbuf, wubuf, wdbuf, a_s, a_t, dy_s, p_s, dgbuf, dubuf, *st):
-        fetch((a1, a_s), (dy, dy_s), (a1_t, a_t))()
-
-        def outs(j, slot):
-            return [pltpu.make_async_copy(buf.at[slot], to.at[j], keep_sem.at[2 * PARTS + slot, k]) for k, (buf, to) in enumerate(((dgbuf, dg), (dubuf, du)))]
-
-        def through(which, j, slot):
-            if which == 0:
-                @pl.when(j > 1)
-                def _():
-                    sent(j - 2, slot, st)
-                    for t in outs(j - 2, slot):
-                        t.wait()
-
-            for rows in blocks[which::2]:
-                a = a_s[rows, :]
-                dp = dot(dy_s[rows, :], wdbuf[slot], NT).astype(BF16).astype(F32)
-                p_s[rows, :], dgbuf[slot, rows, :], dubuf[slot, rows, :] = backward_tile(dot(a, wgbuf[slot]), dot(a, wubuf[slot]), dp)
-
-        def down(j, slot):
-            term(j, slot, 2, p_s, dy_s, st)
-            for t in outs(j, slot):
-                t.start()
-
-        steps([lambda j: wg.at[1, :, slice_of(j)], lambda j: wu.at[1, :, slice_of(j)], lambda j: wd.at[1, slice_of(j), :]], [wgbuf, wubuf, wdbuf], functools.partial(through, 0),
-              functools.partial(through, 1), lambda j, slot: term(j, slot, 0, a_t, dgbuf.at[slot], st), lambda j, slot: term(j, slot, 1, a_t, dubuf.at[slot], st), down)
-        for k in range(2):
-            sent(TILES - 2 + k, k, st)
-            for t in outs(TILES - 2 + k, k):
-                t.wait()
-
-    V = lambda *s: pltpu.VMEM(s, BF16)
-    W = lambda *s: pltpu.VMEM(s, F32)
-    stages = V(2, 2, D, tile), V(2, tile, D)
-    pl.run_scoped(layer_1, V(2, D, tile), V(2, D, tile), V(2, tile, D), V(n, D), V(D, n), V(n, D), V(n, tile), V(2, n, tile), V(2, n, tile), *stages)
-
-    def by_input(gbuf, ubuf, wgbuf, wubuf, by_g, by_u, h_s, dy_s):
-        arrived = fetch((h, h_s), (dy, dy_s))
-
-        def clear(rows):
-            by_g[rows, :] = jnp.zeros_like(by_g[rows, :])
-            by_u[rows, :] = jnp.zeros_like(by_u[rows, :])
-
-        by_rows(n, 64, clear)
-
-        def part(which, j, slot):
-            for rows in blocks[which::2]:
-                by_g[rows, :] += dot(gbuf[slot, rows, :], wgbuf[slot], NT)
-                by_u[rows, :] += dot(ubuf[slot, rows, :], wubuf[slot], NT)
-
-        steps([lambda j: dg.at[j], lambda j: du.at[j], lambda j: wg.at[1, :, slice_of(j)], lambda j: wu.at[1, :, slice_of(j)]], [gbuf, ubuf, wgbuf, wubuf],
-              functools.partial(part, 0), functools.partial(part, 1))
-        arrived()
-
-        def back(rows):
-            by_a = (by_g[rows, :].astype(BF16) + by_u[rows, :].astype(BF16)).astype(F32)
-            wide = h_s[rows, :].astype(F32)
-            s = scale_of(wide)
-            by_h = by_a * s - wide * (s * s * s * jnp.mean(by_a * wide, -1, keepdims=True))
-            dh[rows, :] = dy_s[rows, :] + by_h.astype(BF16)
-
-        by_rows(n, 32, back)
-
-    pl.run_scoped(by_input, V(2, n, tile), V(2, n, tile), V(2, D, tile), V(2, D, tile), W(n, D), W(n, D), V(n, D), V(n, D))
-
-    def layer_0(gbuf, ubuf, wbuf, a_t, p_s, dg_s, du_s, *st):
-        fetch((a0_t, a_t))()
-
-        def through(which, j, slot):
-            if which == 0:
-                @pl.when(j > 1)
-                def _():
-                    sent(TILES + j - 2, slot, st)
-
-            for rows in blocks[which::2]:
-                dp = dot(dh[rows, :], wbuf[slot], NT).astype(BF16).astype(F32)
-                p_s[rows, :], dg_s[rows, :], du_s[rows, :] = backward_tile(gbuf[slot, rows, :], ubuf[slot, rows, :], dp)
-
-        steps([lambda j: gate.at[j], lambda j: up.at[j], lambda j: wd.at[0, slice_of(j), :]], [gbuf, ubuf, wbuf], functools.partial(through, 0),
-              functools.partial(through, 1), *[lambda j, slot, k=k: term(TILES + j, slot, *k, st) for k in ((0, a_t, dg_s), (1, a_t, du_s), (2, p_s, dh))])
-        for k in range(2):
-            sent(2 * TILES - 2 + k, k, st)
-
-    pl.run_scoped(layer_0, W(2, n, tile), W(2, n, tile), V(2, tile, D), V(D, n), V(n, tile), V(n, tile), V(n, tile), *stages)
     emit(tail)
     for count in sorted(set(counts)):
         def wait(k, carry, count=count):
@@ -662,29 +646,29 @@
         lax.fori_loop(counts.index(count), counts.index(count) + counts.count(count), wait, 0)
 
 
-def gradient_sums(a1, a1_t, h, dy, a0_t, gate, up, wg, wu, wd):
-    (n, d), ff = h.shape, wg.shape[-1]
+def gradient_sums(g1, u1, d1, a0_t, dh, gate, up, wd):
+    (n, d), ff = dh.shape, g1.shape[1]
     ru, cu = d // SUBLANES, ff // NZ // PARTS
-    HD, CR, fs, N = d // 2, cu // 2, ff // PARTS, 2 * PARTS
+    HD, CR, fs, N, tile = d // 2, cu // 2, ff // PARTS, 2 * PARTS, ff // TILES
     V = lambda *s: pltpu.VMEM(s, BF16)
     W = lambda *s: pltpu.VMEM(s, F32)
     DMA = lambda *s: pltpu.SemaphoreType.DMA(s)
     return pl.pallas_call(
         functools.partial(sum_kernel, ru, cu),
         name="gradient_sums",
-        out_shape=(jax.ShapeDtypeStruct((2, 2, d, ff), BF16), jax.ShapeDtypeStruct((2, ff, d), BF16), jax.ShapeDtypeStruct(BLOCK, F32)) + (jax.ShapeDtypeStruct((TILES, n, ff // TILES), BF16),) * 2,
-        in_specs=[ANY] * 10,
-        out_specs=(ANY, ANY, VMEM, ANY, ANY),
+        out_shape=(jax.ShapeDtypeStruct((2, 2, d, ff), BF16), jax.ShapeDtypeStruct((2, ff, d), BF16), jax.ShapeDtypeStruct(BLOCK, F32)),
+        in_specs=[ANY] * 3 + [VMEM] * 2 + [ANY] * 3,
+        out_specs=(ANY, ANY, VMEM),
         scratch_shapes=[
             V(N, 2, HD, fs), V(N, fs, HD), V(N, 2, HD, fs), V(N, fs, HD),
             V(N, 2, 2, 2 * ru, fs), V(N, 2, 2, ru, fs), V(N, 2, 2, ru, fs // 2), V(N, 2, 2, ru, fs // 4),
             V(N, NZ - 1, ru, cu), V(N, 2, NZ - 1, CR, HD), V(N, 2, NX - 1, CR // 4, HD), V(N, 2, NY, CR // 4, HD), V(N, ru, cu), V(N, 2, CR // 4, HD),
             W(*BLOCK), W(NZ, *BLOCK), W(NY, *BLOCK), W(NX, *BLOCK), W(CORES, *BLOCK),
-            V(n, d),
-            DMA(NUMBER_OF_XFERS), DMA(NUMBER_OF_XFERS), DMA(3), DMA(N + 2, 3), DMA(2, 4), DMA(2, 3), DMA(2 * TILES, 3),
+            W(2, n, tile), W(2, n, tile), V(2, tile, d), V(n, tile), V(n, tile), V(n, tile), V(2, 2, d, tile), V(2, tile, d),
+            DMA(NUMBER_OF_XFERS), DMA(NUMBER_OF_XFERS), DMA(3), DMA(N, 3), DMA(2, 3), DMA(2, 3), DMA(TILES, 3),
         ],
         compiler_params=pltpu.CompilerParams(collective_id=0, has_side_effects=True, vmem_limit_bytes=62 << 20),
-    )(a1, a1_t, h, dy, a0_t, gate, up, wg, wu, wd)
+    )(g1, u1, d1, a0_t, dh, gate, up, wd)
 
 
 def adamw(w, m, v, g):
@@ -694,16 +678,45 @@
     return (w - 0.02 * step).astype(BF16), m, v
 
 
+def optimizer_kernel(count, sq, *refs):
+    factor = jnp.minimum(1.0, 0.5 * lax.rsqrt(jnp.sum(sq[...], keepdims=True) / count + 1e-30))
+    ws, ms, vs, gs, *outs = (refs[i : i + 3] for i in range(0, len(refs), 3))
+    for k in range(3):
+        wide = ws[k].shape[-1]
+
+        def rows_of(i, _, k=k, wide=wide):
+            at = 0, pl.ds(pl.multiple_of(i * SUBLANES, SUBLANES), SUBLANES), slice(None)
+            g = gs[k][(0,) * (len(gs[k].shape) - 3) + at].astype(F32) * factor
+            for out, new in zip(outs, adamw(ws[k][at].astype(F32), ms[k][at], vs[k][at], g), strict=True):
+                out[k][at] = new
+            return _
+
+        lax.fori_loop(0, ws[k].shape[1] // SUBLANES, rows_of, 0)
+
+
+def optimizer(sq, weights, m, v, gu, down, blocks=24):
+    def spec(a, lead=()):
+        l, rows, cols = a.shape[-3:]
+        return pl.BlockSpec((1,) * len(lead) + (1, rows // blocks, cols), lambda j: (*lead, j // blocks, j % blocks, 0))
+
+    plain = [spec(w) for w in weights]
+    return pl.pallas_call(
+        functools.partial(optimizer_kernel, sum(w.size for w in weights)),
+        name="optimizer",
+        grid=(2 * blocks,),
+        in_specs=[pl.BlockSpec(sq.shape, lambda j: (0, 0))] + plain * 3 + [spec(gu, (0,)), spec(gu, (1,)), spec(down)],
+        out_specs=plain * 3,
+        out_shape=[jax.ShapeDtypeStruct(w.shape, t) for t in (BF16, F32, F32) for w in weights],
+        compiler_params=pltpu.CompilerParams(vmem_limit_bytes=60 << 20),
+    )(sq, *weights, *m, *v, gu, gu, down)
+
+
 def solution(mesh):
     def step(x, dy, *arrays):
         weights, m, v = (arrays[i : i + 3] for i in (0, 3, 6))
-        gate, up, a0_t, h, a1, a1_t = forward(x[0], *weights)
-        gu, down, squares, *_ = gradient_sums(a1, a1_t, h, dy[0], a0_t, gate, up, *weights)
-        gradients = [gu[0], gu[1], down]
-        count = sum(g.size for g in gradients)
-        factor = jnp.minimum(1.0, 0.5 * lax.rsqrt(jnp.sum(squares) / count + 1e-30))
-        new = [adamw(w.astype(F32), m, v, g.astype(F32) * factor) for w, m, v, g in zip(weights, m, v, gradients, strict=True)]
-        return tuple(one[which] for which in range(3) for one in new)
+        gate, up, a0_t, dh, *by_1 = layers(x[0], dy[0], *weights)
+        gu, down, squares = gradient_sums(*by_1, a0_t, dh, gate, up, weights[2])
+        return tuple(optimizer(squares, weights, m, v, gu, down))
 
     whole = P(None, None, None)
     return jax.shard_map(

time: 387 us -> 394 us (1.018)
  Pallas kernels: 278 us -> 392 us
  other arithmetic: 107 us -> 0 us
    pallas_call x1 -> x2, Pallas kernels: 29.7 us -> 199 us  [the longest x1 121 us: optimizer(): pl.pallas_call(functools.partial(optimizer_kernel, sum((w.size for w in w...]
    convert_element_type x2 -> x0, other arithmetic: 105 us -> none  [adamw(): return ((w - 0.02 * step).astype(BF16), m, v)]
    pallas_call x1, Pallas kernels: 248 us -> 193 us  [gradient_sums(): pl.pallas_call(functools.partial(sum_kernel, ru, cu), name='gradient_sums...]
where the time goes in v4:
time: 394 us; the launch traced here: 393 us
  Pallas kernels  392 us (99%)
    pallas_call x1, Pallas kernels, gradient_sums(): pl.pallas_call(functools.partial(sum_kernel, ru, cu), name='gradient_sums...  193 us
    pallas_call x1, Pallas kernels, optimizer(): pl.pallas_call(functools.partial(optimizer_kernel, sum((w.size for w in w...  121 us
    pallas_call x1, Pallas kernels, layers(): pl.pallas_call(functools.partial(layers_kernel, tiles), name='layers', gr...  78.1 us

profile of v4, /device:TPU:1, one launch (start us, length us, event | category | flops | bytes accessed | tf_op | source)
XLA Modules:
  0.0 393.2 jit_solution(2981984874246358897)
XLA Ops:
  0.6 78.1 %layers.1 = (f32[12,1024,256]{2,1,0:T(8,128)}, f32[12,1024,256]{2,1,0:T(8,128)}, bf16[768,1024]{1,0:T(8,128)(2,1)}, bf16[1024,768]{1,0:T(8,128)(2,1)}, bf16[768,...) custom-call(bf16[1024,768]{1,0:T(8,128)(2,1)} %bitcast.2, bf16[1024,768]{1,0:T(8,128)(2,1)} %bitcast.3, ...), custom_call_target="tpu_custom_call" | custom-call | tf_op jit(solution)/shard_map/layers/pallas_call | solution.py:138
  78.8 193.1 %gradient_sums.1 = (bf16[2,2,768,3072]{3,2,1,0:T(8,128)(2,1)}, bf16[2,3072,768]{2,1,0:T(8,128)(2,1)}, f32[8,128]{1,0:T(8,128)}) custom-call(bf16[768,3072]{1,0:T(8,128)(2,1)} %get-tuple-element.19.refs_0_, bf16[768,3072]{1,0:T(8,128)(2,1)} %get-tuple-element.20.refs_1_, bf16[3072,768]{1,0:T(8,128)(2,1)} %get-tuple-element.21.refs_2_, ...), custom_call_target="tpu_custom_call" | custom-call | tf_op jit(solution)/shard_map/gradient_sums/pallas_call | solution.py:656
  271.9 121.2 %optimizer.1 = (bf16[2,768,3072]{2,1,0:T(8,128)(2,1)}, bf16[2,768,3072]{2,1,0:T(8,128)(2,1)}, bf16[2,3072,768]{2,1,0:T(8,128)(2,1)}, f32[2,768,3072]{2,1,0:T(8,1...) custom-call(f32[8,128]{1,0:T(8,128)} %get-tuple-element.26.sq, ...), custom_call_target="tpu_custom_call" | custom-call | tf_op jit(solution)/shard_map/optimizer/pallas_call | solution.py:703

commit v5 on v4

--- a/solution.py
+++ b/solution.py
@@ -16,7 +16,7 @@
 ANY = pl.BlockSpec(memory_space=pl.ANY)
 VMEM = pl.BlockSpec(memory_space=pltpu.VMEM)
 SUBLANES, LANES = 16, 128
-TILES, PARTS = 12, 1
+TILES, PARTS = 6, 1
 BLOCK = (8, LANES)
 NUMBER_OF_XFERS = 680
 
@@ -64,8 +64,6 @@
 def layers_kernel(tiles, x_ref, dy_ref, wg_ref, wu_ref, wd_ref, g_ref, u_ref, a0_t, dh_ref, dwg_ref, dwu_ref, dwd_ref, a_s, a_t, h_s, by_g, by_u, p_s, dg_s, du_s):
     j = pl.program_id(0)
     n, d = x_ref.shape
-    blocks = [pl.ds(k * (n // 4), n // 4) for k in range(4)]
-
     def clear(rows):
         by_g[rows, :] = jnp.zeros_like(by_g[rows, :])
 
@@ -80,14 +78,11 @@
 
     @pl.when(j < tiles)
     def _():
-        for rows in blocks:
-            a = a_s[rows, :]
-            g = dot(a, wg_ref[0])
-            u = dot(a, wu_ref[0])
-            for to, by in ((g_ref, g), (u_ref, u)):
-                for t in range(to.shape[0]):
-                    to[t, rows, :] = by[:, t * to.shape[2] : (t + 1) * to.shape[2]]
-            by_g[rows, :] += dot((g * jax.nn.sigmoid(g) * u).astype(BF16), wd_ref[0])
+        a = a_s[...]
+        g = dot(a, wg_ref[0])
+        u = dot(a, wu_ref[0])
+        g_ref[0], u_ref[0] = g, u
+        by_g[...] += dot((g * jax.nn.sigmoid(g) * u).astype(BF16), wd_ref[0])
 
     @pl.when(j == tiles - 1)
     def _():
@@ -103,13 +98,11 @@
 
     @pl.when(j >= tiles)
     def _():
-        for rows in blocks:
-            a = a_s[rows, :]
-            dp = dot(dy_ref[rows, :], wd_ref[0], NT).astype(BF16).astype(F32)
-            p_s[rows, :], dg, du = backward_tile(dot(a, wg_ref[0]), dot(a, wu_ref[0]), dp)
-            dg_s[rows, :], du_s[rows, :] = dg, du
-            by_g[rows, :] += dot(dg, wg_ref[0], NT)
-            by_u[rows, :] += dot(du, wu_ref[0], NT)
+        a = a_s[...]
+        dp = dot(dy_ref[...], wd_ref[0], NT).astype(BF16).astype(F32)
+        p_s[...], dg_s[...], du_s[...] = backward_tile(dot(a, wg_ref[0]), dot(a, wu_ref[0]), dp)
+        by_g[...] += dot(dg_s[...], wg_ref[0], NT)
+        by_u[...] += dot(du_s[...], wu_ref[0], NT)
         dwg_ref[...] = dot(a_t[...], dg_s[...]).astype(BF16)
         dwu_ref[...] = dot(a_t[...], du_s[...]).astype(BF16)
         dwd_ref[...] = dot(p_s[...], dy_ref[...], TN).astype(BF16)
@@ -126,12 +119,12 @@
         by_rows(n, 32, body)
 
 
-def layers(x, dy, wg, wu, wd, tile=512):
+def layers(x, dy, wg, wu, wd):
     (n, d), ff = x.shape, wg.shape[-1]
-    tiles, per = ff // tile, tile * TILES // ff
+    tiles, tile = TILES, ff // TILES
     early, late = lambda j: jnp.minimum(j, tiles - 1), lambda j: jnp.maximum(j - tiles, 0)
     whole, turned_ = blocks_of((n, d), lambda j: (0, 0)), blocks_of((d, n), lambda j: (0, 0))
-    wide = blocks_of((per, n, ff // TILES), lambda j: (early(j), 0, 0))
+    wide = blocks_of((1, n, tile), lambda j: (early(j), 0, 0))
     weight = blocks_of((1, d, tile), lambda j: (j // tiles, 0, j % tiles))
     across = blocks_of((d, tile), lambda j: (0, late(j)))
     V = lambda *s: pltpu.VMEM(s, BF16)
@@ -141,7 +134,7 @@
         grid=(2 * tiles,),
         in_specs=[whole, whole, weight, weight, blocks_of((1, tile, d), lambda j: (j // tiles, j % tiles, 0))],
         out_specs=[wide, wide, turned_, whole, across, across, blocks_of((tile, d), lambda j: (late(j), 0))],
-        out_shape=[jax.ShapeDtypeStruct((TILES, n, ff // TILES), F32)] * 2 + [jax.ShapeDtypeStruct(s, BF16) for s in ((d, n), (n, d), (d, ff), (d, ff), (ff, d))],
+        out_shape=[jax.ShapeDtypeStruct((TILES, n, tile), F32)] * 2 + [jax.ShapeDtypeStruct(s, BF16) for s in ((d, n), (n, d), (d, ff), (d, ff), (ff, d))],
         scratch_shapes=[V(n, d), V(d, n), V(n, d), pltpu.VMEM((n, d), F32), pltpu.VMEM((n, d), F32), V(n, tile), V(n, tile), V(n, tile)],
         compiler_params=pltpu.CompilerParams(vmem_limit_bytes=62 << 20),
     )(x, dy, wg, wu, wd)
@@ -207,9 +200,9 @@
         self.done = None
 
 
-RATE, CHIP_RATE, DELAY, GAP, SLACK = 46.0e3, 450.0e3, 2.3, 0.1, 0.5
+RATE, CHIP_RATE, DELAY, GAP, SLACK = 43.0e3, 450.0e3, 2.0, 0.1, 0.5
 LATE = {("share", 0): -2, ("share", 1): 2, ("across", 0): 1, ("across", 1): 2, ("halve", 0): 1, ("round", 0): -2}
-STEP = (0.6, 0.6, 0.65, 0.65, 0.65)
+STEP = (1.2, 1.2, 1.3, 1.3, 1.3)
 SLOTS = STEP * TILES
 
 
@@ -293,7 +286,7 @@
     CR = cu // 2
     XR = CR // 4
     around = [z * CR] + [to * CR for to in others["z"]]
-    arrived, pieces = [], []
+    arrived, copies, pieces = [], [], []
 
     for i in range(2 * PARTS):
         l, f0 = 1 - i // PARTS, i % PARTS * FF
@@ -350,17 +343,17 @@
         tz = to_all("z", NZ, ru * cu, from_piece, lambda d, to, i=i: block(rz, i, d - 1))
         e = event([], ends, sends=tz)
         mc, ma, mb = piece(z)
-        home, mine = window(gu_out, (mc, l), core * HD + ma, ru, f0 + mb, cu), block(f_ab, i)
-
-        def work(i=i, mc=mc, ma=ma, mb=mb, mine=mine, home=home):
+        home, mine = window(own_ab, (i, mc), ma, ru, mb, cu), block(f_ab, i)
+
+        def work(i=i, mc=mc, ma=ma, mb=mb):
             total((f_ab, (i,), 0, 0), [(p_ab, (i, mc), ma, mb)] + [(rz, (i, d), 0, 0) for d in range(NZ - 1)], ru, cu)
             squares(f_ab, (i,), 1.0)
-            local(i, 0, mine, home).start()
+            total((own_ab, (i, mc), ma, mb), [(f_ab, (i,), 0, 0)], ru, cu)
 
         ta = to_all("z", NZ, ru * cu, lambda d, to, m=mine: m, lambda d, to, h=home: h)
         e = event(tz, [e], work, 0.4, ta)
         pieces.append(e)
-        spread = event(ta, [e], lambda i=i, mine=mine, home=home: local(i, 0, mine, home).wait(), 0.1)
+        spread = event(ta, [e])
         for c in range(2):
             ri, ci, rax, cax = (y, x, "y", "x") if c else (x, y, "x", "y")
             for s in range(2):
@@ -368,9 +361,10 @@
 
                 kind = "spread", l
 
-                def same(link, row, rows, col, cols, l=l, c=c, f0=f0, s=s, **to):
-                    ref = window(gu_out, (c, l), core * HD + s * S + row * ru, rows * ru, f0 + col, cols)
-                    return xfer(link, rows * ru * cols, ref, ref, **to)
+                def same(link, row, rows, col, cols, i=i, l=l, c=c, f0=f0, s=s, **to):
+                    ref = window(own_ab, (i, c), s * S + row * ru, rows * ru, col, cols)
+                    out = ref if link != "chip" else window(gu_out, (c, l), core * HD + s * S + row * ru, rows * ru, f0 + col, cols)
+                    return xfer(link, rows * ru * cols, ref, out, **to)
 
                 q, b1 = quarter(s, ri), 2 * half(s, ri)
                 ts = [same(cax + e2, q, 1, quarter(s, ci) * QC, QC, **{cax: second(s, ci)}), same(cax + e1, q, 1, half(s, ci) * HC, HC, **{cax: first(s, ci)}),
@@ -379,8 +373,10 @@
                 e = spread
                 for n, t in enumerate(ts):
                     e = event(ts[n - 1 : n], [e], sends=[t] + fw[: n // 3])
-                event(ts[-1:], [e], sends=fw[1:])
+                copy = part_of(local, i, 2 * c + s, window(own_ab, (i, c), s * S, S, 0, FF), window(gu_out, (c, l), core * HD + s * S, S, f0, FF))
+                event(ts[-1:], [e], lambda copy=copy: copy().start(), sends=fw[1:])
                 arrived += fw
+                copies.append(copy)
 
         for s in range(2):
             key, base, kind = (i, s), s * HC, ("down", l)
@@ -410,29 +406,31 @@
             mine, kind = block(ry, *key, y), ("across", l)
             ty = to_all("y", NY, XR * HD, lambda d, to, m=mine: m, lambda d, to, m=mine: m)
             e = event(tx, [e], work_x, adds(XR * HD, 4), ty)
-            home, mine = window(dn_out, (l,), f0 + base + z * CR + x * XR, XR, core * HD, HD), block(f_c, *key)
-
-            def work_y(key=key, mine=mine, home=home):
+            row, mine = base + z * CR + x * XR, block(f_c, *key)
+            home = window(own_c, (i,), row, XR, 0, HD)
+
+            def work_y(key=key, row=row):
                 total((f_c, key, 0, 0), [(ry, (*key, k), 0, 0) for k in range(NY)], XR, HD)
                 squares(f_c, key, 1.0 / NY)
-                local(key[0], 1 + key[1], mine, home).start()
+                total((own_c, key[:1], row, 0), [(f_c, key, 0, 0)], XR, HD)
 
             hx = to_all("x", NX, XR * HD, lambda d, to, m=mine: m, lambda d, to, h=home: h)
             e = event(ty, [e], work_y, 0.3, hx)
             pieces.append(e)
-            e = event(hx, [e, spread], lambda key=key, mine=mine, home=home: local(key[0], 1 + key[1], mine, home).wait(), 0.1)
+            e = event(hx, [e, spread])
             prev, ends = [[], []], [e, e]
             kind = "round", l
             for t in range(4):
                 for k, (sg, zl, slot, n) in enumerate(arms):
                     if t < n:
-                        ref = window(dn_out, (l,), f0 + chunk(-sg * t), CR, core * HD, HD)
+                        ref = window(own_c, (i,), chunk(-sg * t), CR, 0, HD)
                         ring = xfer(zl, CR * HD, ref, ref, z=others["z"][-(sg < 0)])
                         ends[k] = event(prev[k], [ends[k]], sends=[ring])
                         prev[k] = [ring]
-            ref = window(dn_out, (l,), f0 + base, HC, core * HD, HD)
-            arrived.append(xfer("chip", HC * HD, ref, ref, core=other))
-            event(prev[0] + prev[1], ends, sends=arrived[-1:])
+            ref, out = window(own_c, (i,), base, HC, 0, HD), window(dn_out, (l,), f0 + base, HC, core * HD, HD)
+            arrived.append(xfer("chip", HC * HD, ref, out, core=other))
+            copies.append(part_of(local, i, 4 + s, ref, out))
+            event(prev[0] + prev[1], ends, lambda copy=copies[-1]: copy().start(), sends=arrived[-1:])
 
     kind = None
     e, ts, prev = None, [], None
@@ -451,7 +449,8 @@
         sq_out[...] = norms[3][0] + norms[3][1]
 
     event(ts, [e], finish, 0.1)
-    event(arrived, [])
+    every = list(events)
+    event(arrived, every, lambda: [copy().wait() for copy in copies])
     return xfers, events
 
 
@@ -483,10 +482,10 @@
         pl.semaphore_signal(barrier, inc=1, device_id=p, device_id_type=LOGICAL)
     pl.semaphore_wait(barrier, len(peers))
 
-    def tile_sends(j, srcs=None, slot=0):
+    def tile_sends(j, srcs=None):
         i, cols = PARTS + div(j, per), slice_of(rem(j, per))
         dsts = [p_ab.at[i, c, :, cols] for c in range(2)] + [p_c.at[i, cols, :]]
-        return [pltpu.make_async_remote_copy(src_ref=src, dst_ref=dst, send_sem=out_sem.at[slot, k], recv_sem=in_sem.at[j, k], device_id=partner,
+        return [pltpu.make_async_remote_copy(src_ref=src, dst_ref=dst, send_sem=out_sem.at[k], recv_sem=in_sem.at[j, k], device_id=partner,
                                              device_id_type=LOGICAL) for k, (src, dst) in enumerate(zip(srcs or dsts, dsts, strict=True))]
 
     def total(dst, srcs, rows, cols):
@@ -607,14 +606,14 @@
     groups.append([])
 
     rows_in, rows_out = (pl.ds(pl.multiple_of(c * HD, SUBLANES), HD) for c in (core, other))
-    staged = lambda slot: [st_ab.at[slot, 0, rows_out, :], st_ab.at[slot, 1, rows_out, :], st_c.at[slot, :, yours]]
-    blocks = [pl.ds(k * (n // 4), n // 4) for k in range(4)]
+    staged = lambda: [st_ab.at[0, rows_out, :], st_ab.at[1, rows_out, :], st_c.at[:, yours]]
+    blocks = [pl.ds(k * (n // 2), n // 2) for k in range(2)]
 
     def through(which, j, slot):
         if which == 0:
-            @pl.when(j > 1)
+            @pl.when(j > 0)
             def _():
-                for t in tile_sends(j - 2, staged(slot), slot):
+                for t in tile_sends(j - 1, staged()):
                     t.wait_send()
 
         for rows in blocks[which::2]:
@@ -624,19 +623,18 @@
     def term(c, j, slot):
         i, cols = PARTS + div(j, per), slice_of(rem(j, per))
         if c < 2:
-            st_ab[slot, c] = dot(a0_t[...], (dg_s, du_s)[c][...]).astype(BF16)
-            own_ab[i, c, :, cols] = st_ab[slot, c, rows_in, :]
+            st_ab[c] = dot(a0_t[...], (dg_s, du_s)[c][...]).astype(BF16)
+            own_ab[i, c, :, cols] = st_ab[c, rows_in, :]
         else:
-            st_c[slot] = dot(p_s[...], dh[...], TN).astype(BF16)
-            own_c[i, cols, :] = st_c[slot, :, mine]
-            for t in tile_sends(j, staged(slot), slot):
+            st_c[...] = dot(p_s[...], dh[...], TN).astype(BF16)
+            own_c[i, cols, :] = st_c[:, mine]
+            for t in tile_sends(j, staged()):
                 t.start()
 
     steps([lambda j: gate.at[j], lambda j: up.at[j], lambda j: wd.at[0, slice_of(j), :]], [gbuf, ubuf, wbuf],
           *[functools.partial(f, k) for f, k in ((through, 0), (through, 1), (term, 0), (term, 1), (term, 2))])
-    for k in range(2):
-        for t in tile_sends(TILES - 2 + k, staged(k), k):
-            t.wait_send()
+    for t in tile_sends(TILES - 1, staged()):
+        t.wait_send()
     emit(tail)
     for count in sorted(set(counts)):
         def wait(k, carry, count=count):
@@ -664,10 +662,10 @@
             V(N, 2, 2, 2 * ru, fs), V(N, 2, 2, ru, fs), V(N, 2, 2, ru, fs // 2), V(N, 2, 2, ru, fs // 4),
             V(N, NZ - 1, ru, cu), V(N, 2, NZ - 1, CR, HD), V(N, 2, NX - 1, CR // 4, HD), V(N, 2, NY, CR // 4, HD), V(N, ru, cu), V(N, 2, CR // 4, HD),
             W(*BLOCK), W(NZ, *BLOCK), W(NY, *BLOCK), W(NX, *BLOCK), W(CORES, *BLOCK),
-            W(2, n, tile), W(2, n, tile), V(2, tile, d), V(n, tile), V(n, tile), V(n, tile), V(2, 2, d, tile), V(2, tile, d),
-            DMA(NUMBER_OF_XFERS), DMA(NUMBER_OF_XFERS), DMA(3), DMA(N, 3), DMA(2, 3), DMA(2, 3), DMA(TILES, 3),
+            W(2, n, tile), W(2, n, tile), V(2, tile, d), V(n, tile), V(n, tile), V(n, tile), V(2, d, tile), V(tile, d),
+            DMA(NUMBER_OF_XFERS), DMA(NUMBER_OF_XFERS), DMA(3), DMA(N, 6), DMA(2, 3), DMA(3), DMA(TILES, 3),
         ],
-        compiler_params=pltpu.CompilerParams(collective_id=0, has_side_effects=True, vmem_limit_bytes=62 << 20),
+        compiler_params=pltpu.CompilerParams(collective_id=0, has_side_effects=True, vmem_limit_bytes=63 << 20),
     )(g1, u1, d1, a0_t, dh, gate, up, wd)
 
 
@@ -678,45 +676,16 @@
     return (w - 0.02 * step).astype(BF16), m, v
 
 
-def optimizer_kernel(count, sq, *refs):
-    factor = jnp.minimum(1.0, 0.5 * lax.rsqrt(jnp.sum(sq[...], keepdims=True) / count + 1e-30))
-    ws, ms, vs, gs, *outs = (refs[i : i + 3] for i in range(0, len(refs), 3))
-    for k in range(3):
-        wide = ws[k].shape[-1]
-
-        def rows_of(i, _, k=k, wide=wide):
-            at = 0, pl.ds(pl.multiple_of(i * SUBLANES, SUBLANES), SUBLANES), slice(None)
-            g = gs[k][(0,) * (len(gs[k].shape) - 3) + at].astype(F32) * factor
-            for out, new in zip(outs, adamw(ws[k][at].astype(F32), ms[k][at], vs[k][at], g), strict=True):
-                out[k][at] = new
-            return _
-
-        lax.fori_loop(0, ws[k].shape[1] // SUBLANES, rows_of, 0)
-
-
-def optimizer(sq, weights, m, v, gu, down, blocks=24):
-    def spec(a, lead=()):
-        l, rows, cols = a.shape[-3:]
-        return pl.BlockSpec((1,) * len(lead) + (1, rows // blocks, cols), lambda j: (*lead, j // blocks, j % blocks, 0))
-
-    plain = [spec(w) for w in weights]
-    return pl.pallas_call(
-        functools.partial(optimizer_kernel, sum(w.size for w in weights)),
-        name="optimizer",
-        grid=(2 * blocks,),
-        in_specs=[pl.BlockSpec(sq.shape, lambda j: (0, 0))] + plain * 3 + [spec(gu, (0,)), spec(gu, (1,)), spec(down)],
-        out_specs=plain * 3,
-        out_shape=[jax.ShapeDtypeStruct(w.shape, t) for t in (BF16, F32, F32) for w in weights],
-        compiler_params=pltpu.CompilerParams(vmem_limit_bytes=60 << 20),
-    )(sq, *weights, *m, *v, gu, gu, down)
-
-
 def solution(mesh):
     def step(x, dy, *arrays):
         weights, m, v = (arrays[i : i + 3] for i in (0, 3, 6))
         gate, up, a0_t, dh, *by_1 = layers(x[0], dy[0], *weights)
         gu, down, squares = gradient_sums(*by_1, a0_t, dh, gate, up, weights[2])
-        return tuple(optimizer(squares, weights, m, v, gu, down))
+        gradients = [gu[0], gu[1], down]
+        count = sum(g.size for g in gradients)
+        factor = jnp.minimum(1.0, 0.5 * lax.rsqrt(jnp.sum(squares) / count + 1e-30))
+        new = [adamw(w.astype(F32), m, v, g.astype(F32) * factor) for w, m, v, g in zip(weights, m, v, gradients, strict=True)]
+        return tuple(one[which] for which in range(3) for one in new)
 
     whole = P(None, None, None)
     return jax.shard_map(

time: 394 us -> 384 us (0.975)
  Pallas kernels: 392 us -> 276 us
  other arithmetic: 0 us -> 107 us
    pallas_call x1 -> x0, Pallas kernels: 121 us -> none  [optimizer(): pl.pallas_call(functools.partial(optimizer_kernel, sum((w.size for w in w...]
    convert_element_type x0 -> x2, other arithmetic: none -> 105 us  [adamw(): return ((w - 0.02 * step).astype(BF16), m, v)]
    pallas_call x1, Pallas kernels: 193 us -> 200 us  [gradient_sums(): pl.pallas_call(functools.partial(sum_kernel, ru, cu), name='gradient_sums...]
where the time goes in v5:
time: 384 us
  Pallas kernels  276 us (72%)
  other arithmetic  107 us (28%)
    pallas_call x1, Pallas kernels, gradient_sums(): pl.pallas_call(functools.partial(sum_kernel, ru, cu), name='gradient_sums...  200 us
    convert_element_type x2, other arithmetic, adamw(): return ((w - 0.02 * step).astype(BF16), m, v)  105 us
    pallas_call x1, Pallas kernels, layers(): pl.pallas_call(functools.partial(layers_kernel, tiles), name='layers', gr...  76.2 us

profile of v5, /device:TPU:1, one launch (start us, length us, event | category | flops | bytes accessed | tf_op | source)
XLA Modules:
  0.0 383.8 jit_solution(1259378066830083980)
XLA Ops:
  0.6 76.2 %layers.1 = (f32[6,1024,512]{2,1,0:T(8,128)}, f32[6,1024,512]{2,1,0:T(8,128)}, bf16[768,1024]{1,0:T(8,128)(2,1)}, bf16[1024,768]{1,0:T(8,128)(2,1)}, bf16[768,30...) custom-call(bf16[1024,768]{1,0:T(8,128)(2,1)} %bitcast.16, bf16[1024,768]{1,0:T(8,128)(2,1)} %bitcast.17, ...), custom_call_target="tpu_custom_call" | custom-call | tf_op jit(solution)/shard_map/layers/pallas_call | solution.py:131
  76.8 199.5 %gradient_sums.1 = (bf16[2,2,768,3072]{3,2,1,0:T(8,128)(2,1)}, bf16[2,3072,768]{2,1,0:T(8,128)(2,1)}, f32[8,128]{1,0:T(8,128)}) custom-call(bf16[768,3072]{1,0:T(8,128)(2,1)} %get-tuple-element.19.refs_0_, bf16[768,3072]{1,0:T(8,128)(2,1)} %get-tuple-element.20.refs_1_, bf16[3072,768]{1,0:T(8,128)(2,1)} %get-tuple-element.21.refs_2_, ...), custom_call_target="tpu_custom_call" | custom-call | tf_op jit(solution)/shard_map/gradient_sums/pallas_call | solution.py:654
  276.4 1.3 reduce_sum.9
  278.3 68.9 %fusion.5 = (bf16[2,768,3072]{2,1,0:T(8,128)(2,1)}, f32[2,768,3072]{2,1,0:T(8,128)}, f32[2,768,3072]{2,1,0:T(8,128)}, bf16[2,768,3072]{2,1,0:T(8,128)(2,1)}, f32...) fusion(bf16[2,768,3072]{2,1,0:T(8,128)(2,1)} %wu_ref.1, f32[]{:T(128)S(6)} %min_shard_map.3, ...), kind=kLoop, calls=%fused_computation.14 | loop fusion | flops 160432128 | bytes 207618048 | tf_op jit(solution)/shard_map/convert_element_type | solution.py:676
  347.2 36.6 %fusion.8 = (bf16[2,3072,768]{2,1,0:T(8,128)(2,1)}, f32[2,3072,768]{2,1,0:T(8,128)}, f32[2,3072,768]{2,1,0:T(8,128)}) fusion(bf16[2,3072,768]{2,1,0:T(8,128)(2,1)} %refs_7_.1, f32[]{:T(128)S(6)} %min_shard_map.3, bf16[2,3072,768]{2,1,0:T(8,128)(2,1)} %get-tuple-element.28, f32[2,3072,768]{2,1,0:T(8,128)} %param.21, f32[2,3072,768]{2,1,0:T(8,128)} %param.18), kind=kLoop, calls=%fused_computation.17 | loop fusion | flops 80216064 | bytes 103809024 | tf_op jit(solution)/shard_map/convert_element_type | solution.py:676

commit v6 on v4

--- a/solution.py
+++ b/solution.py
@@ -64,8 +64,6 @@
 def layers_kernel(tiles, x_ref, dy_ref, wg_ref, wu_ref, wd_ref, g_ref, u_ref, a0_t, dh_ref, dwg_ref, dwu_ref, dwd_ref, a_s, a_t, h_s, by_g, by_u, p_s, dg_s, du_s):
     j = pl.program_id(0)
     n, d = x_ref.shape
-    blocks = [pl.ds(k * (n // 4), n // 4) for k in range(4)]
-
     def clear(rows):
         by_g[rows, :] = jnp.zeros_like(by_g[rows, :])
 
@@ -80,14 +78,13 @@
 
     @pl.when(j < tiles)
     def _():
-        for rows in blocks:
-            a = a_s[rows, :]
-            g = dot(a, wg_ref[0])
-            u = dot(a, wu_ref[0])
-            for to, by in ((g_ref, g), (u_ref, u)):
-                for t in range(to.shape[0]):
-                    to[t, rows, :] = by[:, t * to.shape[2] : (t + 1) * to.shape[2]]
-            by_g[rows, :] += dot((g * jax.nn.sigmoid(g) * u).astype(BF16), wd_ref[0])
+        a = a_s[...]
+        g = dot(a, wg_ref[0])
+        u = dot(a, wu_ref[0])
+        for to, by in ((g_ref, g), (u_ref, u)):
+            for t in range(to.shape[0]):
+                to[t] = by[:, t * to.shape[2] : (t + 1) * to.shape[2]]
+        by_g[...] += dot((g * jax.nn.sigmoid(g) * u).astype(BF16), wd_ref[0])
 
     @pl.when(j == tiles - 1)
     def _():
@@ -103,13 +100,11 @@
 
     @pl.when(j >= tiles)
     def _():
-        for rows in blocks:
-            a = a_s[rows, :]
-            dp = dot(dy_ref[rows, :], wd_ref[0], NT).astype(BF16).astype(F32)
-            p_s[rows, :], dg, du = backward_tile(dot(a, wg_ref[0]), dot(a, wu_ref[0]), dp)
-            dg_s[rows, :], du_s[rows, :] = dg, du
-            by_g[rows, :] += dot(dg, wg_ref[0], NT)
-            by_u[rows, :] += dot(du, wu_ref[0], NT)
+        a = a_s[...]
+        dp = dot(dy_ref[...], wd_ref[0], NT).astype(BF16).astype(F32)
+        p_s[...], dg_s[...], du_s[...] = backward_tile(dot(a, wg_ref[0]), dot(a, wu_ref[0]), dp)
+        by_g[...] += dot(dg_s[...], wg_ref[0], NT)
+        by_u[...] += dot(du_s[...], wu_ref[0], NT)
         dwg_ref[...] = dot(a_t[...], dg_s[...]).astype(BF16)
         dwu_ref[...] = dot(a_t[...], du_s[...]).astype(BF16)
         dwd_ref[...] = dot(p_s[...], dy_ref[...], TN).astype(BF16)
@@ -448,7 +443,7 @@
         ts, prev = new, (ref, n)
 
     def finish():
-        sq_out[...] = norms[3][0] + norms[3][1]
+        sq_out[...] = jnp.broadcast_to(jnp.sum(norms[3][0] + norms[3][1], keepdims=True), BLOCK)
 
     event(ts, [e], finish, 0.1)
     event(arrived, [])
@@ -678,45 +673,16 @@
     return (w - 0.02 * step).astype(BF16), m, v
 
 
-def optimizer_kernel(count, sq, *refs):
-    factor = jnp.minimum(1.0, 0.5 * lax.rsqrt(jnp.sum(sq[...], keepdims=True) / count + 1e-30))
-    ws, ms, vs, gs, *outs = (refs[i : i + 3] for i in range(0, len(refs), 3))
-    for k in range(3):
-        wide = ws[k].shape[-1]
-
-        def rows_of(i, _, k=k, wide=wide):
-            at = 0, pl.ds(pl.multiple_of(i * SUBLANES, SUBLANES), SUBLANES), slice(None)
-            g = gs[k][(0,) * (len(gs[k].shape) - 3) + at].astype(F32) * factor
-            for out, new in zip(outs, adamw(ws[k][at].astype(F32), ms[k][at], vs[k][at], g), strict=True):
-                out[k][at] = new
-            return _
-
-        lax.fori_loop(0, ws[k].shape[1] // SUBLANES, rows_of, 0)
-
-
-def optimizer(sq, weights, m, v, gu, down, blocks=24):
-    def spec(a, lead=()):
-        l, rows, cols = a.shape[-3:]
-        return pl.BlockSpec((1,) * len(lead) + (1, rows // blocks, cols), lambda j: (*lead, j // blocks, j % blocks, 0))
-
-    plain = [spec(w) for w in weights]
-    return pl.pallas_call(
-        functools.partial(optimizer_kernel, sum(w.size for w in weights)),
-        name="optimizer",
-        grid=(2 * blocks,),
-        in_specs=[pl.BlockSpec(sq.shape, lambda j: (0, 0))] + plain * 3 + [spec(gu, (0,)), spec(gu, (1,)), spec(down)],
-        out_specs=plain * 3,
-        out_shape=[jax.ShapeDtypeStruct(w.shape, t) for t in (BF16, F32, F32) for w in weights],
-        compiler_params=pltpu.CompilerParams(vmem_limit_bytes=60 << 20),
-    )(sq, *weights, *m, *v, gu, gu, down)
-
-
 def solution(mesh):
     def step(x, dy, *arrays):
         weights, m, v = (arrays[i : i + 3] for i in (0, 3, 6))
         gate, up, a0_t, dh, *by_1 = layers(x[0], dy[0], *weights)
         gu, down, squares = gradient_sums(*by_1, a0_t, dh, gate, up, weights[2])
-        return tuple(optimizer(squares, weights, m, v, gu, down))
+        gradients = [gu[0], gu[1], down]
+        count = sum(g.size for g in gradients)
+        factor = jnp.minimum(1.0, 0.5 * lax.rsqrt(squares[0, 0] / count + 1e-30))
+        new = [adamw(w.astype(F32), m, v, g.astype(F32) * factor) for w, m, v, g in zip(weights, m, v, gradients, strict=True)]
+        return tuple(one[which] for which in range(3) for one in new)
 
     whole = P(None, None, None)
     return jax.shard_map(

time: 394 us -> 378 us (0.959)
  Pallas kernels: 392 us -> 270 us
  other arithmetic: 0 us -> 105 us
    pallas_call x1 -> x0, Pallas kernels: 121 us -> none  [optimizer(): pl.pallas_call(functools.partial(optimizer_kernel, sum((w.size for w in w...]
    convert_element_type x0 -> x2, other arithmetic: none -> 105 us  [adamw(): return ((w - 0.02 * step).astype(BF16), m, v)]
where the time goes in v6:
time: 378 us
  Pallas kernels  270 us (71%)
  other arithmetic  105 us (28%)
    pallas_call x1, Pallas kernels, gradient_sums(): pl.pallas_call(functools.partial(sum_kernel, ru, cu), name='gradient_sums...  194 us
    convert_element_type x2, other arithmetic, adamw(): return ((w - 0.02 * step).astype(BF16), m, v)  105 us
    pallas_call x1, Pallas kernels, layers(): pl.pallas_call(functools.partial(layers_kernel, tiles), name='layers', gr...  76.2 us

profile of v6, /device:TPU:1, one launch (start us, length us, event | category | flops | bytes accessed | tf_op | source)
XLA Modules:
  0.0 377.9 jit_solution(9649187457150362067)
XLA Ops:
  0.6 76.2 %layers.1 = (f32[12,1024,256]{2,1,0:T(8,128)}, f32[12,1024,256]{2,1,0:T(8,128)}, bf16[768,1024]{1,0:T(8,128)(2,1)}, bf16[1024,768]{1,0:T(8,128)(2,1)}, bf16[768,...) custom-call(bf16[1024,768]{1,0:T(8,128)(2,1)} %bitcast.17, bf16[1024,768]{1,0:T(8,128)(2,1)} %bitcast.18, ...), custom_call_target="tpu_custom_call" | custom-call | tf_op jit(solution)/shard_map/layers/pallas_call | solution.py:133
  76.8 193.7 %gradient_sums.1 = (bf16[2,2,768,3072]{3,2,1,0:T(8,128)(2,1)}, bf16[2,3072,768]{2,1,0:T(8,128)(2,1)}, f32[8,128]{1,0:T(8,128)}) custom-call(bf16[768,3072]{1,0:T(8,128)(2,1)} %get-tuple-element.19.refs_0_, bf16[768,3072]{1,0:T(8,128)(2,1)} %get-tuple-element.20.refs_1_, bf16[3072,768]{1,0:T(8,128)(2,1)} %get-tuple-element.21.refs_2_, ...), custom_call_target="tpu_custom_call" | custom-call | tf_op jit(solution)/shard_map/gradient_sums/pallas_call | solution.py:651
  270.5 1.2 slice.10
  272.4 68.9 %fusion.5 = (bf16[2,768,3072]{2,1,0:T(8,128)(2,1)}, f32[2,768,3072]{2,1,0:T(8,128)}, f32[2,768,3072]{2,1,0:T(8,128)}, bf16[2,768,3072]{2,1,0:T(8,128)(2,1)}, f32...) fusion(bf16[2,768,3072]{2,1,0:T(8,128)(2,1)} %wu_ref.1, f32[]{:T(128)} %bitcast.2, ...), kind=kLoop, calls=%fused_computation.14 | loop fusion | flops 160432128 | bytes 207618048 | tf_op jit(solution)/shard_map/convert_element_type | solution.py:673
  341.3 36.6 %fusion.8 = (bf16[2,3072,768]{2,1,0:T(8,128)(2,1)}, f32[2,3072,768]{2,1,0:T(8,128)}, f32[2,3072,768]{2,1,0:T(8,128)}) fusion(bf16[2,3072,768]{2,1,0:T(8,128)(2,1)} %refs_7_.1, f32[]{:T(128)} %bitcast.2, bf16[2,3072,768]{2,1,0:T(8,128)(2,1)} %get-tuple-element.28, f32[2,3072,768]{2,1,0:T(8,128)} %param.21, f32[2,3072,768]{2,1,0:T(8,128)} %param.18), kind=kLoop, calls=%fused_computation.17 | loop fusion | flops 80216064 | bytes 103809024 | tf_op jit(solution)/shard_map/convert_element_type | solution.py:673
